TPU v7x, 128 devices: a whole 4x4x4 slice. The times are simulated.
128 devices in a mesh: lat: 16 (over y, z), lon: 8 (over x, core).
Axes of the slice: x: 4, y: 4, z: 4, core: 2. Of those that a mesh axis runs over, the one named last changes fastest.
Arguments:
- features: bfloat16 [1572864, 128], P(('lat', 'lon')), may hold values from -6 to 6
- cell_index: int32 [1572864], P(('lat', 'lon')), may hold values from 0 to 2547
- tile_rows: int32 [16384], P(('lat', 'lon')), may hold values from 1 to 96, as said below
- spread: float32 [3, 3], replicated, may hold values from 0.2 to 1
- w_in: bfloat16 [128, 256], replicated, may hold values from -0.5 to 0.5
- w_dens: float32 [256], replicated, may hold values from -3 to 3
- w_one: bfloat16 [3, 3, 256, 256], replicated, may hold values from -0.125 to 0.125
- w_two: bfloat16 [3, 3, 256, 256], replicated, may hold values from -0.125 to 0.125
Outputs:
- encoded: bfloat16 [384, 768, 256], P('lat', 'lon')
Inputs may be any that keep to these rules, and one draw needn't show every extreme that they name: `tile_rows`: every block has 1 to 96 used slots; on every device some block has exactly 96.
All inputs are finite; a program needn't handle non-finite values.
Results may differ from a plain program's by a relative error of at most 0.0054.
Values may be sent and summed in bfloat16 or wider, within the bound.
No kernel may reach another device: no remote copies, remote signals or barrier semaphores. Data moves between devices by JAX's collectives and lax.ppermute only.
A program may use at most 64 MiB of HBM per device.

v0:
```python
import jax
import jax.numpy as jnp
from jax import lax
from jax.sharding import PartitionSpec as P

TH = 24
TW = 96
F = 128
C = 256
CAP = 96
PH = 26
PW = 98


def cut_along(value, dim, count):
    lengths = value.shape
    parts = value.reshape(*lengths[:dim], count, lengths[dim] // count, *lengths[dim + 1 :])
    return jnp.moveaxis(parts, dim, 0)


def in_order(parts, dim):
    parts = jnp.moveaxis(parts, 0, dim)
    lengths = parts.shape
    return parts.reshape(*lengths[:dim], lengths[dim] * lengths[dim + 1], *lengths[dim + 2 :])


def joined_exchange(value, axis, axes, splits, concats):
    sizes = [lax.axis_size(a) for a in axes]
    parts = cut_along(value, splits[0], sizes[0])
    parts = jnp.moveaxis(cut_along(parts, splits[1] + 1, sizes[1]), 0, 1)
    inside = parts.shape[2:]
    parts = parts.reshape(-1, *inside)
    parts = lax.all_to_all(parts, axis, split_axis=0, concat_axis=0, tiled=True)
    parts = in_order(parts.reshape(*sizes, *inside), concats[0] + 1)
    return in_order(parts, concats[1])


def padded_2(cells, sides, width):
    for axis, dim in sides:
        count = lax.axis_size(axis)
        head = lax.slice_in_dim(cells, 0, width, axis=dim)
        tail = lax.slice_in_dim(cells, cells.shape[dim] - width, cells.shape[dim], axis=dim)
        cells = jnp.concatenate(
            [
                lax.ppermute(tail, axis, [(i, (i + 1) % count) for i in range(count)]),
                cells,
                lax.ppermute(head, axis, [((i + 1) % count, i) for i in range(count)]),
            ],
            axis=dim,
        )
    return cells


def clear_edges(padded, width, tile_rows_count):
    lat_pos = lax.axis_index("lat")
    lat_count = lax.axis_size("lat")
    global_rows = jnp.arange(padded.shape[0], dtype=jnp.int32) + lat_pos * tile_rows_count - width
    keep = (global_rows >= 0) & (global_rows < lat_count * tile_rows_count)
    return jnp.where(keep[:, None, None], padded, jnp.zeros((), padded.dtype))


def conv_tile(padded, weight, out_rows, out_cols):
    chans = padded.shape[2]
    total = jnp.zeros((out_rows * out_cols, weight.shape[3]), jnp.float32)
    for row_off in range(3):
        for col_off in range(3):
            window = padded[row_off : row_off + out_rows, col_off : col_off + out_cols].reshape(
                -1, chans
            )
            total = total + jnp.dot(
                window, weight[row_off, col_off], preferred_element_type=jnp.float32
            )
    return total.reshape(out_rows, out_cols, -1)


def shards(features, cell_index, tile_rows, spread, w_in, w_dens, w_one, w_two):
    lat_count = lax.axis_size("lat")
    lon_count = lax.axis_size("lon")
    tiles = lat_count * lon_count
    frame_cells = PH * PW
    slot_ids = jnp.arange(CAP, dtype=jnp.int32)
    valid = slot_ids[None, :] < tile_rows[:, None]
    cells = jnp.where(valid, cell_index.reshape(tiles, CAP), frame_cells)
    got_rows, got_cells = (
        joined_exchange(
            features.reshape(lat_count, lon_count, CAP, F),
            ("lat", "lon"),
            ("lat", "lon"),
            (0, 1),
            (0, 1),
        ),
        joined_exchange(
            cells.reshape(lat_count, lon_count, CAP), ("lat", "lon"), ("lat", "lon"), (0, 1), (0, 1)
        ),
    )
    received = tiles * CAP
    got_rows = got_rows.reshape(received, F)
    got_cells = got_cells.reshape(received)
    block_rows = 1024
    blocks = received // block_rows
    frame_ids = jnp.arange(frame_cells, dtype=jnp.int32)

    def add_block(carry, item):
        sums, counts = carry
        rows_blk, cells_blk = item
        onehot = frame_ids[:, None] == cells_blk[None, :]
        sums = sums + jnp.dot(
            onehot.astype(jnp.bfloat16), rows_blk, preferred_element_type=jnp.float32
        )
        counts = counts + jnp.sum(onehot.astype(jnp.float32), axis=1)
        return ((sums, counts), None)

    start_carry = (jnp.zeros((frame_cells, F), jnp.float32), jnp.zeros((frame_cells,), jnp.float32))
    (frame_sum, frame_count), _ = lax.scan(
        add_block,
        start_carry,
        (got_rows.reshape(blocks, block_rows, F), got_cells.reshape(blocks, block_rows)),
    )
    frame_sum = frame_sum.reshape(PH, PW, F)
    frame_count = frame_count.reshape(PH, PW)
    data = jnp.zeros((TH, TW, F), jnp.float32)
    density = jnp.zeros((TH, TW), jnp.float32)
    for row_off in range(3):
        for col_off in range(3):
            data = (
                data
                + spread[row_off, col_off]
                * frame_sum[row_off : row_off + TH, col_off : col_off + TW]
            )
            density = (
                density
                + spread[row_off, col_off]
                * frame_count[row_off : row_off + TH, col_off : col_off + TW]
            )
    mean = (data / (1.0 + density)[..., None]).astype(jnp.bfloat16)
    grid = jnp.dot(mean.reshape(-1, F), w_in, preferred_element_type=jnp.float32)
    grid = grid + jnp.log1p(density).reshape(-1, 1) * w_dens[None, :]
    grid = grid.astype(jnp.bfloat16).reshape(TH, TW, C)
    padded = clear_edges(padded_2(grid, (("lat", 0), ("lon", 1)), 1), 1, TH)
    hidden = jax.nn.silu(conv_tile(padded, w_one, TH, TW)).astype(jnp.bfloat16)
    hidden_pad = clear_edges(padded_2(hidden, (("lat", 0), ("lon", 1)), 1), 1, TH)
    encoded = grid.astype(jnp.float32) + conv_tile(hidden_pad, w_two, TH, TW)
    return encoded.astype(jnp.bfloat16)


def solution(mesh):
    in_specs = (
        P(("lat", "lon"), None),
        P(("lat", "lon")),
        P(("lat", "lon")),
        P(),
        P(),
        P(),
        P(),
        P(),
    )
    out_specs = P("lat", "lon", None)
    return jax.shard_map(shards, mesh=mesh, in_specs=in_specs, out_specs=out_specs, check_vma=False)
```

profile of v0, /device:TPU:7, one launch (start us, length us, event | category | flops | bytes accessed | tf_op | source)
XLA Modules:
  0.0 177.9 jit_solution(282316406212761419)
XLA Ops:
  1.7 18.7 %all_to_all.10 = s32[128,1,1,96]{3,2,1,0:T(1,128)S(1)} all-to-all(s32[128,1,1,96]{3,2,1,0:T(1,128)S(1)} %bitcast.165), channel_id=1, replica_groups=mesh['lat'=16,'lon'=8] {'lat','lon'}, dimensions={0} | all-to-all | bytes 98304 | tf_op jit(solution)/shard_map/all_to_all | solution.py:33
  20.3 6.9 %all-to-all-start.1 = ((bf16[128,1,1,96,128]{4,3,2,1,0:T(8,128)(2,1)}), bf16[128,1,1,96,128]{4,3,2,1,0:T(8,128)(2,1)}, u32[]{:S(2)}, u32[]{:S(2)}) async-start(bf16[128,1,1,96,128]{4,3,2,1,0:T(8,128)(2,1)} %bitcast.162), calls=%async_computation.1 | async-start | bytes 6291456 | tf_op jit(solution)/shard_map/all_to_all | solution.py:33
  28.1 38.3 %all-to-all-done.1 = bf16[128,1,1,96,128]{4,3,2,1,0:T(8,128)(2,1)} async-done(((bf16[128,1,1,96,128]{4,3,2,1,0:T(8,128)(2,1)}), bf16[128,1,1,96,128]{4,3,2,1,0:T(8,128)(2,1)}, u32[]{:S(2)}, u32[]{:S(2)}) %all-to-all-start.1) | async-done | bytes 3145760 | tf_op jit(solution)/shard_map/all_to_all | solution.py:33
  66.3 52.1 %while.13 = (s32[]{:T(128)}, f32[2548,128]{1,0:T(8,128)S(1)}, f32[2548]{0:T(1024)S(1)}, s32[12,1024]{1,0:T(8,128)S(1)}, bf16[12,1024,128]{2,1,0:T(8,128)(2,1)}, /*index=5*/s32[]{:T(128)}, s32[]{:T(128)}) while((s32[]{:T(128)}, f32[2548,128]{1,0:T(8,128)S(1)}, f32[2548]{0:T(1024)S(1)}, s32[12,1024]{1,0:T(8,128)S(1)}, ...), condition=%wide.region_2.3_spmd.clone, body=%wide.region_0.2_spmd.clone.sunk | while | flops 679034368 | bytes 2928552 | solution.py:114
  67.5 3.2 %fusion.98 = f32[2548,128]{1,0:T(8,128)S(1)} fusion(s32[1024]{0:T(1024)S(1)} %bitcast.167, f32[2548,128]{1,0:T(8,128)S(1)} %get-tuple-element.146, pred[]{:T(512)S(6)} %compare.3, bf16[12,1024,128]{2,1,0:T(8,128)(2,1)} %get-tuple-element.156, s32[]{:T(128)S(6)} %copy.14), kind=kOutput, calls=%fused_computation.6.clone.1 | convolution fusion | flops 671204352 | bytes 2875397 | tf_op jit(solution)/shard_map/while/body/eval_jaxpr/dot_general | solution.py:107
  71.8 3.2 %fusion.98 = f32[2548,128]{1,0:T(8,128)S(1)} fusion(s32[1024]{0:T(1024)S(1)} %bitcast.167, f32[2548,128]{1,0:T(8,128)S(1)} %get-tuple-element.146, pred[]{:T(512)S(6)} %compare.3, bf16[12,1024,128]{2,1,0:T(8,128)(2,1)} %get-tuple-element.156, s32[]{:T(128)S(6)} %copy.14), kind=kOutput, calls=%fused_computation.6.clone.1 | convolution fusion | flops 671204352 | bytes 2875397 | tf_op jit(solution)/shard_map/while/body/eval_jaxpr/dot_general | solution.py:107
  76.2 3.2 %fusion.98 = f32[2548,128]{1,0:T(8,128)S(1)} fusion(s32[1024]{0:T(1024)S(1)} %bitcast.167, f32[2548,128]{1,0:T(8,128)S(1)} %get-tuple-element.146, pred[]{:T(512)S(6)} %compare.3, bf16[12,1024,128]{2,1,0:T(8,128)(2,1)} %get-tuple-element.156, s32[]{:T(128)S(6)} %copy.14), kind=kOutput, calls=%fused_computation.6.clone.1 | convolution fusion | flops 671204352 | bytes 2875397 | tf_op jit(solution)/shard_map/while/body/eval_jaxpr/dot_general | solution.py:107
  80.5 3.1 %fusion.98 = f32[2548,128]{1,0:T(8,128)S(1)} fusion(s32[1024]{0:T(1024)S(1)} %bitcast.167, f32[2548,128]{1,0:T(8,128)S(1)} %get-tuple-element.146, pred[]{:T(512)S(6)} %compare.3, bf16[12,1024,128]{2,1,0:T(8,128)(2,1)} %get-tuple-element.156, s32[]{:T(128)S(6)} %copy.14), kind=kOutput, calls=%fused_computation.6.clone.1 | convolution fusion | flops 671204352 | bytes 2875397 | tf_op jit(solution)/shard_map/while/body/eval_jaxpr/dot_general | solution.py:107
  84.9 3.2 %fusion.98 = f32[2548,128]{1,0:T(8,128)S(1)} fusion(s32[1024]{0:T(1024)S(1)} %bitcast.167, f32[2548,128]{1,0:T(8,128)S(1)} %get-tuple-element.146, pred[]{:T(512)S(6)} %compare.3, bf16[12,1024,128]{2,1,0:T(8,128)(2,1)} %get-tuple-element.156, s32[]{:T(128)S(6)} %copy.14), kind=kOutput, calls=%fused_computation.6.clone.1 | convolution fusion | flops 671204352 | bytes 2875397 | tf_op jit(solution)/shard_map/while/body/eval_jaxpr/dot_general | solution.py:107
  89.2 3.2 %fusion.98 = f32[2548,128]{1,0:T(8,128)S(1)} fusion(s32[1024]{0:T(1024)S(1)} %bitcast.167, f32[2548,128]{1,0:T(8,128)S(1)} %get-tuple-element.146, pred[]{:T(512)S(6)} %compare.3, bf16[12,1024,128]{2,1,0:T(8,128)(2,1)} %get-tuple-element.156, s32[]{:T(128)S(6)} %copy.14), kind=kOutput, calls=%fused_computation.6.clone.1 | convolution fusion | flops 671204352 | bytes 2875397 | tf_op jit(solution)/shard_map/while/body/eval_jaxpr/dot_general | solution.py:107
  93.5 3.1 %fusion.98 = f32[2548,128]{1,0:T(8,128)S(1)} fusion(s32[1024]{0:T(1024)S(1)} %bitcast.167, f32[2548,128]{1,0:T(8,128)S(1)} %get-tuple-element.146, pred[]{:T(512)S(6)} %compare.3, bf16[12,1024,128]{2,1,0:T(8,128)(2,1)} %get-tuple-element.156, s32[]{:T(128)S(6)} %copy.14), kind=kOutput, calls=%fused_computation.6.clone.1 | convolution fusion | flops 671204352 | bytes 2875397 | tf_op jit(solution)/shard_map/while/body/eval_jaxpr/dot_general | solution.py:107
  97.9 3.2 %fusion.98 = f32[2548,128]{1,0:T(8,128)S(1)} fusion(s32[1024]{0:T(1024)S(1)} %bitcast.167, f32[2548,128]{1,0:T(8,128)S(1)} %get-tuple-element.146, pred[]{:T(512)S(6)} %compare.3, bf16[12,1024,128]{2,1,0:T(8,128)(2,1)} %get-tuple-element.156, s32[]{:T(128)S(6)} %copy.14), kind=kOutput, calls=%fused_computation.6.clone.1 | convolution fusion | flops 671204352 | bytes 2875397 | tf_op jit(solution)/shard_map/while/body/eval_jaxpr/dot_general | solution.py:107
  102.2 3.2 %fusion.98 = f32[2548,128]{1,0:T(8,128)S(1)} fusion(s32[1024]{0:T(1024)S(1)} %bitcast.167, f32[2548,128]{1,0:T(8,128)S(1)} %get-tuple-element.146, pred[]{:T(512)S(6)} %compare.3, bf16[12,1024,128]{2,1,0:T(8,128)(2,1)} %get-tuple-element.156, s32[]{:T(128)S(6)} %copy.14), kind=kOutput, calls=%fused_computation.6.clone.1 | convolution fusion | flops 671204352 | bytes 2875397 | tf_op jit(solution)/shard_map/while/body/eval_jaxpr/dot_general | solution.py:107
  106.6 3.1 %fusion.98 = f32[2548,128]{1,0:T(8,128)S(1)} fusion(s32[1024]{0:T(1024)S(1)} %bitcast.167, f32[2548,128]{1,0:T(8,128)S(1)} %get-tuple-element.146, pred[]{:T(512)S(6)} %compare.3, bf16[12,1024,128]{2,1,0:T(8,128)(2,1)} %get-tuple-element.156, s32[]{:T(128)S(6)} %copy.14), kind=kOutput, calls=%fused_computation.6.clone.1 | convolution fusion | flops 671204352 | bytes 2875397 | tf_op jit(solution)/shard_map/while/body/eval_jaxpr/dot_general | solution.py:107
  110.9 3.2 %fusion.98 = f32[2548,128]{1,0:T(8,128)S(1)} fusion(s32[1024]{0:T(1024)S(1)} %bitcast.167, f32[2548,128]{1,0:T(8,128)S(1)} %get-tuple-element.146, pred[]{:T(512)S(6)} %compare.3, bf16[12,1024,128]{2,1,0:T(8,128)(2,1)} %get-tuple-element.156, s32[]{:T(128)S(6)} %copy.14), kind=kOutput, calls=%fused_computation.6.clone.1 | convolution fusion | flops 671204352 | bytes 2875397 | tf_op jit(solution)/shard_map/while/body/eval_jaxpr/dot_general | solution.py:107
  115.3 3.2 %fusion.98 = f32[2548,128]{1,0:T(8,128)S(1)} fusion(s32[1024]{0:T(1024)S(1)} %bitcast.167, f32[2548,128]{1,0:T(8,128)S(1)} %get-tuple-element.146, pred[]{:T(512)S(6)} %compare.3, bf16[12,1024,128]{2,1,0:T(8,128)(2,1)} %get-tuple-element.156, s32[]{:T(128)S(6)} %copy.14), kind=kOutput, calls=%fused_computation.6.clone.1 | convolution fusion | flops 671204352 | bytes 2875397 | tf_op jit(solution)/shard_map/while/body/eval_jaxpr/dot_general | solution.py:107
  118.5 5.5 %fusion.68 = (f32[24,96]{1,0:T(8,128)S(1)}, f32[24,96]{1,0:T(8,128)S(1)}) fusion(f32[26,98]{1,0:T(8,128)S(1)} %reshape.145, f32[]{:T(128)} %bitcast.19, f32[]{:T(128)} %bitcast.18, f32[]{:T(128)} %bitcast.17, f32[]{:T(128)} %bitcast.16, f32[]{:T(128)} %bitcast.15, f32[]{:T(128)} %bitcast.14, f32[]{:T(128)} %bitcast.13, f32[]{:T(128)} %bitcast.12, f32[]{:T(128)} %bitcast), kind=kLoop, calls=%fused_computation.120 | loop fusion | flops 39168 | bytes 101412 | tf_op jit(solution)/shard_map/log1p | solution.py:137
  125.5 6.7 %fusion.20 = bf16[24,96,128]{2,1,0:T(8,128)(2,1)S(1)} fusion(f32[26,98,128]{2,1,0:T(8,128)S(1)} %reshape.144, f32[24,96]{1,0:T(8,128)S(1)} %broadcast_add_fusion, f32[]{:T(128)} %bitcast.19, f32[]{:T(128)} %bitcast.18, f32[]{:T(128)} %bitcast.17, f32[]{:T(128)} %bitcast.16, f32[]{:T(128)} %bitcast.15, f32[]{:T(128)} %bitcast.14, f32[]{:T(128)} %bitcast.13, ...), kind=kLoop, calls=%fused_computation.52 | loop fusion | flops 5603328 | bytes 11215908 | tf_op jit(solution)/shard_map/convert_element_type | solution.py:135
  133.0 4.6 %collective-permute-start.1 = (bf16[1,96,256]{2,1,0:T(8,128)(2,1)S(1)}, bf16[1,96,256]{2,1,0:T(8,128)(2,1)S(1)}, u32[]{:S(2)}, u32[]{:S(2)}) collective-permute-start(bf16[1,96,256]{2,1,0:T(8,128)(2,1)S(1)} %get-tuple-element.97), channel_id=1, source_target_pairs={{8,0},{16,8},{24,16},{32,24},{40,32},{48,40},{56,48},{64,56},{72,6... | collective-permute-start | bytes 147464 | tf_op jit(solution)/shard_map/ppermute | solution.py:47
  139.1 4.5 %collective-permute-start.2 = (bf16[26,1,256]{2,1,0:T(2,128)(2,1)S(1)}, bf16[26,1,256]{2,1,0:T(2,128)(2,1)S(1)}, u32[]{:S(2)}, u32[]{:S(2)}) collective-permute-start(bf16[26,1,256]{2,1,0:T(2,128)(2,1)S(1)} %get-tuple-element.92), channel_id=1, source_target_pairs={{0,1},{1,2},{2,3},{3,4},{4,5},{5,6},{6,7},{7,0},{8,9},{9,10},{10,1... | collective-permute-start | bytes 39944 | tf_op jit(solution)/shard_map/ppermute | solution.py:45
  144.7 3.5 %collective-permute-done.3 = bf16[26,1,256]{2,1,0:T(2,128)(2,1)S(1)} collective-permute-done((bf16[26,1,256]{2,1,0:T(2,128)(2,1)S(1)}, bf16[26,1,256]{2,1,0:T(2,128)(2,1)S(1)}, u32[]{:S(2)}, u32[]{:S(2)}) %collective-permute-start.3) | collective-permute-done | bytes 13344 | tf_op jit(solution)/shard_map/ppermute | solution.py:47
  156.7 5.4 %collective-permute-start.5 = (bf16[1,96,256]{2,1,0:T(8,128)(2,1)S(1)}, bf16[1,96,256]{2,1,0:T(8,128)(2,1)S(1)}, u32[]{:S(2)}, u32[]{:S(2)}) collective-permute-start(bf16[1,96,256]{2,1,0:T(8,128)(2,1)S(1)} %get-tuple-element.95), channel_id=1, source_target_pairs={{8,0},{16,8},{24,16},{32,24},{40,32},{48,40},{56,48},{64,56},{72,6... | collective-permute-start | bytes 147464 | tf_op jit(solution)/shard_map/ppermute | solution.py:47
  165.1 3.5 %collective-permute-done.7 = bf16[26,1,256]{2,1,0:T(2,128)(2,1)S(1)} collective-permute-done((bf16[26,1,256]{2,1,0:T(2,128)(2,1)S(1)}, bf16[26,1,256]{2,1,0:T(2,128)(2,1)S(1)}, u32[]{:S(2)}, u32[]{:S(2)}) %collective-permute-start.7) | collective-permute-done | bytes 13344 | tf_op jit(solution)/shard_map/ppermute | solution.py:47
  169.5 2.5 %fusion.70 = (bf16[24,96,256]{2,1,0:T(8,128)(2,1)S(1)}, bf16[24,96,256]{2,1,0:T(8,128)(2,1)S(1)}, bf16[24,96,256]{2,1,0:T(8,128)(2,1)S(1)}, bf16[24,96,256]{2,1,...) fusion(bf16[26,98,256]{2,1,0:T(8,128)(2,1)S(1)} %maximum_select, ...), kind=kLoop, calls=%fused_computation.121 | loop fusion | bytes 21233664 | tf_op jit(solution)/shard_map/slice | solution.py:67
  (100 shorter events, 39.2 us)
Async XLA Ops:
  0.0 132.2 %copy-start = (bf16[128,256]{1,0:T(8,128)(2,1)S(1)}, bf16[128,256]{1,0:T(8,128)(2,1)}, u32[]{:S(2)}) copy-start(bf16[128,256]{1,0:T(8,128)(2,1)} %param.14) | copy-start | bytes 196612
  20.3 7.0 %copy-start.5 = (f32[3,3]{1,0:T(4,128)S(1)}, f32[3,3]{1,0:T(4,128)}, u32[]{:S(2)}) copy-start(f32[3,3]{1,0:T(4,128)} %param.13) | copy-start | bytes 112
  20.3 46.0 %all-to-all-start.1 = ((bf16[128,1,1,96,128]{4,3,2,1,0:T(8,128)(2,1)}), bf16[128,1,1,96,128]{4,3,2,1,0:T(8,128)(2,1)}, u32[]{:S(2)}, u32[]{:S(2)}) async-start(bf16[128,1,1,96,128]{4,3,2,1,0:T(8,128)(2,1)} %bitcast.162), calls=%async_computation.1 | async-start | bytes 6291456 | tf_op jit(solution)/shard_map/all_to_all | solution.py:33
  118.4 5.7 %copy-start.2 = (f32[2548,128]{1,0:T(8,128)}, f32[2548,128]{1,0:T(8,128)S(1)}, u32[]{:S(2)}) copy-start(f32[2548,128]{1,0:T(8,128)S(1)} %get-tuple-element.38) | copy-start | bytes 3913732
  125.5 6.7 %copy-start.6 = (f32[256]{0:T(256)S(1)}, f32[256]{0:T(256)}, u32[]{:S(2)}) copy-start(f32[256]{0:T(256)} %param.15) | copy-start | bytes 3076
  132.8 6.3 %collective-permute-start = (bf16[1,96,256]{2,1,0:T(8,128)(2,1)S(1)}, bf16[1,96,256]{2,1,0:T(8,128)(2,1)S(1)}, u32[]{:S(2)}, u32[]{:S(2)}) collective-permute-start(bf16[1,96,256]{2,1,0:T(8,128)(2,1)S(1)} %get-tuple-element.96), channel_id=1, source_target_pairs={{0,8},{8,16},{16,24},{24,32},{32,40},{40,48},{48,56},{56,64},{64,7... | collective-permute-start | bytes 147464 | tf_op jit(solution)/shard_map/ppermute | solution.py:45
  133.0 6.1 %collective-permute-start.1 = (bf16[1,96,256]{2,1,0:T(8,128)(2,1)S(1)}, bf16[1,96,256]{2,1,0:T(8,128)(2,1)S(1)}, u32[]{:S(2)}, u32[]{:S(2)}) collective-permute-start(bf16[1,96,256]{2,1,0:T(8,128)(2,1)S(1)} %get-tuple-element.97), channel_id=1, source_target_pairs={{8,0},{16,8},{24,16},{32,24},{40,32},{48,40},{56,48},{64,56},{72,6... | collective-permute-start | bytes 147464 | tf_op jit(solution)/shard_map/ppermute | solution.py:47
  139.1 5.5 %collective-permute-start.2 = (bf16[26,1,256]{2,1,0:T(2,128)(2,1)S(1)}, bf16[26,1,256]{2,1,0:T(2,128)(2,1)S(1)}, u32[]{:S(2)}, u32[]{:S(2)}) collective-permute-start(bf16[26,1,256]{2,1,0:T(2,128)(2,1)S(1)} %get-tuple-element.92), channel_id=1, source_target_pairs={{0,1},{1,2},{2,3},{3,4},{4,5},{5,6},{6,7},{7,0},{8,9},{9,10},{10,1... | collective-permute-start | bytes 39944 | tf_op jit(solution)/shard_map/ppermute | solution.py:45
  143.7 4.5 %collective-permute-start.3 = (bf16[26,1,256]{2,1,0:T(2,128)(2,1)S(1)}, bf16[26,1,256]{2,1,0:T(2,128)(2,1)S(1)}, u32[]{:S(2)}, u32[]{:S(2)}) collective-permute-start(bf16[26,1,256]{2,1,0:T(2,128)(2,1)S(1)} %get-tuple-element.93), channel_id=1, source_target_pairs={{1,0},{2,1},{3,2},{4,3},{5,4},{6,5},{7,6},{0,7},{9,8},{10,9},{11,1... | collective-permute-start | bytes 39944 | tf_op jit(solution)/shard_map/ppermute | solution.py:47
  149.0 2.5 %copy-start.3 = (bf16[3,3,256,256]{3,2,1,0:T(8,128)(2,1)S(1)}, bf16[3,3,256,256]{3,2,1,0:T(8,128)(2,1)}, u32[]{:S(2)}) copy-start(bf16[3,3,256,256]{3,2,1,0:T(8,128)(2,1)} %param.16) | copy-start | bytes 3538948
  156.6 6.6 %collective-permute-start.4 = (bf16[1,96,256]{2,1,0:T(8,128)(2,1)S(1)}, bf16[1,96,256]{2,1,0:T(8,128)(2,1)S(1)}, u32[]{:S(2)}, u32[]{:S(2)}) collective-permute-start(bf16[1,96,256]{2,1,0:T(8,128)(2,1)S(1)} %get-tuple-element.94), channel_id=1, source_target_pairs={{0,8},{8,16},{16,24},{24,32},{32,40},{40,48},{48,56},{56,64},{64,7... | collective-permute-start | bytes 147464 | tf_op jit(solution)/shard_map/ppermute | solution.py:45
  156.7 6.5 %collective-permute-start.5 = (bf16[1,96,256]{2,1,0:T(8,128)(2,1)S(1)}, bf16[1,96,256]{2,1,0:T(8,128)(2,1)S(1)}, u32[]{:S(2)}, u32[]{:S(2)}) collective-permute-start(bf16[1,96,256]{2,1,0:T(8,128)(2,1)S(1)} %get-tuple-element.95), channel_id=1, source_target_pairs={{8,0},{16,8},{24,16},{32,24},{40,32},{48,40},{56,48},{64,56},{72,6... | collective-permute-start | bytes 147464 | tf_op jit(solution)/shard_map/ppermute | solution.py:47
  163.3 1.9 %collective-permute-start.6 = (bf16[26,1,256]{2,1,0:T(2,128)(2,1)S(1)}, bf16[26,1,256]{2,1,0:T(2,128)(2,1)S(1)}, u32[]{:S(2)}, u32[]{:S(2)}) collective-permute-start(bf16[26,1,256]{2,1,0:T(2,128)(2,1)S(1)} %get-tuple-element.90), channel_id=1, source_target_pairs={{0,1},{1,2},{2,3},{3,4},{4,5},{5,6},{6,7},{7,0},{8,9},{9,10},{10,1... | collective-permute-start | bytes 39944 | tf_op jit(solution)/shard_map/ppermute | solution.py:45
  164.2 4.5 %collective-permute-start.7 = (bf16[26,1,256]{2,1,0:T(2,128)(2,1)S(1)}, bf16[26,1,256]{2,1,0:T(2,128)(2,1)S(1)}, u32[]{:S(2)}, u32[]{:S(2)}) collective-permute-start(bf16[26,1,256]{2,1,0:T(2,128)(2,1)S(1)} %get-tuple-element.91), channel_id=1, source_target_pairs={{1,0},{2,1},{3,2},{4,3},{5,4},{6,5},{7,6},{0,7},{9,8},{10,9},{11,1... | collective-permute-start | bytes 39944 | tf_op jit(solution)/shard_map/ppermute | solution.py:47
  169.5 2.5 %copy-start.4 = (bf16[3,3,256,256]{3,2,1,0:T(8,128)(2,1)S(1)}, bf16[3,3,256,256]{3,2,1,0:T(8,128)(2,1)}, u32[]{:S(2)}) copy-start(bf16[3,3,256,256]{3,2,1,0:T(8,128)(2,1)} %param.17) | copy-start | bytes 3538948
  176.4 1.5 copy-start.1
where the time goes:
time: 179 us; the launch traced here: 178 us
  waiting for transfers between devices  49.9 us (28%)
  matrix products  47 us (26%)
  other arithmetic  30.4 us (17%)
  starting transfers between devices  22.6 us (13%)
  blocking collectives  18.7 us (10%)
  local copies, waits for them, and re-layouts  8.41 us (5%)
    all_to_all x1, waiting for transfers between devices, joined_exchange(): parts = lax.all_to_all(parts, axis, split_axis=0, concat_axis=0, tiled=True)  38.3 us
    dot_general x12, matrix products, add_block(): jnp.dot(onehot.astype(jnp.bfloat16), rows_blk, preferred_element_type=jnp...  37.8 us
    all_to_all x1, blocking collectives, joined_exchange(): parts = lax.all_to_all(parts, axis, split_axis=0, concat_axis=0, tiled=True)  18.7 us
    reduce_sum x12, other arithmetic, add_block(): counts = counts + jnp.sum(onehot.astype(jnp.float32), axis=1)  13.6 us
    ppermute x4, starting transfers between devices, padded_2(): lax.ppermute(head, axis, [((i + 1) % count, i) for i in range(count)])  9.93 us
    dot_general x18, matrix products, conv_tile(): jnp.dot(window, weight[row_off, col_off], preferred_element_type=jnp.floa...  8.75 us
    ppermute x4, waiting for transfers between devices, padded_2(): lax.ppermute(head, axis, [((i + 1) % count, i) for i in range(count)])  7.04 us
    all_to_all x1, starting transfers between devices, joined_exchange(): parts = lax.all_to_all(parts, axis, split_axis=0, concat_axis=0, tiled=True)  6.92 us
  transfers between devices with their start and end apart: 9, of which 7 were waited for; matrix products, arithmetic and copies ran while one was open for 0% of the time, Pallas kernels for 0%

commit v1 on v0

v1 whole, which is shorter than its diff:
```python
import functools

import jax
import jax.numpy as jnp
from jax import lax
from jax.experimental import pallas as pl
from jax.experimental.pallas import tpu as pltpu
from jax.sharding import PartitionSpec as P

TH = 24
TW = 96
F = 128
C = 256
CAP = 96
PH = 26
PW = 98
NP = 6
NQ = 16
HALF = PH // 2
SOURCES = 128
ROWS = CAP + 8
MAIN = HALF * TW
LHS = MAIN + 32
GROUPS = 4
BF = jnp.bfloat16
F32 = jnp.float32


def dot(a, b):
    return jnp.dot(a, b, preferred_element_type=F32)


def iota(shape, dim):
    return lax.broadcasted_iota(jnp.int32, shape, dim)


def with_row(tile, shift, row, at):
    rolled = pltpu.roll(tile, shift, 0)
    return jnp.where(iota(tile.shape, 0) == at, row, rolled)


def frame_kernel(
    x_ref, spread_ref, win_ref, wdens_ref, grid_ref, west_ref, east_ref, c32, lanes, acc, cnt, fr, mean, cols
):
    c32[...] = x_ref[:, CAP:, :].astype(F32).reshape(SOURCES * 8, 128)

    def placed(which):
        return [pltpu.roll(c32[pl.ds(8 * j + which, 32, stride=32), :], (96 * j) % 128, 1) for j in range(4)]

    lane = iota((32, 128), 1)

    def joined(parts):
        return [
            jnp.where(lane < 96, parts[0], parts[1]),
            jnp.where(lane < 64, parts[1], parts[2]),
            jnp.where(lane < 32, parts[2], parts[3]),
        ]

    for v, (r, pos) in enumerate(zip(joined(placed(0)), joined(placed(1)))):
        low = jnp.where(r >= HALF, r - HALF, r)
        edge = jnp.where(pos >= TW, low + HALF * (pos - TW), -1.0)
        lanes[0, v] = r
        lanes[1, v] = low
        lanes[2, v] = pos
        lanes[3, v] = edge
    upper = jnp.where(c32[pl.ds(0, SOURCES, stride=8), :] >= HALF, 1.0, 0.0)
    upper = jnp.transpose(upper)

    per = SOURCES // GROUPS
    for g in range(GROUPS):
        units = per // 4

        def row(which):
            pieces = [lanes[which, v, pl.ds(g * units + u, 1), :] for u in range(units) for v in range(3)]
            return jnp.broadcast_to(jnp.concatenate(pieces, axis=1), (16, per * CAP)).astype(BF)

        r16, low16, pos16, edge16 = (row(w) for w in range(4))
        one, zero = jnp.ones((), BF), jnp.zeros((), BF)
        ids = iota((16, per * CAP), 0).astype(F32).astype(BF)

        def hot(values, tile):
            return jnp.where(ids + jnp.asarray(16 * tile, BF) == values, one, zero)

        place = [hot(pos16, t) for t in range(8)]
        parts = []
        for k in range(HALF):
            at = jnp.where(low16 == jnp.asarray(k, BF), one, zero)
            parts += [b * at for b in place[:NP]]
        parts += [hot(edge16, 0), hot(edge16, 1)]
        left = jnp.concatenate(parts, axis=0)
        right = []
        for s in range(g * per, (g + 1) * per):
            x = x_ref[s, :CAP, :]
            up = x * jnp.broadcast_to(upper[:CAP, s : s + 1], (CAP, 128)).astype(BF)
            right.append(jnp.concatenate([x - up, up], axis=1))
        part = dot(left, jnp.concatenate(right, axis=0))
        some = lax.dot_general(
            jnp.concatenate(place, axis=0),
            jnp.concatenate([hot(r16, 0), hot(r16, 1)], axis=0),
            (((1,), (1,)), ((), ())),
            preferred_element_type=F32,
        )
        if g == 0:
            acc[...] = part
            cnt[...] = some
        else:
            acc[...] += part
            cnt[...] += some

    for r in range(PH):
        base, side = (r % HALF) * TW, (r // HALF) * 128
        lanes_of = slice(side, side + 128)
        tile = acc[base : base + TW, lanes_of].reshape(NP, NQ, 128)
        fr[r, 1 : NP + 1] = tile
        first = acc[MAIN + r % HALF : MAIN + r % HALF + 1, lanes_of]
        last = acc[MAIN + HALF + r % HALF : MAIN + HALF + r % HALF + 1, lanes_of]
        fr[r, 0] = with_row(tile[NP - 1], 1, first, 0)
        fr[r, NP + 1] = with_row(tile[0], NQ - 1, last, NQ - 1)

    number = cnt[...]
    number = [
        with_row(number[TW - NQ : TW], 1, number[TW : TW + 1], 0),
        *(number[NQ * p : NQ * (p + 1)] for p in range(NP)),
        with_row(number[:NQ], NQ - 1, number[TW + 1 : TW + 2], NQ - 1),
    ]
    density = None
    for a in range(3):
        line = [sum(spread_ref[a, b] * number[p + b] for b in range(3)) for p in range(NP)]
        line = jnp.concatenate(line, axis=0)[:, a : a + TH]
        density = line if density is None else density + line
    scale = 1.0 / (1.0 + density)
    log_density = jnp.log(1.0 + density)

    for i in range(TH):
        data = None
        for a in range(3):
            for b in range(3):
                term = spread_ref[a, b] * fr[i + a, b : b + NP]
                data = term if data is None else data + term
        data = data.reshape(TW, F) * jnp.broadcast_to(scale[:, i : i + 1], (TW, F))
        mean[i * TW : (i + 1) * TW, :] = data.astype(BF)
    step = 4
    for i in range(0, TH, step):
        out = dot(mean[i * TW : (i + step) * TW, :], win_ref[...])
        for k in range(step):
            extra = jnp.broadcast_to(log_density[:, i + k : i + k + 1], (TW, C)) * wdens_ref[...]
            cell = (out[k * TW : (k + 1) * TW] + extra).astype(BF)
            grid_ref[i + k] = cell.reshape(NP, NQ, C)
            wide = cell.astype(F32)
            for c, at in enumerate((0, NQ, 5 * NQ - 1, 6 * NQ - 1)):
                cols[c, i + k : i + k + 1, :] = wide[at : at + 1]
    west_ref[...] = cols[0:2].astype(BF)
    east_ref[...] = cols[2:4].astype(BF)


def silu(v):
    return v / (1.0 + jnp.exp(-v))


def conv_kernel(
    lat_ref, grid_ref, north_ref, south_ref, west_ref, east_ref, one_ref, two_ref, out_ref, gp, hp, cs, hs, flat
):
    lat = lat_ref[0]
    keep_top = jnp.where(lat > 0, 1.0, 0.0)
    keep_bottom = jnp.where(lat < 15, 1.0, 0.0)
    cs[...] = jnp.zeros_like(cs)
    for c in range(4):
        ref = west_ref if c < 2 else east_ref
        cs[c, 2 : 2 + TH, :] = ref[c % 2].astype(F32)
    for ref, at in ((north_ref, 0), (south_ref, 2 + TH)):
        corner = ref[2 * TW : 2 * TW + 8].astype(F32)
        for c in range(4):
            cs[c, at : at + 2, :] = corner[2 * c : 2 * c + 2]
    for g in range(TH + 4):
        if g < 2:
            tile = north_ref[g * TW : (g + 1) * TW].reshape(NP, NQ, C)
        elif g < TH + 2:
            tile = grid_ref[g - 2]
        else:
            tile = south_ref[(g - TH - 2) * TW : (g - TH - 1) * TW].reshape(NP, NQ, C)
        gp[g, 1 : NP + 1] = tile
        first, last = tile[0].astype(F32), tile[NP - 1].astype(F32)
        cs[4, g : g + 1, :] = first[:1]
        cs[5, g : g + 1, :] = last[NQ - 1 :]
        gp[g, 0] = with_row(last, 1, cs[1, g : g + 1, :], 0).astype(BF)
        gp[g, NP + 1] = with_row(first, NQ - 1, cs[2, g : g + 1, :], NQ - 1).astype(BF)

    side = None
    for a in range(3):
        for b in range(3):
            lhs = jnp.concatenate(
                [cs[(0, 1, 4)[b], a : a + 32, :], cs[(5, 2, 3)[b], a : a + 32, :]], axis=0
            ).astype(BF)
            term = dot(lhs, one_ref[3 * a + b])
            side = term if side is None else side + term
    side = silu(side)
    line = iota((64, C), 0)
    side = jnp.where((line == 0) | (line == 32), side * keep_top, side)
    side = jnp.where((line == TH + 1) | (line == TH + 33), side * keep_bottom, side)
    hs[...] = side

    def rows_of(src, weight, start, count):
        total = None
        for a in range(3):
            for b in range(3):
                window = src[start + a : start + a + count, b : b + NP].reshape(count * TW, C)
                term = dot(window, weight[3 * a + b])
                total = term if total is None else total + term
        return total

    start = 0
    for count in (4, 4, 4, 4, 4, 4, 2):
        value = silu(rows_of(gp, one_ref, start, count))
        for k in range(count):
            g = start + k
            row = value[k * TW : (k + 1) * TW]
            if g == 0:
                row = row * keep_top
            if g == TH + 1:
                row = row * keep_bottom
            row = row.reshape(NP, NQ, C)
            hp[g, 1 : NP + 1] = row.astype(BF)
            hp[g, 0] = with_row(row[NP - 1], 1, hs[g : g + 1, :], 0).astype(BF)
            hp[g, NP + 1] = with_row(row[0], NQ - 1, hs[32 + g : 33 + g, :], NQ - 1).astype(BF)
        start += count

    step = 4
    for i in range(0, TH, step):
        value = rows_of(hp, two_ref, i, step).reshape(step, NP, NQ, C)
        value = value + grid_ref[i : i + step].astype(F32)
        for k in range(step):
            for p in range(NP):
                for h in range(2):
                    flat[h, pl.ds((i + k) * TW + p, NQ, stride=NP), :] = value[k, p, :, 128 * h : 128 * (h + 1)]
        for h in range(2):
            done = flat[h, i * TW : (i + step) * TW, :].astype(BF)
            out_ref[i : i + step, :, 128 * h : 128 * (h + 1)] = done.reshape(step, TW, 128)


def vmem(count):
    return [pl.BlockSpec(memory_space=pltpu.VMEM)] * count


def smem():
    return pl.BlockSpec(memory_space=pltpu.SMEM)


LIMIT = 60 * 1024 * 1024


def frame_call(received, spread, w_in, w_dens):
    return pl.pallas_call(
        frame_kernel,
        out_shape=(
            jax.ShapeDtypeStruct((TH, NP, NQ, C), BF),
            jax.ShapeDtypeStruct((2, TH, C), BF),
            jax.ShapeDtypeStruct((2, TH, C), BF),
        ),
        in_specs=[*vmem(1), smem(), *vmem(2)],
        out_specs=tuple(vmem(3)),
        scratch_shapes=[
            pltpu.VMEM((SOURCES * 8, 128), F32),
            pltpu.VMEM((4, 3, 32, 128), F32),
            pltpu.VMEM((LHS, C), F32),
            pltpu.VMEM((128, 32), F32),
            pltpu.VMEM((PH, NP + 2, NQ, F), F32),
            pltpu.VMEM((TH * TW, F), BF),
            pltpu.VMEM((4, TH, C), F32),
        ],
        compiler_params=pltpu.CompilerParams(vmem_limit_bytes=LIMIT),
        name="frame",
    )(received, spread, w_in, w_dens.reshape(1, C))


def conv_call(lat, grid, north, south, west, east, w_one, w_two):
    return pl.pallas_call(
        conv_kernel,
        out_shape=jax.ShapeDtypeStruct((TH, TW, C), BF),
        in_specs=[smem(), *vmem(7)],
        out_specs=vmem(1)[0],
        scratch_shapes=[
            pltpu.VMEM((TH + 4, NP + 2, NQ, C), BF),
            pltpu.VMEM((TH + 2, NP + 2, NQ, C), BF),
            pltpu.VMEM((6, 40, C), F32),
            pltpu.VMEM((64, C), F32),
            pltpu.VMEM((2, TH * TW, 128), F32),
        ],
        compiler_params=pltpu.CompilerParams(vmem_limit_bytes=LIMIT),
        name="conv",
    )(lat, grid, north, south, west, east, w_one.reshape(9, C, C), w_two.reshape(9, C, C))


def payload(features, cell_index, tile_rows):
    slot = jnp.arange(CAP, dtype=jnp.int32)
    cells = cell_index.reshape(SOURCES, CAP)
    r = cells // PW
    s = cells - r * PW
    j = s - 1
    q = j // NP
    pos = (j - q * NP) * NQ + q
    pos = jnp.where(s == 0, TW, jnp.where(s == PW - 1, TW + 1, pos))
    r = jnp.where(slot[None, :] < tile_rows[:, None], r, 63)
    where = jnp.stack([r, pos], axis=1).astype(F32).astype(BF)
    where = jnp.pad(where, ((0, 0), (0, 6), (0, 128 - CAP)))
    return jnp.concatenate([features.reshape(SOURCES, CAP, F), where], axis=1)


def step(axis, by, around):
    count = lax.axis_size(axis)
    return [(i, (i + by) % count) for i in range(count) if around or 0 <= i + by < count]


def shards(features, cell_index, tile_rows, spread, w_in, w_dens, w_one, w_two):
    sent = payload(features, cell_index, tile_rows)
    received = lax.all_to_all(sent, ("lat", "lon"), split_axis=0, concat_axis=0, tiled=True)
    grid, west_cols, east_cols = frame_call(received, spread, w_in, w_dens)
    from_west = lax.ppermute(east_cols, "lon", step("lon", 1, True))
    from_east = lax.ppermute(west_cols, "lon", step("lon", -1, True))

    def edge_rows(at):
        corner = jnp.concatenate([from_west[:, at : at + 2], from_east[:, at : at + 2]], axis=0)
        return jnp.concatenate([grid[at : at + 2].reshape(2 * TW, C), corner.reshape(8, C)], axis=0)

    from_north = lax.ppermute(edge_rows(TH - 2), "lat", step("lat", 1, False))
    from_south = lax.ppermute(edge_rows(0), "lat", step("lat", -1, False))
    lat = lax.axis_index("lat").reshape(1).astype(jnp.int32)
    return conv_call(lat, grid, from_north, from_south, from_west, from_east, w_one, w_two)


def solution(mesh):
    in_specs = (
        P(("lat", "lon"), None),
        P(("lat", "lon")),
        P(("lat", "lon")),
        P(),
        P(),
        P(),
        P(),
        P(),
    )
    out_specs = P("lat", "lon", None)
    return jax.shard_map(shards, mesh=mesh, in_specs=in_specs, out_specs=out_specs, check_vma=False)
```

time: 179 us -> 100 us (0.56)
  the two profiles are of different devices: /device:TPU:7 before, /device:TPU:8 now
where the time goes in v1:
time: 100 us
  blocking collectives  54.1 us (54%)
  Pallas kernels  23.4 us (23%)
  starting transfers between devices  8.98 us (9%)
  waiting for transfers between devices  6.8 us (7%)
  other arithmetic  3.98 us (4%)
  local copies, waits for them, and re-layouts  2.74 us (3%)
    all_to_all x1, blocking collectives, shards(): lax.all_to_all(sent, ('lat', 'lon'), split_axis=0, concat_axis=0, tiled=T...  54.1 us
    pallas_call x1, Pallas kernels, frame_call(): pl.pallas_call(frame_kernel, out_shape=(jax.ShapeDtypeStruct((TH, NP, NQ,...  14.2 us
    pallas_call x1, Pallas kernels, conv_call(): pl.pallas_call(conv_kernel, out_shape=jax.ShapeDtypeStruct((TH, TW, C), B...  9.26 us
    ppermute x1, waiting for transfers between devices, shards(): from_north = lax.ppermute(edge_rows(TH - 2), 'lat', step('lat', 1, False))  5.56 us
    ppermute x1, starting transfers between devices, shards(): from_south = lax.ppermute(edge_rows(0), 'lat', step('lat', -1, False))  3.41 us
    ppermute x1, starting transfers between devices, shards(): from_east = lax.ppermute(west_cols, 'lon', step('lon', -1, True))  2.95 us
    ppermute x1, starting transfers between devices, shards(): from_north = lax.ppermute(edge_rows(TH - 2), 'lat', step('lat', 1, False))  2.61 us
    concatenate x1, other arithmetic, payload(): return jnp.concatenate([features.reshape(SOURCES, CAP, F), where], axis=1)  2.23 us
  transfers between devices with their start and end apart: 4, of which 3 were waited for; matrix products, arithmetic and copies ran while one was open for 1% of the time, Pallas kernels for 0%

profile of v1, /device:TPU:8, one launch (start us, length us, event | category | flops | bytes accessed | tf_op | source)
XLA Modules:
  0.0 100.2 jit_solution(1610752381773898379)
XLA Ops:
  0.0 0.9 reshape.178
  0.9 0.1 copy.13
  1.0 0.2 copy.16
  1.2 1.0 %compare_select_fusion.2 = (s32[128,1,96]{2,1,0:T(1,128)S(1)}, s32[128,1,96]{2,1,0:T(1,128)S(1)}) fusion(s32[128]{0:T(128)} %param.10, s32[128,1,96]{2,1,0:T(1,128)S(1)} %bitcast.11, pred[128,1,96]{2,1,0:T(4,128)(4,1)S(1)} %copy.16), kind=kLoop, calls=%fused_computation.7 | loop fusion | flops 98304 | bytes 160256 | tf_op jit(solution)/shard_map/jit(_where)/select_n | solution.py:302
  2.2 0.5 compare_select_fusion.1
  2.7 0.1 fusion.2
  2.9 2.2 %fusion.1 = bf16[128,104,128]{2,1,0:T(8,128)(2,1)S(1)} fusion(bf16[128,2,96]{2,1,0:T(2,128)(2,1)S(1)} %fusion.2, bf16[128,96,128]{2,1,0:T(8,128)(2,1)} %bitcast.8), kind=kLoop, calls=%fused_computation.2 | loop fusion | flops 10223616 | bytes 6602752 | tf_op jit(solution)/shard_map/concatenate | solution.py:305
  5.1 54.1 %all_to_all.5.x_ref = bf16[128,104,128]{2,1,0:T(8,128)(2,1)} all-to-all(bf16[128,104,128]{2,1,0:T(8,128)(2,1)S(1)} %fusion.1), channel_id=1, replica_groups=mesh['lat'=16,'lon'=8] {'lat','lon'}, dimensions={0} | all-to-all | bytes 6815744 | tf_op jit(solution)/shard_map/all_to_all | solution.py:315
  59.2 14.2 %frame.1 = (bf16[24,6,16,256]{3,2,1,0:T(8,128)(2,1)}, bf16[2,24,256]{2,1,0:T(8,128)(2,1)}, bf16[2,24,256]{2,1,0:T(8,128)(2,1)}) custom-call(bf16[128,104,128]{2,1,0:T(8,128)(2,1)} %all_to_all.5.x_ref, f32[3,3]{1,0:T(4,128)} %spread_ref.1, bf16[128,256]{1,0:T(8,128)(2,1)} %win_ref.1, f32[1,256]{1,0:T(1,128)} %bitcast.15), custom_call_target="tpu_custom_call" | custom-call | tf_op jit(solution)/shard_map/frame/pallas_call | solution.py:252
  73.4 0.0 collective-permute-start
  73.4 3.0 %collective-permute-start.1 = (bf16[2,24,256]{2,1,0:T(8,128)(2,1)}, bf16[2,24,256]{2,1,0:T(8,128)(2,1)S(1)}, u32[]{:S(2)}, u32[]{:S(2)}) collective-permute-start(bf16[2,24,256]{2,1,0:T(8,128)(2,1)} %get-tuple-element.10), channel_id=1, source_target_pairs={{0,7},{1,0},{2,1},{3,2},{4,3},{5,4},{6,5},{7,6},{8,15},{9,8},{10,9... | collective-permute-start | bytes 73736 | tf_op jit(solution)/shard_map/ppermute | solution.py:318
  76.3 1.0 fusion.3
  77.3 0.8 collective-permute-done.west_ref
  78.1 0.0 collective-permute-done.1.east_ref
  78.1 0.0 copy-start.3
  78.2 3.4 %collective-permute-start.3 = (bf16[200,256]{1,0:T(8,128)(2,1)S(1)}, bf16[200,256]{1,0:T(8,128)(2,1)S(1)}, u32[]{:S(2)}, u32[]{:S(2)}) collective-permute-start(bf16[200,256]{1,0:T(8,128)(2,1)S(1)} %pad_maximum_fusion.1), channel_id=1, source_target_pairs={{8,0},{16,8},{24,16},{32,24},{40,32},{48,40},{56,48},{64,56},{72,6... | collective-permute-start | bytes 307208 | tf_op jit(solution)/shard_map/ppermute | solution.py:325
  81.6 2.6 %collective-permute-start.2 = (bf16[200,256]{1,0:T(8,128)(2,1)S(1)}, bf16[200,256]{1,0:T(8,128)(2,1)S(1)}, u32[]{:S(2)}, u32[]{:S(2)}) collective-permute-start(bf16[200,256]{1,0:T(8,128)(2,1)S(1)} %pad_maximum_fusion), channel_id=1, source_target_pairs={{0,8},{8,16},{16,24},{24,32},{32,40},{40,48},{48,56},{56,64},{64,7... | collective-permute-start | bytes 307208 | tf_op jit(solution)/shard_map/ppermute | solution.py:324
  84.2 0.5 collective-permute-done.3.south_ref
  84.7 5.6 %collective-permute-done.2.north_ref = bf16[200,256]{1,0:T(8,128)(2,1)S(1)} collective-permute-done((bf16[200,256]{1,0:T(8,128)(2,1)S(1)}, bf16[200,256]{1,0:T(8,128)(2,1)S(1)}, u32[]{:S(2)}, u32[]{:S(2)}) %collective-permute-start.2) | collective-permute-done | bytes 102432 | tf_op jit(solution)/shard_map/ppermute | solution.py:324
  90.3 0.0 copy-done.2
  90.3 0.0 copy-done.3
  90.3 0.0 copy-done
  90.3 0.6 copy-done.1
  90.9 9.3 %conv.1 = bf16[24,96,256]{2,1,0:T(8,128)(2,1)} custom-call(s32[1]{0:T(128)} %bitcast.lat_ref, bf16[24,6,16,256]{3,2,1,0:T(8,128)(2,1)} %get-tuple-element.8.grid_ref, bf16[200,256]{1,0:T(8,128)(2,1)} %copy-done.1, bf16[200,256]{1,0:T(8,128)(2,1)} %copy-done, bf16[2,24,256]{2,1,0:T(8,128)(2,1)} %copy-done.2, bf16[2,24,256]{2,1,0:T(8,128)(2,1)} %copy-done.3, ...), custom_call_target="tpu_custom_call" | custom-call | tf_op jit(solution)/shard_map/conv/pallas_call | solution.py:276
  (11 shorter events, 0.1 us)
Async XLA Ops:
  73.4 4.7 %collective-permute-start = (bf16[2,24,256]{2,1,0:T(8,128)(2,1)}, bf16[2,24,256]{2,1,0:T(8,128)(2,1)S(1)}, u32[]{:S(2)}, u32[]{:S(2)}) collective-permute-start(bf16[2,24,256]{2,1,0:T(8,128)(2,1)} %get-tuple-element.9), channel_id=1, source_target_pairs={{0,1},{1,2},{2,3},{3,4},{4,5},{5,6},{6,7},{7,0},{8,9},{9,10},{10,1... | collective-permute-start | bytes 73736 | tf_op jit(solution)/shard_map/ppermute | solution.py:317
  73.4 4.7 %collective-permute-start.1 = (bf16[2,24,256]{2,1,0:T(8,128)(2,1)}, bf16[2,24,256]{2,1,0:T(8,128)(2,1)S(1)}, u32[]{:S(2)}, u32[]{:S(2)}) collective-permute-start(bf16[2,24,256]{2,1,0:T(8,128)(2,1)} %get-tuple-element.10), channel_id=1, source_target_pairs={{0,7},{1,0},{2,1},{3,2},{4,3},{5,4},{6,5},{7,6},{8,15},{9,8},{10,9... | collective-permute-start | bytes 73736 | tf_op jit(solution)/shard_map/ppermute | solution.py:318
  78.1 12.2 %copy-start.2 = (bf16[2,24,256]{2,1,0:T(8,128)(2,1)}, bf16[2,24,256]{2,1,0:T(8,128)(2,1)S(1)}, u32[]{:S(2)}) copy-start(bf16[2,24,256]{2,1,0:T(8,128)(2,1)S(1)} %collective-permute-done.west_ref) | copy-start | bytes 73732
  78.1 12.2 %copy-start.3 = (bf16[2,24,256]{2,1,0:T(8,128)(2,1)}, bf16[2,24,256]{2,1,0:T(8,128)(2,1)S(1)}, u32[]{:S(2)}) copy-start(bf16[2,24,256]{2,1,0:T(8,128)(2,1)S(1)} %collective-permute-done.1.east_ref) | copy-start | bytes 73732
  78.2 6.6 %collective-permute-start.3 = (bf16[200,256]{1,0:T(8,128)(2,1)S(1)}, bf16[200,256]{1,0:T(8,128)(2,1)S(1)}, u32[]{:S(2)}, u32[]{:S(2)}) collective-permute-start(bf16[200,256]{1,0:T(8,128)(2,1)S(1)} %pad_maximum_fusion.1), channel_id=1, source_target_pairs={{8,0},{16,8},{24,16},{32,24},{40,32},{48,40},{56,48},{64,56},{72,6... | collective-permute-start | bytes 307208 | tf_op jit(solution)/shard_map/ppermute | solution.py:325
  81.6 8.7 %collective-permute-start.2 = (bf16[200,256]{1,0:T(8,128)(2,1)S(1)}, bf16[200,256]{1,0:T(8,128)(2,1)S(1)}, u32[]{:S(2)}, u32[]{:S(2)}) collective-permute-start(bf16[200,256]{1,0:T(8,128)(2,1)S(1)} %pad_maximum_fusion), channel_id=1, source_target_pairs={{0,8},{8,16},{16,24},{24,32},{32,40},{40,48},{48,56},{56,64},{64,7... | collective-permute-start | bytes 307208 | tf_op jit(solution)/shard_map/ppermute | solution.py:324
  84.7 5.6 %copy-start = (bf16[200,256]{1,0:T(8,128)(2,1)}, bf16[200,256]{1,0:T(8,128)(2,1)S(1)}, u32[]{:S(2)}) copy-start(bf16[200,256]{1,0:T(8,128)(2,1)S(1)} %collective-permute-done.3.south_ref) | copy-start | bytes 307204
  90.3 0.6 copy-start.1

commit v2 on v1

--- a/solution.py
+++ b/solution.py
@@ -18,10 +18,12 @@
 NQ = 16
 HALF = PH // 2
 SOURCES = 128
-ROWS = CAP + 8
+ROWS = CAP + 2
+PAIRS = ROWS // 2
 MAIN = HALF * TW
 LHS = MAIN + 32
-GROUPS = 4
+GROUPS = 7
+PER = ROWS // GROUPS
 BF = jnp.bfloat16
 F32 = jnp.float32
 
@@ -39,44 +41,81 @@
     return jnp.where(iota(tile.shape, 0) == at, row, rolled)
 
 
+def send_kernel(shift_ref, features_ref, cells_ref, used_ref, out_ref, flat, where, sems):
+    cut = SOURCES // 4
+    copies = [
+        pltpu.make_async_copy(
+            features_ref.at[cut * k : cut * (k + 1)],
+            out_ref.at[cut * k : cut * (k + 1), 0 : PAIRS - 1],
+            sems.at[k],
+        )
+        for k in range(4)
+    ]
+    for copy in copies:
+        copy.start()
+    lines = [cells_ref[pl.ds(v, 32, stride=3), :].astype(F32) for v in range(3)]
+    lane = iota((32, 128), 1)
+    cells = [
+        lines[0],
+        jnp.where(lane < 32, pltpu.roll(lines[0], 32, 1), pltpu.roll(lines[1], 32, 1)),
+        jnp.where(lane < 64, pltpu.roll(lines[1], 64, 1), pltpu.roll(lines[2], 64, 1)),
+        pltpu.roll(lines[2], 96, 1),
+    ]
+    for j, cell in enumerate(cells):
+        r = jnp.floor((cell + 0.5) * (1.0 / PW))
+        s = cell - r * PW
+        q = jnp.floor((s - 0.5) * (1.0 / NP))
+        pos = (s - 1.0 - q * NP) * NQ + q
+        pos = jnp.where(s == 0.0, float(TW), jnp.where(s == PW - 1.0, TW + 1.0, pos))
+        r = jnp.where(lane < used_ref[:, j : j + 1], r, 63.0)
+        flat[pl.ds(2 * j, 32, stride=8), :] = pltpu.roll(r, shift_ref[0], 1)
+        flat[pl.ds(2 * j + 1, 32, stride=8), :] = pltpu.roll(pos, shift_ref[0], 1)
+    for t in range(SOURCES):
+        where[t, 0] = flat[2 * t : 2 * t + 2, :].astype(BF)
+    last = pltpu.make_async_copy(where, out_ref.at[:, PAIRS - 1 : PAIRS], sems.at[4])
+    last.start()
+    for copy in copies:
+        copy.wait()
+    last.wait()
+
+
 def frame_kernel(
-    x_ref, spread_ref, win_ref, wdens_ref, grid_ref, west_ref, east_ref, c32, lanes, acc, cnt, fr, mean, cols
+    x_ref, where_ref, spread_ref, win_ref, wdens_ref, grid_ref, west_ref, east_ref, c32, lanes, acc, cnt, fr, mean, cols
 ):
-    c32[...] = x_ref[:, CAP:, :].astype(F32).reshape(SOURCES * 8, 128)
-
-    def placed(which):
-        return [pltpu.roll(c32[pl.ds(8 * j + which, 32, stride=32), :], (96 * j) % 128, 1) for j in range(4)]
-
-    lane = iota((32, 128), 1)
-
-    def joined(parts):
-        return [
-            jnp.where(lane < 96, parts[0], parts[1]),
-            jnp.where(lane < 64, parts[1], parts[2]),
-            jnp.where(lane < 32, parts[2], parts[3]),
-        ]
-
-    for v, (r, pos) in enumerate(zip(joined(placed(0)), joined(placed(1)))):
-        low = jnp.where(r >= HALF, r - HALF, r)
-        edge = jnp.where(pos >= TW, low + HALF * (pos - TW), -1.0)
-        lanes[0, v] = r
-        lanes[1, v] = low
-        lanes[2, v] = pos
-        lanes[3, v] = edge
-    upper = jnp.where(c32[pl.ds(0, SOURCES, stride=8), :] >= HALF, 1.0, 0.0)
-    upper = jnp.transpose(upper)
-
-    per = SOURCES // GROUPS
+    for t in range(SOURCES):
+        c32[2 * t : 2 * t + 2, :] = where_ref[t, PAIRS - 1].astype(F32)
+    both = jnp.concatenate([c32[pl.ds(w, SOURCES, stride=2), :] for w in range(2)], axis=1).astype(BF)
+    high = 104
+    tile = iota((high, 128), 0).astype(F32) * 128.0
+    first = jnp.floor((tile + 0.5) * (1.0 / ROWS))
+    source = iota((high, 128), 1).astype(F32)
+    picked = [dot(jnp.where(source == first + k, 1.0, 0.0).astype(BF), both) for k in range(3)]
+    bound = (first + 1.0) * ROWS - tile
+
+    def joined(side):
+        parts = [part[:, 128 * side : 128 * (side + 1)] for part in picked]
+        return jnp.where(source < bound, parts[0], jnp.where(source < bound + ROWS, parts[1], parts[2]))
+
+    r, pos = joined(0), joined(1)
+    low = jnp.where(r >= HALF, r - HALF, r)
+    lanes[0] = r
+    lanes[1] = low
+    lanes[2] = pos
+    lanes[3] = jnp.where(pos >= TW, low + HALF * (pos - TW), -1.0)
+    upper = jnp.where(r >= HALF, 1.0, 0.0)
+    upper = jnp.transpose(jnp.concatenate([upper, jnp.zeros((128 - high, 128), F32)], axis=0))
+
     for g in range(GROUPS):
-        units = per // 4
+        tiles = range(g * PER, (g + 1) * PER)
+        width = PER * 128
 
         def row(which):
-            pieces = [lanes[which, v, pl.ds(g * units + u, 1), :] for u in range(units) for v in range(3)]
-            return jnp.broadcast_to(jnp.concatenate(pieces, axis=1), (16, per * CAP)).astype(BF)
+            pieces = [lanes[which, t : t + 1, :] for t in tiles]
+            return jnp.broadcast_to(jnp.concatenate(pieces, axis=1), (16, width)).astype(BF)
 
         r16, low16, pos16, edge16 = (row(w) for w in range(4))
         one, zero = jnp.ones((), BF), jnp.zeros((), BF)
-        ids = iota((16, per * CAP), 0).astype(F32).astype(BF)
+        ids = iota((16, width), 0).astype(F32).astype(BF)
 
         def hot(values, tile):
             return jnp.where(ids + jnp.asarray(16 * tile, BF) == values, one, zero)
@@ -89,9 +128,9 @@
         parts += [hot(edge16, 0), hot(edge16, 1)]
         left = jnp.concatenate(parts, axis=0)
         right = []
-        for s in range(g * per, (g + 1) * per):
-            x = x_ref[s, :CAP, :]
-            up = x * jnp.broadcast_to(upper[:CAP, s : s + 1], (CAP, 128)).astype(BF)
+        for t in tiles:
+            x = x_ref[128 * t : 128 * (t + 1), :]
+            up = x * jnp.broadcast_to(upper[:, t : t + 1], (128, 128)).astype(BF)
             right.append(jnp.concatenate([x - up, up], axis=1))
         part = dot(left, jnp.concatenate(right, axis=0))
         some = lax.dot_general(
@@ -158,7 +197,7 @@
 
 
 def conv_kernel(
-    lat_ref, grid_ref, north_ref, south_ref, west_ref, east_ref, one_ref, two_ref, out_ref, gp, hp, cs, hs, flat
+    lat_ref, grid_ref, north_ref, south_ref, west_ref, east_ref, one_ref, two_ref, out_ref, gp, hp, cs, hs, flat, done, sems
 ):
     lat = lat_ref[0]
     keep_top = jnp.where(lat > 0, 1.0, 0.0)
@@ -225,6 +264,7 @@
         start += count
 
     step = 4
+    copies = []
     for i in range(0, TH, step):
         value = rows_of(hp, two_ref, i, step).reshape(step, NP, NQ, C)
         value = value + grid_ref[i : i + step].astype(F32)
@@ -233,8 +273,13 @@
                 for h in range(2):
                     flat[h, pl.ds((i + k) * TW + p, NQ, stride=NP), :] = value[k, p, :, 128 * h : 128 * (h + 1)]
         for h in range(2):
-            done = flat[h, i * TW : (i + step) * TW, :].astype(BF)
-            out_ref[i : i + step, :, 128 * h : 128 * (h + 1)] = done.reshape(step, TW, 128)
+            block = flat[h, i * TW : (i + step) * TW, :].astype(BF)
+            done[i : i + step, :, 128 * h : 128 * (h + 1)] = block.reshape(step, TW, 128)
+        copy = pltpu.make_async_copy(done.at[i : i + step], out_ref.at[i : i + step], sems.at[i // step])
+        copy.start()
+        copies.append(copy)
+    for copy in copies:
+        copy.wait()
 
 
 def vmem(count):
@@ -245,22 +290,44 @@
     return pl.BlockSpec(memory_space=pltpu.SMEM)
 
 
-LIMIT = 60 * 1024 * 1024
+LIMIT = 40 * 1024 * 1024
+
+
+def near(value):
+    return pltpu.with_memory_space_constraint(value, pltpu.VMEM)
+
+
+def send_call(features, cell_index, tile_rows):
+    here = lax.axis_index("lat") * lax.axis_size("lon") + lax.axis_index("lon")
+    shift = lax.rem(here * ROWS, 128).reshape(1).astype(jnp.int32)
+    return pl.pallas_call(
+        send_kernel,
+        out_shape=pltpu.VMEM((SOURCES, PAIRS, 2, F), BF),
+        in_specs=[smem(), pl.BlockSpec(memory_space=pl.ANY), *vmem(2)],
+        out_specs=vmem(1)[0],
+        scratch_shapes=[
+            pltpu.VMEM((2 * SOURCES, 128), F32),
+            pltpu.VMEM((SOURCES, 1, 2, F), BF),
+            pltpu.SemaphoreType.DMA((5,)),
+        ],
+        compiler_params=pltpu.CompilerParams(vmem_limit_bytes=LIMIT),
+        name="send",
+    )(shift, features.reshape(SOURCES, PAIRS - 1, 2, F), cell_index.reshape(96, 128), tile_rows.reshape(32, 4))
 
 
 def frame_call(received, spread, w_in, w_dens):
     return pl.pallas_call(
         frame_kernel,
         out_shape=(
-            jax.ShapeDtypeStruct((TH, NP, NQ, C), BF),
-            jax.ShapeDtypeStruct((2, TH, C), BF),
-            jax.ShapeDtypeStruct((2, TH, C), BF),
+            pltpu.VMEM((TH, NP, NQ, C), BF),
+            pltpu.VMEM((2, TH, C), BF),
+            pltpu.VMEM((2, TH, C), BF),
         ),
-        in_specs=[*vmem(1), smem(), *vmem(2)],
+        in_specs=[*vmem(2), smem(), *vmem(2)],
         out_specs=tuple(vmem(3)),
         scratch_shapes=[
-            pltpu.VMEM((SOURCES * 8, 128), F32),
-            pltpu.VMEM((4, 3, 32, 128), F32),
+            pltpu.VMEM((SOURCES * 2, 128), F32),
+            pltpu.VMEM((4, 104, 128), F32),
             pltpu.VMEM((LHS, C), F32),
             pltpu.VMEM((128, 32), F32),
             pltpu.VMEM((PH, NP + 2, NQ, F), F32),
@@ -269,7 +336,7 @@
         ],
         compiler_params=pltpu.CompilerParams(vmem_limit_bytes=LIMIT),
         name="frame",
-    )(received, spread, w_in, w_dens.reshape(1, C))
+    )(near(received.reshape(SOURCES * ROWS, F)), near(received), spread, near(w_in), near(w_dens.reshape(1, C)))
 
 
 def conv_call(lat, grid, north, south, west, east, w_one, w_two):
@@ -277,32 +344,28 @@
         conv_kernel,
         out_shape=jax.ShapeDtypeStruct((TH, TW, C), BF),
         in_specs=[smem(), *vmem(7)],
-        out_specs=vmem(1)[0],
+        out_specs=pl.BlockSpec(memory_space=pl.ANY),
         scratch_shapes=[
             pltpu.VMEM((TH + 4, NP + 2, NQ, C), BF),
             pltpu.VMEM((TH + 2, NP + 2, NQ, C), BF),
             pltpu.VMEM((6, 40, C), F32),
             pltpu.VMEM((64, C), F32),
             pltpu.VMEM((2, TH * TW, 128), F32),
+            pltpu.VMEM((TH, TW, C), BF),
+            pltpu.SemaphoreType.DMA((6,)),
         ],
         compiler_params=pltpu.CompilerParams(vmem_limit_bytes=LIMIT),
         name="conv",
-    )(lat, grid, north, south, west, east, w_one.reshape(9, C, C), w_two.reshape(9, C, C))
-
-
-def payload(features, cell_index, tile_rows):
-    slot = jnp.arange(CAP, dtype=jnp.int32)
-    cells = cell_index.reshape(SOURCES, CAP)
-    r = cells // PW
-    s = cells - r * PW
-    j = s - 1
-    q = j // NP
-    pos = (j - q * NP) * NQ + q
-    pos = jnp.where(s == 0, TW, jnp.where(s == PW - 1, TW + 1, pos))
-    r = jnp.where(slot[None, :] < tile_rows[:, None], r, 63)
-    where = jnp.stack([r, pos], axis=1).astype(F32).astype(BF)
-    where = jnp.pad(where, ((0, 0), (0, 6), (0, 128 - CAP)))
-    return jnp.concatenate([features.reshape(SOURCES, CAP, F), where], axis=1)
+    )(
+        lat,
+        near(grid),
+        near(north),
+        near(south),
+        near(west),
+        near(east),
+        near(w_one.reshape(9, C, C)),
+        near(w_two.reshape(9, C, C)),
+    )
 
 
 def step(axis, by, around):
@@ -311,7 +374,7 @@
 
 
 def shards(features, cell_index, tile_rows, spread, w_in, w_dens, w_one, w_two):
-    sent = payload(features, cell_index, tile_rows)
+    sent = send_call(features, cell_index, tile_rows)
     received = lax.all_to_all(sent, ("lat", "lon"), split_axis=0, concat_axis=0, tiled=True)
     grid, west_cols, east_cols = frame_call(received, spread, w_in, w_dens)
     from_west = lax.ppermute(east_cols, "lon", step("lon", 1, True))

time: 100 us -> 95 us (0.950); the launches traced: 100 us -> 93.9 us
  local copies, waits for them, and re-layouts: 2.74 us -> 6.85 us
  waiting for transfers between devices: 6.8 us -> 2.87 us
  Pallas kernels: 23.4 us -> 19.5 us
  blocking collectives: 54.1 us -> 51.5 us
  other arithmetic: 3.98 us -> 1.82 us
  starting transfers between devices: 8.98 us -> 11.1 us
    ppermute x1, waiting for transfers between devices: 5.56 us -> 0.01 us  [shards(): from_north = lax.ppermute(edge_rows(TH - 2), 'lat', step('lat', 1, False))]
    unnamed x8 -> x22, local copies, waits for them, and re-layouts: 0.63 us -> 5.38 us
    all_to_all x1, blocking collectives: 54.1 us -> 51.5 us  [shards(): lax.all_to_all(sent, ('lat', 'lon'), split_axis=0, concat_axis=0, tiled=T...]
    pallas_call x1, Pallas kernels: 9.26 us -> 6.87 us  [conv_call(): pl.pallas_call(conv_kernel, out_shape=jax.ShapeDtypeStruct((TH, TW, C), B...]
    concatenate x1 -> x0, other arithmetic: 2.23 us -> none  [payload(): return jnp.concatenate([features.reshape(SOURCES, CAP, F), where], axis=1)]
    ppermute x1, starting transfers between devices: 3.41 us -> 5.46 us  [shards(): from_south = lax.ppermute(edge_rows(0), 'lat', step('lat', -1, False))]
    concatenate x2, other arithmetic: 0.02 us -> 1.8 us  [edge_rows(): jnp.concatenate([grid[at:at + 2].reshape(2 * TW, C), corner.reshape(8, C)...]
    ppermute x1, waiting for transfers between devices: 0.48 us -> 2.04 us  [shards(): from_south = lax.ppermute(edge_rows(0), 'lat', step('lat', -1, False))]
  transfers between devices with their start and end apart: 4 -> 4, of which waited for: 3 -> 2; matrix products, arithmetic and copies ran while one was open for 1% -> 2% of each run, Pallas kernels for 0% -> 0%
where the time goes in v2:
time: 95 us; the launch traced here: 93.9 us
  blocking collectives  51.5 us (54%)
  Pallas kernels  19.5 us (21%)
  starting transfers between devices  11.1 us (12%)
  local copies, waits for them, and re-layouts  6.85 us (7%)
  waiting for transfers between devices  2.87 us (3%)
  other arithmetic  1.82 us (2%)
    all_to_all x1, blocking collectives, shards(): lax.all_to_all(sent, ('lat', 'lon'), split_axis=0, concat_axis=0, tiled=T...  51.5 us
    pallas_call x1, Pallas kernels, frame_call(): pl.pallas_call(frame_kernel, out_shape=(pltpu.VMEM((TH, NP, NQ, C), BF),...  12.1 us
    pallas_call x1, Pallas kernels, conv_call(): pl.pallas_call(conv_kernel, out_shape=jax.ShapeDtypeStruct((TH, TW, C), B...  6.87 us
    ppermute x1, starting transfers between devices, shards(): from_south = lax.ppermute(edge_rows(0), 'lat', step('lat', -1, False))  5.46 us
    unnamed x22, local copies, waits for them, and re-layouts  5.38 us
    ppermute x1, starting transfers between devices, shards(): from_east = lax.ppermute(west_cols, 'lon', step('lon', -1, True))  2.94 us
    ppermute x1, starting transfers between devices, shards(): from_north = lax.ppermute(edge_rows(TH - 2), 'lat', step('lat', 1, False))  2.65 us
    ppermute x1, waiting for transfers between devices, shards(): from_south = lax.ppermute(edge_rows(0), 'lat', step('lat', -1, False))  2.04 us
  transfers between devices with their start and end apart: 4, of which 2 were waited for; matrix products, arithmetic and copies ran while one was open for 2% of the time, Pallas kernels for 0%

profile of v2, /device:TPU:8, one launch (start us, length us, event | category | flops | bytes accessed | tf_op | source)
XLA Modules:
  0.0 93.9 jit_solution(17075617603405076665)
XLA Ops:
  0.0 0.7 reshape.43.used_ref
  0.8 0.0 copy-start
  0.8 1.9 %copy-done = bf16[12288,128]{1,0:T(8,128)(2,1)S(1)} copy-done((bf16[12288,128]{1,0:T(8,128)(2,1)S(1)}, bf16[12288,128]{1,0:T(8,128)(2,1)}, u32[]{:S(2)}) %copy-start) | copy-done | bytes 3145752
  2.7 0.8 copy-done.4
  3.5 0.5 send.1
  4.0 0.0 copy-start.9
  4.0 0.0 copy-start.10
  4.0 51.5 %all_to_all.5.where_ref = bf16[128,49,2,128]{3,2,1,0:T(2,128)(2,1)S(1)} all-to-all(bf16[128,49,2,128]{3,2,1,0:T(2,128)(2,1)S(1)} %send.1), channel_id=1, replica_groups=mesh['lat'=16,'lon'=8] {'lat','lon'}, dimensions={0} | all-to-all | bytes 6422528 | tf_op jit(solution)/shard_map/all_to_all | solution.py:378
  55.5 0.0 copy-start.1
  55.6 12.1 %frame.1 = (bf16[24,6,16,256]{3,2,1,0:T(8,128)(2,1)S(1)}, bf16[2,24,256]{2,1,0:T(8,128)(2,1)S(1)}, bf16[2,24,256]{2,1,0:T(8,128)(2,1)S(1)}) custom-call(bf16[12544,128]{1,0:T(8,128)(2,1)S(1)} %bitcast.10, bf16[128,49,2,128]{3,2,1,0:T(2,128)(2,1)S(1)} %all_to_all.5.where_ref, f32[3,3]{1,0:T(4,128)S(1)} %copy-done.9, bf16[128,256]{1,0:T(8,128)(2,1)S(1)} %copy-done.3, ...), custom_call_target="tpu_custom_call" | custom-call | tf_op jit(solution)/shard_map/frame/pallas_call | solution.py:319
  67.7 0.0 collective-permute-start
  67.7 2.9 %collective-permute-start.1 = (bf16[2,24,256]{2,1,0:T(8,128)(2,1)S(1)}, bf16[2,24,256]{2,1,0:T(8,128)(2,1)S(1)}, u32[]{:S(2)}, u32[]{:S(2)}) collective-permute-start(bf16[2,24,256]{2,1,0:T(8,128)(2,1)S(1)} %get-tuple-element.10), channel_id=1, source_target_pairs={{0,7},{1,0},{2,1},{3,2},{4,3},{5,4},{6,5},{7,6},{8,15},{9,8},{10,9... | collective-permute-start | bytes 73736 | tf_op jit(solution)/shard_map/ppermute | solution.py:381
  70.6 0.7 fusion
  71.3 0.8 collective-permute-done.west_ref
  72.2 0.6 copy-done.5
  72.8 0.6 copy-done.7
  73.4 0.9 pad_maximum_fusion
  74.3 2.6 %collective-permute-start.2 = (bf16[200,256]{1,0:T(8,128)(2,1)S(1)}, bf16[200,256]{1,0:T(8,128)(2,1)S(1)}, u32[]{:S(2)}, u32[]{:S(2)}) collective-permute-start(bf16[200,256]{1,0:T(8,128)(2,1)S(1)} %pad_maximum_fusion), channel_id=1, source_target_pairs={{0,8},{8,16},{16,24},{24,32},{32,40},{40,48},{48,56},{56,64},{64,7... | collective-permute-start | bytes 307208 | tf_op jit(solution)/shard_map/ppermute | solution.py:387
  77.0 0.9 pad_maximum_fusion.1
  77.9 5.5 %collective-permute-start.3 = (bf16[200,256]{1,0:T(8,128)(2,1)S(1)}, bf16[200,256]{1,0:T(8,128)(2,1)S(1)}, u32[]{:S(2)}, u32[]{:S(2)}) collective-permute-start(bf16[200,256]{1,0:T(8,128)(2,1)S(1)} %pad_maximum_fusion.1), channel_id=1, source_target_pairs={{8,0},{16,8},{24,16},{32,24},{40,32},{48,40},{56,48},{64,56},{72,6... | collective-permute-start | bytes 307208 | tf_op jit(solution)/shard_map/ppermute | solution.py:388
  83.4 2.0 %collective-permute-done.3.south_ref = bf16[200,256]{1,0:T(8,128)(2,1)S(1)} collective-permute-done((bf16[200,256]{1,0:T(8,128)(2,1)S(1)}, bf16[200,256]{1,0:T(8,128)(2,1)S(1)}, u32[]{:S(2)}, u32[]{:S(2)}) %collective-permute-start.3) | collective-permute-done | bytes 102432 | tf_op jit(solution)/shard_map/ppermute | solution.py:388
  85.4 0.7 copy-done.6
  86.1 0.7 copy-done.8
  86.9 6.9 %conv.1 = bf16[24,96,256]{2,1,0:T(8,128)(2,1)} custom-call(s32[1]{0:T(128)} %bitcast.lat_ref, bf16[24,6,16,256]{3,2,1,0:T(8,128)(2,1)S(1)} %get-tuple-element.8.grid_ref, bf16[200,256]{1,0:T(8,128)(2,1)S(1)} %collective-permute-done.2.north_ref, bf16[200,256]{1,0:T(8,128)(2,1)S(1)} %collective-permute-done.3.south_ref, bf16[2,24,256]{2,1,0:T(8,128)(2,1)S(1)} %copy-done.6, ...), custom_call_target="tpu_custom_call" | custom-call | tf_op jit(solution)/shard_map/conv/pallas_call | solution.py:343
  (19 shorter events, 0.1 us)
Async XLA Ops:
  0.8 1.9 %copy-start = (bf16[12288,128]{1,0:T(8,128)(2,1)S(1)}, bf16[12288,128]{1,0:T(8,128)(2,1)}, u32[]{:S(2)}) copy-start(bf16[12288,128]{1,0:T(8,128)(2,1)} %param.8) | copy-start | bytes 9437188
  2.7 0.8 copy-start.4
  4.0 51.5 %copy-start.3 = (bf16[128,256]{1,0:T(8,128)(2,1)S(1)}, bf16[128,256]{1,0:T(8,128)(2,1)}, u32[]{:S(2)}) copy-start(bf16[128,256]{1,0:T(8,128)(2,1)} %win_ref.1) | copy-start | bytes 196612
  4.0 51.5 %copy-start.9 = (f32[3,3]{1,0:T(4,128)S(1)}, f32[3,3]{1,0:T(4,128)}, u32[]{:S(2)}) copy-start(f32[3,3]{1,0:T(4,128)} %spread_ref.1) | copy-start | bytes 112
  4.0 51.5 %copy-start.10 = (f32[256]{0:T(256)S(1)}, f32[256]{0:T(256)}, u32[]{:S(2)}) copy-start(f32[256]{0:T(256)} %param.13) | copy-start | bytes 3076
  55.5 29.9 %copy-start.1 = (bf16[3,3,256,256]{3,2,1,0:T(8,128)(2,1)S(1)}, bf16[3,3,256,256]{3,2,1,0:T(8,128)(2,1)}, u32[]{:S(2)}) copy-start(bf16[3,3,256,256]{3,2,1,0:T(8,128)(2,1)} %param.14) | copy-start | bytes 3538948
  55.5 29.9 %copy-start.2 = (bf16[3,3,256,256]{3,2,1,0:T(8,128)(2,1)S(1)}, bf16[3,3,256,256]{3,2,1,0:T(8,128)(2,1)}, u32[]{:S(2)}) copy-start(bf16[3,3,256,256]{3,2,1,0:T(8,128)(2,1)} %param.15) | copy-start | bytes 3538948
  67.7 4.5 %collective-permute-start = (bf16[2,24,256]{2,1,0:T(8,128)(2,1)S(1)}, bf16[2,24,256]{2,1,0:T(8,128)(2,1)S(1)}, u32[]{:S(2)}, u32[]{:S(2)}) collective-permute-start(bf16[2,24,256]{2,1,0:T(8,128)(2,1)S(1)} %get-tuple-element.9), channel_id=1, source_target_pairs={{0,1},{1,2},{2,3},{3,4},{4,5},{5,6},{6,7},{7,0},{8,9},{9,10},{10,1... | collective-permute-start | bytes 73736 | tf_op jit(solution)/shard_map/ppermute | solution.py:380
  67.7 5.1 %collective-permute-start.1 = (bf16[2,24,256]{2,1,0:T(8,128)(2,1)S(1)}, bf16[2,24,256]{2,1,0:T(8,128)(2,1)S(1)}, u32[]{:S(2)}, u32[]{:S(2)}) collective-permute-start(bf16[2,24,256]{2,1,0:T(8,128)(2,1)S(1)} %get-tuple-element.10), channel_id=1, source_target_pairs={{0,7},{1,0},{2,1},{3,2},{4,3},{5,4},{6,5},{7,6},{8,15},{9,8},{10,9... | collective-permute-start | bytes 73736 | tf_op jit(solution)/shard_map/ppermute | solution.py:381
  72.2 0.6 copy-start.5
  72.8 0.6 copy-start.7
  74.3 9.0 %collective-permute-start.2 = (bf16[200,256]{1,0:T(8,128)(2,1)S(1)}, bf16[200,256]{1,0:T(8,128)(2,1)S(1)}, u32[]{:S(2)}, u32[]{:S(2)}) collective-permute-start(bf16[200,256]{1,0:T(8,128)(2,1)S(1)} %pad_maximum_fusion), channel_id=1, source_target_pairs={{0,8},{8,16},{16,24},{24,32},{32,40},{40,48},{48,56},{56,64},{64,7... | collective-permute-start | bytes 307208 | tf_op jit(solution)/shard_map/ppermute | solution.py:387
  77.9 7.5 %collective-permute-start.3 = (bf16[200,256]{1,0:T(8,128)(2,1)S(1)}, bf16[200,256]{1,0:T(8,128)(2,1)S(1)}, u32[]{:S(2)}, u32[]{:S(2)}) collective-permute-start(bf16[200,256]{1,0:T(8,128)(2,1)S(1)} %pad_maximum_fusion.1), channel_id=1, source_target_pairs={{8,0},{16,8},{24,16},{32,24},{40,32},{48,40},{56,48},{64,56},{72,6... | collective-permute-start | bytes 307208 | tf_op jit(solution)/shard_map/ppermute | solution.py:388
  85.4 0.7 copy-start.6
  86.1 0.7 copy-start.8

commit v3 on v2

--- a/solution.py
+++ b/solution.py
@@ -21,6 +21,7 @@
 ROWS = CAP + 2
 PAIRS = ROWS // 2
 MAIN = HALF * TW
+EDGE = 2 * TW + 8
 LHS = MAIN + 32
 GROUPS = 7
 PER = ROWS // GROUPS
@@ -41,7 +42,9 @@
     return jnp.where(iota(tile.shape, 0) == at, row, rolled)
 
 
-def send_kernel(shift_ref, features_ref, cells_ref, used_ref, out_ref, flat, where, sems):
+def send_kernel(shift_ref, features_ref, index_ref, used_ref, out_ref, cells, flat, where, used, sems):
+    fetch = pltpu.make_async_copy(index_ref, cells, sems.at[5])
+    fetch.start()
     cut = SOURCES // 4
     copies = [
         pltpu.make_async_copy(
@@ -53,21 +56,24 @@
     ]
     for copy in copies:
         copy.start()
-    lines = [cells_ref[pl.ds(v, 32, stride=3), :].astype(F32) for v in range(3)]
+    count = jnp.broadcast_to(used_ref[...].astype(F32), (128, 128))
+    used[...] = jnp.transpose(count)
+    fetch.wait()
+    lines = [cells[pl.ds(v, 32, stride=3), :].astype(F32) for v in range(3)]
     lane = iota((32, 128), 1)
-    cells = [
+    blocks = [
         lines[0],
         jnp.where(lane < 32, pltpu.roll(lines[0], 32, 1), pltpu.roll(lines[1], 32, 1)),
         jnp.where(lane < 64, pltpu.roll(lines[1], 64, 1), pltpu.roll(lines[2], 64, 1)),
         pltpu.roll(lines[2], 96, 1),
     ]
-    for j, cell in enumerate(cells):
+    for j, cell in enumerate(blocks):
         r = jnp.floor((cell + 0.5) * (1.0 / PW))
         s = cell - r * PW
         q = jnp.floor((s - 0.5) * (1.0 / NP))
         pos = (s - 1.0 - q * NP) * NQ + q
         pos = jnp.where(s == 0.0, float(TW), jnp.where(s == PW - 1.0, TW + 1.0, pos))
-        r = jnp.where(lane < used_ref[:, j : j + 1], r, 63.0)
+        r = jnp.where(lane.astype(F32) < used[pl.ds(j, 32, stride=4), :], r, 63.0)
         flat[pl.ds(2 * j, 32, stride=8), :] = pltpu.roll(r, shift_ref[0], 1)
         flat[pl.ds(2 * j + 1, 32, stride=8), :] = pltpu.roll(pos, shift_ref[0], 1)
     for t in range(SOURCES):
@@ -80,7 +86,7 @@
 
 
 def frame_kernel(
-    x_ref, where_ref, spread_ref, win_ref, wdens_ref, grid_ref, west_ref, east_ref, c32, lanes, acc, cnt, fr, mean, cols
+    x_ref, where_ref, spread_ref, win_ref, wdens_ref, grid_ref, west_ref, east_ref, top_ref, bottom_ref, c32, lanes, acc, cnt, fr, mean, cols
 ):
     for t in range(SOURCES):
         c32[2 * t : 2 * t + 2, :] = where_ref[t, PAIRS - 1].astype(F32)
@@ -185,6 +191,10 @@
             extra = jnp.broadcast_to(log_density[:, i + k : i + k + 1], (TW, C)) * wdens_ref[...]
             cell = (out[k * TW : (k + 1) * TW] + extra).astype(BF)
             grid_ref[i + k] = cell.reshape(NP, NQ, C)
+            if i + k < 2:
+                top_ref[(i + k) * TW : (i + k + 1) * TW, :] = cell
+            if i + k >= TH - 2:
+                bottom_ref[(i + k - TH + 2) * TW : (i + k - TH + 3) * TW, :] = cell
             wide = cell.astype(F32)
             for c, at in enumerate((0, NQ, 5 * NQ - 1, 6 * NQ - 1)):
                 cols[c, i + k : i + k + 1, :] = wide[at : at + 1]
@@ -196,85 +206,70 @@
     return v / (1.0 + jnp.exp(-v))
 
 
-def conv_kernel(
-    lat_ref, grid_ref, north_ref, south_ref, west_ref, east_ref, one_ref, two_ref, out_ref, gp, hp, cs, hs, flat, done, sems
-):
-    lat = lat_ref[0]
-    keep_top = jnp.where(lat > 0, 1.0, 0.0)
-    keep_bottom = jnp.where(lat < 15, 1.0, 0.0)
-    cs[...] = jnp.zeros_like(cs)
-    for c in range(4):
-        ref = west_ref if c < 2 else east_ref
-        cs[c, 2 : 2 + TH, :] = ref[c % 2].astype(F32)
-    for ref, at in ((north_ref, 0), (south_ref, 2 + TH)):
-        corner = ref[2 * TW : 2 * TW + 8].astype(F32)
+def corner_kernel(top_in, bottom_in, west_ref, east_ref, top_ref, bottom_ref, part):
+    for source, ref, at in ((top_in, top_ref, 0), (bottom_in, bottom_ref, TH - 2)):
         for c in range(4):
-            cs[c, at : at + 2, :] = corner[2 * c : 2 * c + 2]
-    for g in range(TH + 4):
-        if g < 2:
-            tile = north_ref[g * TW : (g + 1) * TW].reshape(NP, NQ, C)
-        elif g < TH + 2:
-            tile = grid_ref[g - 2]
-        else:
-            tile = south_ref[(g - TH - 2) * TW : (g - TH - 1) * TW].reshape(NP, NQ, C)
-        gp[g, 1 : NP + 1] = tile
-        first, last = tile[0].astype(F32), tile[NP - 1].astype(F32)
-        cs[4, g : g + 1, :] = first[:1]
-        cs[5, g : g + 1, :] = last[NQ - 1 :]
-        gp[g, 0] = with_row(last, 1, cs[1, g : g + 1, :], 0).astype(BF)
-        gp[g, NP + 1] = with_row(first, NQ - 1, cs[2, g : g + 1, :], NQ - 1).astype(BF)
-
-    side = None
+            column = (west_ref if c < 2 else east_ref)[c % 2].astype(F32)
+            part[2 * c : 2 * c + 2, :] = column[at : at + 2]
+        ref[2 * TW : EDGE, :] = part[...].astype(BF)
+
+
+def nine(weight, window):
+    total = None
     for a in range(3):
         for b in range(3):
-            lhs = jnp.concatenate(
-                [cs[(0, 1, 4)[b], a : a + 32, :], cs[(5, 2, 3)[b], a : a + 32, :]], axis=0
-            ).astype(BF)
-            term = dot(lhs, one_ref[3 * a + b])
-            side = term if side is None else side + term
-    side = silu(side)
-    line = iota((64, C), 0)
-    side = jnp.where((line == 0) | (line == 32), side * keep_top, side)
-    side = jnp.where((line == TH + 1) | (line == TH + 33), side * keep_bottom, side)
-    hs[...] = side
-
-    def rows_of(src, weight, start, count):
-        total = None
-        for a in range(3):
-            for b in range(3):
-                window = src[start + a : start + a + count, b : b + NP].reshape(count * TW, C)
-                term = dot(window, weight[3 * a + b])
-                total = term if total is None else total + term
-        return total
-
+            term = dot(window(a, b), weight[3 * a + b])
+            total = term if total is None else total + term
+    return total
+
+
+def rows_of(src, weight, start, count):
+    return nine(weight, lambda a, b: src[start + a : start + a + count, b : b + NP].reshape(count * TW, C))
+
+
+def padded(dst, at, tiles, first, last, before, after):
+    dst[at, 1 : NP + 1] = tiles
+    dst[at, 0] = with_row(last, 1, before, 0).astype(BF)
+    dst[at, NP + 1] = with_row(first, NQ - 1, after, NQ - 1).astype(BF)
+
+
+def spread_out(flat, at, tiles):
+    for p in range(NP):
+        for h in range(2):
+            flat[h, pl.ds(at * TW + p, NQ, stride=NP), :] = tiles[p, :, 128 * h : 128 * (h + 1)]
+
+
+def inner_one_kernel(grid_ref, one_ref, hp_ref, hcols_ref, gp):
+    for g in range(TH):
+        tile = grid_ref[g]
+        first, last = tile[0].astype(F32), tile[NP - 1].astype(F32)
+        padded(gp, g, tile, first, last, first[:1], last[NQ - 1 :])
     start = 0
-    for count in (4, 4, 4, 4, 4, 4, 2):
+    for count in (4, 4, 4, 4, 4, 2):
         value = silu(rows_of(gp, one_ref, start, count))
         for k in range(count):
-            g = start + k
-            row = value[k * TW : (k + 1) * TW]
-            if g == 0:
-                row = row * keep_top
-            if g == TH + 1:
-                row = row * keep_bottom
-            row = row.reshape(NP, NQ, C)
-            hp[g, 1 : NP + 1] = row.astype(BF)
-            hp[g, 0] = with_row(row[NP - 1], 1, hs[g : g + 1, :], 0).astype(BF)
-            hp[g, NP + 1] = with_row(row[0], NQ - 1, hs[32 + g : 33 + g, :], NQ - 1).astype(BF)
+            g = start + k + 2
+            row = value[k * TW : (k + 1) * TW].reshape(NP, NQ, C)
+            padded(hp_ref, g, row.astype(BF), row[0], row[NP - 1], row[0, :1], row[NP - 1, NQ - 1 :])
+            for c, (p, q) in enumerate(((1, 0), (2, 0), (3, NQ - 1), (4, NQ - 1))):
+                hcols_ref[c, g : g + 1, :] = row[p, q : q + 1]
         start += count
 
+
+def inner_two_kernel(hp_ref, grid_ref, two_ref, out_ref, strips_ref, flat, done, sems):
+    copies = []
     step = 4
-    copies = []
-    for i in range(0, TH, step):
-        value = rows_of(hp, two_ref, i, step).reshape(step, NP, NQ, C)
+    for i in range(2, TH - 2, step):
+        value = rows_of(hp_ref, two_ref, i, step).reshape(step, NP, NQ, C)
         value = value + grid_ref[i : i + step].astype(F32)
         for k in range(step):
-            for p in range(NP):
-                for h in range(2):
-                    flat[h, pl.ds((i + k) * TW + p, NQ, stride=NP), :] = value[k, p, :, 128 * h : 128 * (h + 1)]
+            spread_out(flat, i + k, value[k])
         for h in range(2):
-            block = flat[h, i * TW : (i + step) * TW, :].astype(BF)
-            done[i : i + step, :, 128 * h : 128 * (h + 1)] = block.reshape(step, TW, 128)
+            lanes = slice(128 * h, 128 * (h + 1))
+            block = flat[h, i * TW : (i + step) * TW, :].astype(BF).reshape(step, TW, 128)
+            done[i : i + step, :, lanes] = block
+            strips_ref[0, i - 2 : i - 2 + step, :, lanes] = block[:, :8]
+            strips_ref[1, i - 2 : i - 2 + step, :, lanes] = block[:, TW - 8 :]
         copy = pltpu.make_async_copy(done.at[i : i + step], out_ref.at[i : i + step], sems.at[i // step])
         copy.start()
         copies.append(copy)
@@ -282,15 +277,147 @@
         copy.wait()
 
 
+def ring_kernel(
+    lat_ref,
+    grid_ref,
+    north_ref,
+    south_ref,
+    west_ref,
+    east_ref,
+    own_west_ref,
+    own_east_ref,
+    hp_ref,
+    hcols_ref,
+    strips_ref,
+    one_ref,
+    two_ref,
+    partial_ref,
+    out_ref,
+    cs,
+    gp,
+    hc,
+    hr,
+    flat,
+    oc,
+    lines,
+    strips,
+    sems,
+):
+    lat = lat_ref[0]
+    keep_top = jnp.where(lat > 0, 1.0, 0.0)
+    keep_bottom = jnp.where(lat < 15, 1.0, 0.0)
+    cs[:, 24:, :] = jnp.zeros((8, 16, C), F32)
+    for n, ref in enumerate((west_ref, own_west_ref, own_east_ref, east_ref)):
+        for c in range(2):
+            cs[2 * n + c, 2 : 2 + TH, :] = ref[c].astype(F32)
+    for ref, at in ((north_ref, 0), (south_ref, 2 + TH)):
+        corner = ref[2 * TW : EDGE, :].astype(F32)
+        for n, c in enumerate((0, 1, 6, 7)):
+            cs[c, at : at + 2, :] = corner[2 * n : 2 * n + 2]
+        for k in range(2):
+            line = ref[k * TW : (k + 1) * TW, :].astype(F32)
+            for c, place in ((2, 0), (3, NQ), (4, 5 * NQ - 1), (5, 6 * NQ - 1)):
+                cs[c, at + k : at + k + 1, :] = line[place : place + 1]
+            tile = ref[k * TW : (k + 1) * TW, :].reshape(NP, NQ, C)
+            row = at + k
+            slot = row if at == 0 else row - 20
+            padded(gp, slot, tile, line[:NQ], line[TW - NQ :], cs[1, row : row + 1, :], cs[6, row : row + 1, :])
+    for g, slot in ((0, 2), (1, 3), (TH - 2, 4), (TH - 1, 5)):
+        tile = grid_ref[g]
+        row = g + 2
+        padded(
+            gp,
+            slot,
+            tile,
+            tile[0].astype(F32),
+            tile[NP - 1].astype(F32),
+            cs[1, row : row + 1, :],
+            cs[6, row : row + 1, :],
+        )
+
+    def ring(rows, columns, a, b):
+        parts = [rows[at + a : at + a + 2, b : b + NP].reshape(2 * TW, C) for at in (0, 4)]
+        parts += [columns[c + b, a : a + 32, :].astype(BF) for c in (0, 1, 4, 5)]
+        return jnp.concatenate(parts, axis=0)
+
+    value = silu(nine(one_ref, functools.partial(ring, gp, cs)))
+    line = iota((32, C), 0)
+    for n, c in enumerate((0, 1, 6, 7)):
+        column = value[4 * TW + 32 * n : 4 * TW + 32 * (n + 1)]
+        column = jnp.where(line == 0, column * keep_top, column)
+        hc[c, 0:32, :] = jnp.where(line == TH + 1, column * keep_bottom, column)
+    for c in range(4):
+        hc[2 + c, 0:32, :] = hcols_ref[c, 0:32, :]
+    for c in range(8):
+        hc[c, 32:40, :] = jnp.zeros((8, C), F32)
+    for n, g in enumerate((0, 1, TH, TH + 1)):
+        row = value[n * TW : (n + 1) * TW]
+        if g == 0:
+            row = row * keep_top
+        if g == TH + 1:
+            row = row * keep_bottom
+        row = row.reshape(NP, NQ, C)
+        for c, (p, q) in enumerate(((1, 0), (2, 0), (3, NQ - 1), (4, NQ - 1))):
+            hc[2 + c, g : g + 1, :] = row[p, q : q + 1]
+        slot = g if g < 4 else g - 18
+        padded(
+            hr, slot, row.astype(BF), row[0], row[NP - 1], hc[0, g : g + 1, :], hc[7, g : g + 1, :]
+        )
+    place = iota((NQ, C), 0)
+    for g, slot in ((2, 2), (3, 3), (TH - 2, 4), (TH - 1, 5)):
+        tile = hp_ref[g, 1 : NP + 1]
+        first = jnp.where(place == 0, hc[1, g : g + 1, :], tile[0].astype(F32))
+        last = jnp.where(place == NQ - 1, hc[6, g : g + 1, :], tile[NP - 1].astype(F32))
+        padded(hr, slot, tile, first, last, hc[0, g : g + 1, :], hc[7, g : g + 1, :])
+        hr[slot, 1] = first.astype(BF)
+        hr[slot, NP] = last.astype(BF)
+
+    value = nine(two_ref, functools.partial(ring, hr, hc))
+    for n, i in enumerate((0, 1, TH - 2, TH - 1)):
+        row = value[n * TW : (n + 1) * TW].reshape(NP, NQ, C) + grid_ref[i].astype(F32)
+        spread_out(flat, n, row)
+    copies = []
+    for h in range(2):
+        lines[:, :, 128 * h : 128 * (h + 1)] = flat[h].astype(BF).reshape(4, TW, 128)
+    for n, i in enumerate((0, TH - 2)):
+        copies.append(pltpu.make_async_copy(lines.at[2 * n : 2 * n + 2], out_ref.at[i : i + 2], sems.at[n]))
+        copies[-1].start()
+    for c in range(4):
+        column = value[4 * TW + 32 * c : 4 * TW + 32 * c + TH]
+        oc[c] = column + cs[2 + c, 2 : 2 + TH, :]
+    place = iota((8, C), 0)
+    for i in range(2, TH - 2):
+        left, right = strips_ref[0, i - 2].astype(F32), strips_ref[1, i - 2].astype(F32)
+        left = jnp.where(place == 0, oc[0, i : i + 1, :], jnp.where(place == 1, oc[1, i : i + 1, :], left))
+        right = jnp.where(place == 6, oc[2, i : i + 1, :], jnp.where(place == 7, oc[3, i : i + 1, :], right))
+        strips[0, i - 2] = left.astype(BF)
+        strips[1, i - 2] = right.astype(BF)
+    for n, at in enumerate((0, TW - 8)):
+        copies.append(
+            pltpu.make_async_copy(strips.at[n], out_ref.at[2 : TH - 2, at : at + 8], sems.at[2 + n])
+        )
+        copies[-1].start()
+    for copy in copies:
+        copy.wait()
+
+
 def vmem(count):
     return [pl.BlockSpec(memory_space=pltpu.VMEM)] * count
 
 
+def far(count):
+    return [pl.BlockSpec(memory_space=pl.ANY)] * count
+
+
 def smem():
     return pl.BlockSpec(memory_space=pltpu.SMEM)
 
 
 LIMIT = 40 * 1024 * 1024
+
+
+def in_hbm(value):
+    return pltpu.with_memory_space_constraint(value, pltpu.HBM)
 
 
 def near(value):
@@ -303,16 +430,23 @@
     return pl.pallas_call(
         send_kernel,
         out_shape=pltpu.VMEM((SOURCES, PAIRS, 2, F), BF),
-        in_specs=[smem(), pl.BlockSpec(memory_space=pl.ANY), *vmem(2)],
+        in_specs=[smem(), *far(2), *vmem(1)],
         out_specs=vmem(1)[0],
         scratch_shapes=[
+            pltpu.VMEM((96, 128), jnp.int32),
             pltpu.VMEM((2 * SOURCES, 128), F32),
             pltpu.VMEM((SOURCES, 1, 2, F), BF),
-            pltpu.SemaphoreType.DMA((5,)),
+            pltpu.VMEM((128, 128), F32),
+            pltpu.SemaphoreType.DMA((6,)),
         ],
         compiler_params=pltpu.CompilerParams(vmem_limit_bytes=LIMIT),
         name="send",
-    )(shift, features.reshape(SOURCES, PAIRS - 1, 2, F), cell_index.reshape(96, 128), tile_rows.reshape(32, 4))
+    )(
+        shift,
+        in_hbm(features.reshape(SOURCES, PAIRS - 1, 2, F)),
+        in_hbm(cell_index.reshape(96, 128)),
+        near(tile_rows.reshape(1, 128)),
+    )
 
 
 def frame_call(received, spread, w_in, w_dens):
@@ -322,9 +456,11 @@
             pltpu.VMEM((TH, NP, NQ, C), BF),
             pltpu.VMEM((2, TH, C), BF),
             pltpu.VMEM((2, TH, C), BF),
+            pltpu.VMEM((EDGE, C), BF),
+            pltpu.VMEM((EDGE, C), BF),
         ),
         in_specs=[*vmem(2), smem(), *vmem(2)],
-        out_specs=tuple(vmem(3)),
+        out_specs=tuple(vmem(5)),
         scratch_shapes=[
             pltpu.VMEM((SOURCES * 2, 128), F32),
             pltpu.VMEM((4, 104, 128), F32),
@@ -339,33 +475,76 @@
     )(near(received.reshape(SOURCES * ROWS, F)), near(received), spread, near(w_in), near(w_dens.reshape(1, C)))
 
 
-def conv_call(lat, grid, north, south, west, east, w_one, w_two):
+def corner_call(top, bottom, west, east):
     return pl.pallas_call(
-        conv_kernel,
-        out_shape=jax.ShapeDtypeStruct((TH, TW, C), BF),
-        in_specs=[smem(), *vmem(7)],
-        out_specs=pl.BlockSpec(memory_space=pl.ANY),
+        corner_kernel,
+        out_shape=(pltpu.VMEM((EDGE, C), BF),) * 2,
+        in_specs=vmem(4),
+        out_specs=tuple(vmem(2)),
+        scratch_shapes=[pltpu.VMEM((8, C), F32)],
+        input_output_aliases={0: 0, 1: 1},
+        compiler_params=pltpu.CompilerParams(vmem_limit_bytes=LIMIT),
+        name="corner",
+    )(near(top), near(bottom), near(west), near(east))
+
+
+def work(rows):
+    return pl.CostEstimate(flops=2 * rows * TW * 9 * C * C, bytes_accessed=0, transcendentals=0)
+
+
+def inner_one_call(grid, one):
+    return pl.pallas_call(
+        inner_one_kernel,
+        out_shape=(pltpu.VMEM((TH + 2, NP + 2, NQ, C), BF), pltpu.VMEM((4, 40, C), F32)),
+        in_specs=vmem(2),
+        out_specs=tuple(vmem(2)),
+        scratch_shapes=[pltpu.VMEM((TH, NP + 2, NQ, C), BF)],
+        compiler_params=pltpu.CompilerParams(vmem_limit_bytes=LIMIT),
+        cost_estimate=work(TH - 2),
+        name="inner_one",
+    )(near(grid), near(one))
+
+
+def inner_two_call(hp, grid, two):
+    return pl.pallas_call(
+        inner_two_kernel,
+        out_shape=(pltpu.HBM((TH, TW, C), BF), pltpu.VMEM((2, TH - 4, 8, C), BF)),
+        in_specs=vmem(3),
+        out_specs=(*far(1), *vmem(1)),
         scratch_shapes=[
-            pltpu.VMEM((TH + 4, NP + 2, NQ, C), BF),
-            pltpu.VMEM((TH + 2, NP + 2, NQ, C), BF),
-            pltpu.VMEM((6, 40, C), F32),
-            pltpu.VMEM((64, C), F32),
             pltpu.VMEM((2, TH * TW, 128), F32),
             pltpu.VMEM((TH, TW, C), BF),
             pltpu.SemaphoreType.DMA((6,)),
         ],
         compiler_params=pltpu.CompilerParams(vmem_limit_bytes=LIMIT),
-        name="conv",
-    )(
-        lat,
-        near(grid),
-        near(north),
-        near(south),
-        near(west),
-        near(east),
-        near(w_one.reshape(9, C, C)),
-        near(w_two.reshape(9, C, C)),
-    )
+        cost_estimate=work(TH - 4),
+        name="inner_two",
+    )(near(hp), near(grid), near(two))
+
+
+def ring_call(lat, grid, north, south, west, east, own_west, own_east, hp, hcols, strips, one, two, partial):
+    inside = [grid, north, south, west, east, own_west, own_east, hp, hcols, strips, one, two]
+    return pl.pallas_call(
+        ring_kernel,
+        out_shape=jax.ShapeDtypeStruct((TH, TW, C), BF),
+        in_specs=[smem(), *vmem(12), *far(1)],
+        out_specs=far(1)[0],
+        scratch_shapes=[
+            pltpu.VMEM((8, 40, C), F32),
+            pltpu.VMEM((8, NP + 2, NQ, C), BF),
+            pltpu.VMEM((8, 40, C), F32),
+            pltpu.VMEM((8, NP + 2, NQ, C), BF),
+            pltpu.VMEM((2, 4 * TW, 128), F32),
+            pltpu.VMEM((4, TH, C), F32),
+            pltpu.VMEM((4, TW, C), BF),
+            pltpu.VMEM((2, TH - 4, 8, C), BF),
+            pltpu.SemaphoreType.DMA((4,)),
+        ],
+        input_output_aliases={13: 0},
+        compiler_params=pltpu.CompilerParams(vmem_limit_bytes=LIMIT),
+        cost_estimate=work(8),
+        name="ring",
+    )(lat, *(near(value) for value in inside), partial)
 
 
 def step(axis, by, around):
@@ -376,18 +555,19 @@
 def shards(features, cell_index, tile_rows, spread, w_in, w_dens, w_one, w_two):
     sent = send_call(features, cell_index, tile_rows)
     received = lax.all_to_all(sent, ("lat", "lon"), split_axis=0, concat_axis=0, tiled=True)
-    grid, west_cols, east_cols = frame_call(received, spread, w_in, w_dens)
-    from_west = lax.ppermute(east_cols, "lon", step("lon", 1, True))
-    from_east = lax.ppermute(west_cols, "lon", step("lon", -1, True))
-
-    def edge_rows(at):
-        corner = jnp.concatenate([from_west[:, at : at + 2], from_east[:, at : at + 2]], axis=0)
-        return jnp.concatenate([grid[at : at + 2].reshape(2 * TW, C), corner.reshape(8, C)], axis=0)
-
-    from_north = lax.ppermute(edge_rows(TH - 2), "lat", step("lat", 1, False))
-    from_south = lax.ppermute(edge_rows(0), "lat", step("lat", -1, False))
+    grid, own_west, own_east, top, bottom = frame_call(received, spread, w_in, w_dens)
+    one, two = w_one.reshape(9, C, C), w_two.reshape(9, C, C)
+    from_west = lax.ppermute(own_east, "lon", step("lon", 1, True))
+    from_east = lax.ppermute(own_west, "lon", step("lon", -1, True))
+    hp, hcols = inner_one_call(grid, one)
+    top, bottom = corner_call(top, bottom, from_west, from_east)
+    from_north = lax.ppermute(bottom, "lat", step("lat", 1, False))
+    from_south = lax.ppermute(top, "lat", step("lat", -1, False))
+    partial, strips = inner_two_call(hp, grid, two)
     lat = lax.axis_index("lat").reshape(1).astype(jnp.int32)
-    return conv_call(lat, grid, from_north, from_south, from_west, from_east, w_one, w_two)
+    return ring_call(
+        lat, grid, from_north, from_south, from_west, from_east, own_west, own_east, hp, hcols, strips, one, two, partial
+    )
 
 
 def solution(mesh):

time: 95 us -> 87.5 us (0.921)
  local copies, waits for them, and re-layouts: 6.85 us -> 0.68 us
  Pallas kernels: 19.5 us -> 24 us
  waiting for transfers between devices: 2.87 us -> 0.01 us
  other arithmetic: 1.82 us -> 0 us
    unnamed x22 -> x12, local copies, waits for them, and re-layouts: 5.38 us -> 0.68 us
    pallas_call x1 -> x4, Pallas kernels: 6.87 us -> 9.91 us  [the longest x1 3.48 us: ring_call(): pl.pallas_call(ring_kernel, out_shape=jax.ShapeDtypeStruct((TH, TW, C), B...]
    ppermute x4, waiting for transfers between devices: 2.87 us -> 0.01 us  [the longest x1 0.01 us: shards(): from_west = lax.ppermute(own_east, 'lon', step('lon', 1, True))]
    concatenate x3 -> x0, other arithmetic: 1.82 us -> none  [the longest x2 1.8 us: edge_rows(): jnp.concatenate([grid[at:at + 2].reshape(2 * TW, C), corner.reshape(8, C)...]
    pallas_call x1, Pallas kernels: 0.54 us -> 1.93 us  [send_call(): pl.pallas_call(send_kernel, out_shape=pltpu.VMEM((SOURCES, PAIRS, 2, F),...]
  transfers between devices with their start and end apart: 4 -> 4, of which waited for: 2 -> 0; matrix products, arithmetic and copies ran while one was open for 2% -> 0% of each run, Pallas kernels for 0% -> 7%
where the time goes in v3:
time: 87.5 us; the launch traced here: 87.3 us
  blocking collectives  51.5 us (59%)
  Pallas kernels  24 us (27%)
  starting transfers between devices  10.9 us (12%)
    all_to_all x1, blocking collectives, shards(): lax.all_to_all(sent, ('lat', 'lon'), split_axis=0, concat_axis=0, tiled=T...  51.5 us
    pallas_call x1, Pallas kernels, frame_call(): pl.pallas_call(frame_kernel, out_shape=(pltpu.VMEM((TH, NP, NQ, C), BF),...  12.1 us
    ppermute x1, starting transfers between devices, shards(): from_south = lax.ppermute(top, 'lat', step('lat', -1, False))  5.3 us
    pallas_call x1, Pallas kernels, ring_call(): pl.pallas_call(ring_kernel, out_shape=jax.ShapeDtypeStruct((TH, TW, C), B...  3.48 us
    pallas_call x1, Pallas kernels, inner_two_call(): pl.pallas_call(inner_two_kernel, out_shape=(pltpu.HBM((TH, TW, C), BF), p...  3.37 us
    pallas_call x1, Pallas kernels, inner_one_call(): pl.pallas_call(inner_one_kernel, out_shape=(pltpu.VMEM((TH + 2, NP + 2, N...  3.04 us
    ppermute x1, starting transfers between devices, shards(): from_east = lax.ppermute(own_west, 'lon', step('lon', -1, True))  2.94 us
    ppermute x1, starting transfers between devices, shards(): from_north = lax.ppermute(bottom, 'lat', step('lat', 1, False))  2.65 us
  transfers between devices with their start and end apart: 4, of which 0 were waited for; matrix products, arithmetic and copies ran while one was open for 0% of the time, Pallas kernels for 7%

profile of v3, /device:TPU:8, one launch (start us, length us, event | category | flops | bytes accessed | tf_op | source)
XLA Modules:
  0.0 87.3 jit_solution(11347369888608356783)
XLA Ops:
  0.0 0.7 copy-done.5
  0.7 1.9 %send.1 = bf16[128,49,2,128]{3,2,1,0:T(2,128)(2,1)S(1)} custom-call(s32[1]{0:T(128)} %bitcast.1.shift_ref, bf16[128,48,2,128]{3,2,1,0:T(2,128)(2,1)} %bitcast.16, s32[96,128]{1,0:T(8,128)} %bitcast.17, s32[1,128]{1,0:T(1,128)S(1)} %bitcast.15), custom_call_target="tpu_custom_call" | custom-call | tf_op jit(solution)/shard_map/send/pallas_call | solution.py:430
  2.6 0.0 copy-start.2
  2.6 0.0 copy-start.3
  2.6 0.0 copy-start.4
  2.6 51.5 %all_to_all.5.where_ref = bf16[128,49,2,128]{3,2,1,0:T(2,128)(2,1)S(1)} all-to-all(bf16[128,49,2,128]{3,2,1,0:T(2,128)(2,1)S(1)} %send.1), channel_id=1, replica_groups=mesh['lat'=16,'lon'=8] {'lat','lon'}, dimensions={0} | all-to-all | bytes 6422528 | tf_op jit(solution)/shard_map/all_to_all | solution.py:557
  54.1 0.0 copy-done.2
  54.1 0.0 copy-done.3
  54.1 0.0 copy-done.4
  54.1 0.0 copy-start
  54.1 12.1 %frame.1 = (bf16[24,6,16,256]{3,2,1,0:T(8,128)(2,1)S(1)}, bf16[2,24,256]{2,1,0:T(8,128)(2,1)S(1)}, bf16[2,24,256]{2,1,0:T(8,128)(2,1)S(1)}, bf16[200,256]{1,0:T(8,128)(2,1)S(1)}, bf16[200,256]{1,0:T(8,128)(2,1)S(1)}) custom-call(bf16[12544,128]{1,0:T(8,128)(2,1)S(1)} %bitcast.9, bf16[128,49,2,128]{3,2,1,0:T(2,128)(2,1)S(1)} %all_to_all.5.where_ref, ...), custom_call_target="tpu_custom_call" | custom-call | tf_op jit(solution)/shard_map/frame/pallas_call | solution.py:453
  66.3 0.0 collective-permute-start
  66.3 2.9 %collective-permute-start.1 = (bf16[2,24,256]{2,1,0:T(8,128)(2,1)S(1)}, bf16[2,24,256]{2,1,0:T(8,128)(2,1)S(1)}, u32[]{:S(2)}, u32[]{:S(2)}) collective-permute-start(bf16[2,24,256]{2,1,0:T(8,128)(2,1)S(1)} %get-tuple-element.20.own_west_ref), channel_id=1, source_target_pairs={{0,7},{1,0},{2,1},{3,2},{4,3},{5,4},{6,5},{7,6},{8,15},{9,8},{10,9... | collective-permute-start | bytes 73736 | tf_op jit(solution)/shard_map/ppermute | solution.py:561
  69.2 0.0 copy-done
  69.2 3.0 %inner_one.1 = (bf16[26,8,16,256]{3,2,1,0:T(8,128)(2,1)S(1)}, f32[4,40,256]{2,1,0:T(8,128)S(1)}) custom-call(bf16[24,6,16,256]{3,2,1,0:T(8,128)(2,1)S(1)} %get-tuple-element.16.grid_ref, bf16[9,256,256]{2,1,0:T(8,128)(2,1)S(1)} %bitcast.10), custom_call_target="tpu_custom_call" | custom-call | flops 2491416576 | tf_op jit(solution)/shard_map/inner_one/pallas_call | solution.py:496
  72.3 0.0 collective-permute-done.west_ref
  72.3 0.0 collective-permute-done.1.east_ref
  72.3 2.7 %collective-permute-start.2 = (bf16[200,256]{1,0:T(8,128)(2,1)S(1)}, bf16[200,256]{1,0:T(8,128)(2,1)S(1)}, u32[]{:S(2)}, u32[]{:S(2)}) collective-permute-start(bf16[200,256]{1,0:T(8,128)(2,1)S(1)} %get-tuple-element.21), channel_id=1, source_target_pairs={{0,8},{8,16},{16,24},{24,32},{32,40},{40,48},{48,56},{56,64},{64,7... | collective-permute-start | bytes 307208 | tf_op jit(solution)/shard_map/ppermute | solution.py:564
  75.0 5.3 %collective-permute-start.3 = (bf16[200,256]{1,0:T(8,128)(2,1)S(1)}, bf16[200,256]{1,0:T(8,128)(2,1)S(1)}, u32[]{:S(2)}, u32[]{:S(2)}) collective-permute-start(bf16[200,256]{1,0:T(8,128)(2,1)S(1)} %get-tuple-element.22), channel_id=1, source_target_pairs={{8,0},{16,8},{24,16},{32,24},{40,32},{48,40},{56,48},{64,56},{72,6... | collective-permute-start | bytes 307208 | tf_op jit(solution)/shard_map/ppermute | solution.py:565
  80.3 0.0 copy-done.1
  80.3 3.4 %inner_two.1 = (bf16[24,96,256]{2,1,0:T(8,128)(2,1)}, bf16[2,20,8,256]{3,2,1,0:T(8,128)(2,1)S(1)}) custom-call(bf16[26,8,16,256]{3,2,1,0:T(8,128)(2,1)S(1)} %get-tuple-element.23.hp_ref, bf16[24,6,16,256]{3,2,1,0:T(8,128)(2,1)S(1)} %get-tuple-element.16.grid_ref, bf16[9,256,256]{2,1,0:T(8,128)(2,1)S(1)} %bitcast.12), custom_call_target="tpu_custom_call" | custom-call | flops 2264924160 | tf_op jit(solution)/shard_map/inner_two/pallas_call | solution.py:509
  83.7 0.0 collective-permute-done.2.north_ref
  83.7 0.0 collective-permute-done.3.south_ref
  83.7 3.5 %ring.1 = bf16[24,96,256]{2,1,0:T(8,128)(2,1)} custom-call(s32[1]{0:T(128)} %bitcast.lat_ref, bf16[24,6,16,256]{3,2,1,0:T(8,128)(2,1)S(1)} %get-tuple-element.16.grid_ref, bf16[200,256]{1,0:T(8,128)(2,1)S(1)} %collective-permute-done.2.north_ref, bf16[200,256]{1,0:T(8,128)(2,1)S(1)} %collective-permute-done.3.south_ref, ...), custom_call_target="tpu_custom_call", output_to_operand_aliasing={{}: (13, {})} | custom-call | flops 905969664 | tf_op jit(solution)/shard_map/ring/pallas_call | solution.py:527
  (3 shorter events, 0.0 us)
Async XLA Ops:
  0.0 0.7 copy-start.5
  2.6 51.5 %copy-start.2 = (bf16[128,256]{1,0:T(8,128)(2,1)S(1)}, bf16[128,256]{1,0:T(8,128)(2,1)}, u32[]{:S(2)}) copy-start(bf16[128,256]{1,0:T(8,128)(2,1)} %win_ref.1) | copy-start | bytes 196612
  2.6 51.5 %copy-start.3 = (f32[3,3]{1,0:T(4,128)S(1)}, f32[3,3]{1,0:T(4,128)}, u32[]{:S(2)}) copy-start(f32[3,3]{1,0:T(4,128)} %spread_ref.1) | copy-start | bytes 112
  2.6 51.5 %copy-start.4 = (f32[256]{0:T(256)S(1)}, f32[256]{0:T(256)}, u32[]{:S(2)}) copy-start(f32[256]{0:T(256)} %param.13) | copy-start | bytes 3076
  54.1 15.1 %copy-start = (bf16[3,3,256,256]{3,2,1,0:T(8,128)(2,1)S(1)}, bf16[3,3,256,256]{3,2,1,0:T(8,128)(2,1)}, u32[]{:S(2)}) copy-start(bf16[3,3,256,256]{3,2,1,0:T(8,128)(2,1)} %param.14) | copy-start | bytes 3538948
  66.3 6.0 %collective-permute-start = (bf16[2,24,256]{2,1,0:T(8,128)(2,1)S(1)}, bf16[2,24,256]{2,1,0:T(8,128)(2,1)S(1)}, u32[]{:S(2)}, u32[]{:S(2)}) collective-permute-start(bf16[2,24,256]{2,1,0:T(8,128)(2,1)S(1)} %get-tuple-element.19.own_east_ref), channel_id=1, source_target_pairs={{0,1},{1,2},{2,3},{3,4},{4,5},{5,6},{6,7},{7,0},{8,9},{9,10},{10,1... | collective-permute-start | bytes 73736 | tf_op jit(solution)/shard_map/ppermute | solution.py:560
  66.3 6.0 %collective-permute-start.1 = (bf16[2,24,256]{2,1,0:T(8,128)(2,1)S(1)}, bf16[2,24,256]{2,1,0:T(8,128)(2,1)S(1)}, u32[]{:S(2)}, u32[]{:S(2)}) collective-permute-start(bf16[2,24,256]{2,1,0:T(8,128)(2,1)S(1)} %get-tuple-element.20.own_west_ref), channel_id=1, source_target_pairs={{0,7},{1,0},{2,1},{3,2},{4,3},{5,4},{6,5},{7,6},{8,15},{9,8},{10,9... | collective-permute-start | bytes 73736 | tf_op jit(solution)/shard_map/ppermute | solution.py:561
  69.2 11.1 %copy-start.1 = (bf16[3,3,256,256]{3,2,1,0:T(8,128)(2,1)S(1)}, bf16[3,3,256,256]{3,2,1,0:T(8,128)(2,1)}, u32[]{:S(2)}) copy-start(bf16[3,3,256,256]{3,2,1,0:T(8,128)(2,1)} %param.15) | copy-start | bytes 3538948
  72.3 11.4 %collective-permute-start.2 = (bf16[200,256]{1,0:T(8,128)(2,1)S(1)}, bf16[200,256]{1,0:T(8,128)(2,1)S(1)}, u32[]{:S(2)}, u32[]{:S(2)}) collective-permute-start(bf16[200,256]{1,0:T(8,128)(2,1)S(1)} %get-tuple-element.21), channel_id=1, source_target_pairs={{0,8},{8,16},{16,24},{24,32},{32,40},{40,48},{48,56},{56,64},{64,7... | collective-permute-start | bytes 307208 | tf_op jit(solution)/shard_map/ppermute | solution.py:564
  75.0 8.7 %collective-permute-start.3 = (bf16[200,256]{1,0:T(8,128)(2,1)S(1)}, bf16[200,256]{1,0:T(8,128)(2,1)S(1)}, u32[]{:S(2)}, u32[]{:S(2)}) collective-permute-start(bf16[200,256]{1,0:T(8,128)(2,1)S(1)} %get-tuple-element.22), channel_id=1, source_target_pairs={{8,0},{16,8},{24,16},{32,24},{40,32},{48,40},{56,48},{64,56},{72,6... | collective-permute-start | bytes 307208 | tf_op jit(solution)/shard_map/ppermute | solution.py:565

commit v4 on v3

--- a/solution.py
+++ b/solution.py
@@ -42,9 +42,11 @@
     return jnp.where(iota(tile.shape, 0) == at, row, rolled)
 
 
-def send_kernel(shift_ref, features_ref, index_ref, used_ref, out_ref, cells, flat, where, used, sems):
+def send_kernel(shift_ref, features_ref, index_ref, used_ref, out_ref, cells, counts, flat, where, used, sems):
     fetch = pltpu.make_async_copy(index_ref, cells, sems.at[5])
     fetch.start()
+    fetch_used = pltpu.make_async_copy(used_ref, counts, sems.at[6])
+    fetch_used.start()
     cut = SOURCES // 4
     copies = [
         pltpu.make_async_copy(
@@ -56,7 +58,8 @@
     ]
     for copy in copies:
         copy.start()
-    count = jnp.broadcast_to(used_ref[...].astype(F32), (128, 128))
+    fetch_used.wait()
+    count = jnp.broadcast_to(counts[...].astype(F32), (128, 128))
     used[...] = jnp.transpose(count)
     fetch.wait()
     lines = [cells[pl.ds(v, 32, stride=3), :].astype(F32) for v in range(3)]
@@ -86,7 +89,26 @@
 
 
 def frame_kernel(
-    x_ref, where_ref, spread_ref, win_ref, wdens_ref, grid_ref, west_ref, east_ref, top_ref, bottom_ref, c32, lanes, acc, cnt, fr, mean, cols
+    odd_ref,
+    x_ref,
+    where_ref,
+    spread_ref,
+    win_ref,
+    wdens_ref,
+    grid_ref,
+    west_ref,
+    east_ref,
+    cols_a_ref,
+    cols_b_ref,
+    rows_a_ref,
+    rows_b_ref,
+    c32,
+    lanes,
+    acc,
+    cnt,
+    pads,
+    mean,
+    cols,
 ):
     for t in range(SOURCES):
         c32[2 * t : 2 * t + 2, :] = where_ref[t, PAIRS - 1].astype(F32)
@@ -140,8 +162,8 @@
             right.append(jnp.concatenate([x - up, up], axis=1))
         part = dot(left, jnp.concatenate(right, axis=0))
         some = lax.dot_general(
+            jnp.concatenate([hot(r16, 0), hot(r16, 1)], axis=0),
             jnp.concatenate(place, axis=0),
-            jnp.concatenate([hot(r16, 0), hot(r16, 1)], axis=0),
             (((1,), (1,)), ((), ())),
             preferred_element_type=F32,
         )
@@ -152,17 +174,18 @@
             acc[...] += part
             cnt[...] += some
 
+    def tile(r, p):
+        lanes_of = slice((r // HALF) * 128, (r // HALF) * 128 + 128)
+        base = (r % HALF) * TW + NQ * (p - 1)
+        return pads[r, p // NP] if p in (0, NP + 1) else acc[base : base + NQ, lanes_of]
+
     for r in range(PH):
-        base, side = (r % HALF) * TW, (r // HALF) * 128
-        lanes_of = slice(side, side + 128)
-        tile = acc[base : base + TW, lanes_of].reshape(NP, NQ, 128)
-        fr[r, 1 : NP + 1] = tile
-        first = acc[MAIN + r % HALF : MAIN + r % HALF + 1, lanes_of]
-        last = acc[MAIN + HALF + r % HALF : MAIN + HALF + r % HALF + 1, lanes_of]
-        fr[r, 0] = with_row(tile[NP - 1], 1, first, 0)
-        fr[r, NP + 1] = with_row(tile[0], NQ - 1, last, NQ - 1)
-
-    number = cnt[...]
+        lanes_of = slice((r // HALF) * 128, (r // HALF) * 128 + 128)
+        at = MAIN + r % HALF
+        pads[r, 0] = with_row(tile(r, NP), 1, acc[at : at + 1, lanes_of], 0)
+        pads[r, 1] = with_row(tile(r, 1), NQ - 1, acc[at + HALF : at + HALF + 1, lanes_of], NQ - 1)
+
+    number = jnp.transpose(jnp.concatenate([cnt[...], jnp.zeros((96, 128), F32)], axis=0))
     number = [
         with_row(number[TW - NQ : TW], 1, number[TW : TW + 1], 0),
         *(number[NQ * p : NQ * (p + 1)] for p in range(NP)),
@@ -176,42 +199,76 @@
     scale = 1.0 / (1.0 + density)
     log_density = jnp.log(1.0 + density)
 
-    for i in range(TH):
-        data = None
-        for a in range(3):
-            for b in range(3):
-                term = spread_ref[a, b] * fr[i + a, b : b + NP]
-                data = term if data is None else data + term
-        data = data.reshape(TW, F) * jnp.broadcast_to(scale[:, i : i + 1], (TW, F))
-        mean[i * TW : (i + 1) * TW, :] = data.astype(BF)
     step = 4
-    for i in range(0, TH, step):
-        out = dot(mean[i * TW : (i + step) * TW, :], win_ref[...])
+    weights = [[spread_ref[a, b] for b in range(3)] for a in range(3)]
+
+    def average(block):
+        for i in range(block * step, (block + 1) * step):
+            wide = jnp.broadcast_to(scale[:, i : i + 1], (TW, F))
+            for p in range(NP):
+                data = None
+                for a in range(3):
+                    for b in range(3):
+                        term = weights[a][b] * tile(i + a, p + b)
+                        data = term if data is None else data + term
+                at = i * TW + p * NQ
+                mean[at : at + NQ, :] = (data * wide[p * NQ : (p + 1) * NQ]).astype(BF)
+
+    def project(block):
+        return dot(mean[block * step * TW : (block + 1) * step * TW, :], win_ref[...])
+
+    def finish(block, out):
         for k in range(step):
-            extra = jnp.broadcast_to(log_density[:, i + k : i + k + 1], (TW, C)) * wdens_ref[...]
+            i = block * step + k
+            extra = jnp.broadcast_to(log_density[:, i : i + 1], (TW, C)) * wdens_ref[...]
             cell = (out[k * TW : (k + 1) * TW] + extra).astype(BF)
-            grid_ref[i + k] = cell.reshape(NP, NQ, C)
-            if i + k < 2:
-                top_ref[(i + k) * TW : (i + k + 1) * TW, :] = cell
-            if i + k >= TH - 2:
-                bottom_ref[(i + k - TH + 2) * TW : (i + k - TH + 3) * TW, :] = cell
+            grid_ref[i] = cell.reshape(NP, NQ, C)
             wide = cell.astype(F32)
             for c, at in enumerate((0, NQ, 5 * NQ - 1, 6 * NQ - 1)):
-                cols[c, i + k : i + k + 1, :] = wide[at : at + 1]
+                cols[c, i : i + 1, :] = wide[at : at + 1]
+
+    blocks = TH // step
+    average(0)
+    for n in range(blocks):
+        out = project(n)
+        if n + 1 < blocks:
+            average(n + 1)
+        finish(n, out)
     west_ref[...] = cols[0:2].astype(BF)
     east_ref[...] = cols[2:4].astype(BF)
 
+    def give(odd, a_ref, b_ref, after, before):
+        @pl.when(odd == 0)
+        def _():
+            a_ref[...] = after
+            b_ref[...] = before
+
+        @pl.when(odd != 0)
+        def _():
+            a_ref[...] = before
+            b_ref[...] = after
+
+    give(odd_ref[1], cols_a_ref, cols_b_ref, cols[2:4].astype(BF), cols[0:2].astype(BF))
+    rows = [grid_ref[at : at + 2].reshape(2 * TW, C) for at in (TH - 2, 0)]
+    give(odd_ref[0], rows_a_ref.at[: 2 * TW], rows_b_ref.at[: 2 * TW], *rows)
+
 
 def silu(v):
     return v / (1.0 + jnp.exp(-v))
 
 
-def corner_kernel(top_in, bottom_in, west_ref, east_ref, top_ref, bottom_ref, part):
-    for source, ref, at in ((top_in, top_ref, 0), (bottom_in, bottom_ref, TH - 2)):
-        for c in range(4):
-            column = (west_ref if c < 2 else east_ref)[c % 2].astype(F32)
-            part[2 * c : 2 * c + 2, :] = column[at : at + 2]
-        ref[2 * TW : EDGE, :] = part[...].astype(BF)
+def corner_kernel(odd_ref, a_in, b_in, cols_a_ref, cols_b_ref, a_ref, b_ref, part):
+    def write(lon_odd, lat_odd):
+        west, east = (cols_a_ref, cols_b_ref) if lon_odd else (cols_b_ref, cols_a_ref)
+        for ref, at in ((a_ref, 0 if lat_odd else TH - 2), (b_ref, TH - 2 if lat_odd else 0)):
+            for c in range(4):
+                column = (west if c < 2 else east)[c % 2].astype(F32)
+                part[2 * c : 2 * c + 2, :] = column[at : at + 2]
+            ref[2 * TW : EDGE, :] = part[...].astype(BF)
+
+    for lat_odd in (0, 1):
+        for lon_odd in (0, 1):
+            pl.when((odd_ref[0] == lat_odd) & (odd_ref[1] == lon_odd))(functools.partial(write, lon_odd, lat_odd))
 
 
 def nine(weight, window):
@@ -256,43 +313,39 @@
         start += count
 
 
-def inner_two_kernel(hp_ref, grid_ref, two_ref, out_ref, strips_ref, flat, done, sems):
-    copies = []
+def inner_two_kernel(hp_ref, grid_ref, two_ref, body_ref, flat):
     step = 4
     for i in range(2, TH - 2, step):
         value = rows_of(hp_ref, two_ref, i, step).reshape(step, NP, NQ, C)
         value = value + grid_ref[i : i + step].astype(F32)
+        at = i - 2
         for k in range(step):
-            spread_out(flat, i + k, value[k])
+            spread_out(flat, at + k, value[k])
         for h in range(2):
-            lanes = slice(128 * h, 128 * (h + 1))
-            block = flat[h, i * TW : (i + step) * TW, :].astype(BF).reshape(step, TW, 128)
-            done[i : i + step, :, lanes] = block
-            strips_ref[0, i - 2 : i - 2 + step, :, lanes] = block[:, :8]
-            strips_ref[1, i - 2 : i - 2 + step, :, lanes] = block[:, TW - 8 :]
-        copy = pltpu.make_async_copy(done.at[i : i + step], out_ref.at[i : i + step], sems.at[i // step])
-        copy.start()
-        copies.append(copy)
-    for copy in copies:
-        copy.wait()
+            block = flat[h, at * TW : (at + step) * TW, :].astype(BF).reshape(step, TW, 128)
+            body_ref[at : at + step, :, 128 * h : 128 * (h + 1)] = block
 
 
 def ring_kernel(
     lat_ref,
+    odd_ref,
     grid_ref,
+    rows_a_ref,
+    rows_b_ref,
+    cols_a_ref,
+    cols_b_ref,
+    own_west_ref,
+    own_east_ref,
+    hp_ref,
+    hcols_ref,
+    body_ref,
+    one_ref,
+    two_ref,
+    out_ref,
     north_ref,
     south_ref,
     west_ref,
     east_ref,
-    own_west_ref,
-    own_east_ref,
-    hp_ref,
-    hcols_ref,
-    strips_ref,
-    one_ref,
-    two_ref,
-    partial_ref,
-    out_ref,
     cs,
     gp,
     hc,
@@ -303,9 +356,27 @@
     strips,
     sems,
 ):
+    inside = pltpu.make_async_copy(
+        body_ref.at[:, 8 : TW - 8], out_ref.at[2 : TH - 2, 8 : TW - 8], sems.at[4]
+    )
+    inside.start()
     lat = lat_ref[0]
     keep_top = jnp.where(lat > 0, 1.0, 0.0)
     keep_bottom = jnp.where(lat < 15, 1.0, 0.0)
+
+    def take(odd, a_ref, b_ref, after_ref, before_ref):
+        @pl.when(odd == 0)
+        def _():
+            after_ref[...] = a_ref[...]
+            before_ref[...] = b_ref[...]
+
+        @pl.when(odd != 0)
+        def _():
+            after_ref[...] = b_ref[...]
+            before_ref[...] = a_ref[...]
+
+    take(odd_ref[0], rows_a_ref, rows_b_ref, south_ref, north_ref)
+    take(odd_ref[1], cols_a_ref, cols_b_ref, east_ref, west_ref)
     cs[:, 24:, :] = jnp.zeros((8, 16, C), F32)
     for n, ref in enumerate((west_ref, own_west_ref, own_east_ref, east_ref)):
         for c in range(2):
@@ -387,7 +458,7 @@
         oc[c] = column + cs[2 + c, 2 : 2 + TH, :]
     place = iota((8, C), 0)
     for i in range(2, TH - 2):
-        left, right = strips_ref[0, i - 2].astype(F32), strips_ref[1, i - 2].astype(F32)
+        left, right = body_ref[i - 2, :8].astype(F32), body_ref[i - 2, TW - 8 :].astype(F32)
         left = jnp.where(place == 0, oc[0, i : i + 1, :], jnp.where(place == 1, oc[1, i : i + 1, :], left))
         right = jnp.where(place == 6, oc[2, i : i + 1, :], jnp.where(place == 7, oc[3, i : i + 1, :], right))
         strips[0, i - 2] = left.astype(BF)
@@ -397,7 +468,7 @@
             pltpu.make_async_copy(strips.at[n], out_ref.at[2 : TH - 2, at : at + 8], sems.at[2 + n])
         )
         copies[-1].start()
-    for copy in copies:
+    for copy in [*copies, inside]:
         copy.wait()
 
 
@@ -430,14 +501,15 @@
     return pl.pallas_call(
         send_kernel,
         out_shape=pltpu.VMEM((SOURCES, PAIRS, 2, F), BF),
-        in_specs=[smem(), *far(2), *vmem(1)],
+        in_specs=[smem(), *far(3)],
         out_specs=vmem(1)[0],
         scratch_shapes=[
             pltpu.VMEM((96, 128), jnp.int32),
+            pltpu.VMEM((1, 128), jnp.int32),
             pltpu.VMEM((2 * SOURCES, 128), F32),
             pltpu.VMEM((SOURCES, 1, 2, F), BF),
             pltpu.VMEM((128, 128), F32),
-            pltpu.SemaphoreType.DMA((6,)),
+            pltpu.SemaphoreType.DMA((7,)),
         ],
         compiler_params=pltpu.CompilerParams(vmem_limit_bytes=LIMIT),
         name="send",
@@ -445,47 +517,45 @@
         shift,
         in_hbm(features.reshape(SOURCES, PAIRS - 1, 2, F)),
         in_hbm(cell_index.reshape(96, 128)),
-        near(tile_rows.reshape(1, 128)),
+        in_hbm(tile_rows.reshape(1, 128)),
     )
 
 
-def frame_call(received, spread, w_in, w_dens):
+def frame_call(odd, received, spread, w_in, w_dens):
     return pl.pallas_call(
         frame_kernel,
         out_shape=(
             pltpu.VMEM((TH, NP, NQ, C), BF),
-            pltpu.VMEM((2, TH, C), BF),
-            pltpu.VMEM((2, TH, C), BF),
-            pltpu.VMEM((EDGE, C), BF),
-            pltpu.VMEM((EDGE, C), BF),
+            *(pltpu.VMEM((2, TH, C), BF),) * 4,
+            *(pltpu.VMEM((EDGE, C), BF),) * 2,
         ),
-        in_specs=[*vmem(2), smem(), *vmem(2)],
-        out_specs=tuple(vmem(5)),
+        in_specs=[smem(), *vmem(2), smem(), *vmem(2)],
+        out_specs=tuple(vmem(7)),
         scratch_shapes=[
             pltpu.VMEM((SOURCES * 2, 128), F32),
             pltpu.VMEM((4, 104, 128), F32),
             pltpu.VMEM((LHS, C), F32),
-            pltpu.VMEM((128, 32), F32),
-            pltpu.VMEM((PH, NP + 2, NQ, F), F32),
+            pltpu.VMEM((32, 128), F32),
+            pltpu.VMEM((PH, 2, NQ, F), F32),
             pltpu.VMEM((TH * TW, F), BF),
             pltpu.VMEM((4, TH, C), F32),
         ],
         compiler_params=pltpu.CompilerParams(vmem_limit_bytes=LIMIT),
         name="frame",
-    )(near(received.reshape(SOURCES * ROWS, F)), near(received), spread, near(w_in), near(w_dens.reshape(1, C)))
-
-
-def corner_call(top, bottom, west, east):
+    )(odd, near(received.reshape(SOURCES * ROWS, F)), near(received), spread, near(w_in), near(w_dens.reshape(1, C)))
+
+
+def corner_call(odd, rows_a, rows_b, cols_a, cols_b):
     return pl.pallas_call(
         corner_kernel,
         out_shape=(pltpu.VMEM((EDGE, C), BF),) * 2,
-        in_specs=vmem(4),
+        in_specs=[smem(), *vmem(4)],
         out_specs=tuple(vmem(2)),
         scratch_shapes=[pltpu.VMEM((8, C), F32)],
-        input_output_aliases={0: 0, 1: 1},
+        input_output_aliases={1: 0, 2: 1},
         compiler_params=pltpu.CompilerParams(vmem_limit_bytes=LIMIT),
         name="corner",
-    )(near(top), near(bottom), near(west), near(east))
+    )(odd, near(rows_a), near(rows_b), near(cols_a), near(cols_b))
 
 
 def work(rows):
@@ -508,28 +578,25 @@
 def inner_two_call(hp, grid, two):
     return pl.pallas_call(
         inner_two_kernel,
-        out_shape=(pltpu.HBM((TH, TW, C), BF), pltpu.VMEM((2, TH - 4, 8, C), BF)),
+        out_shape=pltpu.VMEM((TH - 4, TW, C), BF),
         in_specs=vmem(3),
-        out_specs=(*far(1), *vmem(1)),
-        scratch_shapes=[
-            pltpu.VMEM((2, TH * TW, 128), F32),
-            pltpu.VMEM((TH, TW, C), BF),
-            pltpu.SemaphoreType.DMA((6,)),
-        ],
+        out_specs=vmem(1)[0],
+        scratch_shapes=[pltpu.VMEM((2, (TH - 4) * TW, 128), F32)],
         compiler_params=pltpu.CompilerParams(vmem_limit_bytes=LIMIT),
         cost_estimate=work(TH - 4),
         name="inner_two",
     )(near(hp), near(grid), near(two))
 
 
-def ring_call(lat, grid, north, south, west, east, own_west, own_east, hp, hcols, strips, one, two, partial):
-    inside = [grid, north, south, west, east, own_west, own_east, hp, hcols, strips, one, two]
+def ring_call(lat, odd, *inside):
     return pl.pallas_call(
         ring_kernel,
         out_shape=jax.ShapeDtypeStruct((TH, TW, C), BF),
-        in_specs=[smem(), *vmem(12), *far(1)],
+        in_specs=[smem(), smem(), *vmem(12)],
         out_specs=far(1)[0],
         scratch_shapes=[
+            *(pltpu.VMEM((EDGE, C), BF),) * 2,
+            *(pltpu.VMEM((2, TH, C), BF),) * 2,
             pltpu.VMEM((8, 40, C), F32),
             pltpu.VMEM((8, NP + 2, NQ, C), BF),
             pltpu.VMEM((8, 40, C), F32),
@@ -538,35 +605,36 @@
             pltpu.VMEM((4, TH, C), F32),
             pltpu.VMEM((4, TW, C), BF),
             pltpu.VMEM((2, TH - 4, 8, C), BF),
-            pltpu.SemaphoreType.DMA((4,)),
+            pltpu.SemaphoreType.DMA((5,)),
         ],
-        input_output_aliases={13: 0},
         compiler_params=pltpu.CompilerParams(vmem_limit_bytes=LIMIT),
         cost_estimate=work(8),
         name="ring",
-    )(lat, *(near(value) for value in inside), partial)
-
-
-def step(axis, by, around):
+    )(lat, odd, *(near(value) for value in inside))
+
+
+def swaps(axis, first, around):
     count = lax.axis_size(axis)
-    return [(i, (i + by) % count) for i in range(count) if around or 0 <= i + by < count]
+    pairs = [(i, (i + 1) % count) for i in range(first, count, 2) if around or i + 1 < count]
+    return pairs + [(j, i) for i, j in pairs]
 
 
 def shards(features, cell_index, tile_rows, spread, w_in, w_dens, w_one, w_two):
     sent = send_call(features, cell_index, tile_rows)
     received = lax.all_to_all(sent, ("lat", "lon"), split_axis=0, concat_axis=0, tiled=True)
-    grid, own_west, own_east, top, bottom = frame_call(received, spread, w_in, w_dens)
+    lat = lax.axis_index("lat").astype(jnp.int32)
+    odd = jnp.stack([lat % 2, lax.axis_index("lon").astype(jnp.int32) % 2])
+    grid, own_west, own_east, cols_a, cols_b, rows_a, rows_b = frame_call(odd, received, spread, w_in, w_dens)
     one, two = w_one.reshape(9, C, C), w_two.reshape(9, C, C)
-    from_west = lax.ppermute(own_east, "lon", step("lon", 1, True))
-    from_east = lax.ppermute(own_west, "lon", step("lon", -1, True))
+    cols_b = lax.ppermute(cols_b, "lon", swaps("lon", 1, True))
+    cols_a = lax.ppermute(cols_a, "lon", swaps("lon", 0, True))
     hp, hcols = inner_one_call(grid, one)
-    top, bottom = corner_call(top, bottom, from_west, from_east)
-    from_north = lax.ppermute(bottom, "lat", step("lat", 1, False))
-    from_south = lax.ppermute(top, "lat", step("lat", -1, False))
-    partial, strips = inner_two_call(hp, grid, two)
-    lat = lax.axis_index("lat").reshape(1).astype(jnp.int32)
+    rows_a, rows_b = corner_call(odd, rows_a, rows_b, cols_a, cols_b)
+    rows_b = lax.ppermute(rows_b, "lat", swaps("lat", 1, False))
+    rows_a = lax.ppermute(rows_a, "lat", swaps("lat", 0, False))
+    body = inner_two_call(hp, grid, two)
     return ring_call(
-        lat, grid, from_north, from_south, from_west, from_east, own_west, own_east, hp, hcols, strips, one, two, partial
+        lat.reshape(1), odd, grid, rows_a, rows_b, cols_a, cols_b, own_west, own_east, hp, hcols, body, one, two
     )
 
 

time: 87.5 us -> 86.7 us (level)
  blocking collectives: 51.5 us -> 0 us
  waiting for transfers between devices: 0.01 us -> 44.1 us
  starting transfers between devices: 10.9 us -> 16.4 us
  local copies, waits for them, and re-layouts: 0.68 us -> 1.68 us
    all_to_all x1 -> x0, blocking collectives: 51.5 us -> none  [shards(): lax.all_to_all(sent, ('lat', 'lon'), split_axis=0, concat_axis=0, tiled=T...]
    all_to_all x0 -> x1, waiting for transfers between devices: none -> 41.1 us  [shards(): lax.all_to_all(sent, ('lat', 'lon'), split_axis=0, concat_axis=0, tiled=T...]
    all_to_all x0 -> x1, starting transfers between devices: none -> 10.4 us  [shards(): lax.all_to_all(sent, ('lat', 'lon'), split_axis=0, concat_axis=0, tiled=T...]
    ppermute x4, starting transfers between devices: 10.9 us -> 5.93 us  [the longest x1 3.29 us: shards(): rows_b = lax.ppermute(rows_b, 'lat', swaps('lat', 1, False))]
    ppermute x4, waiting for transfers between devices: 0.01 us -> 2.94 us  [the longest x1 2.8 us: shards(): rows_b = lax.ppermute(rows_b, 'lat', swaps('lat', 1, False))]
    unnamed x12, local copies, waits for them, and re-layouts: 0.68 us -> 1.68 us
  transfers between devices with their start and end apart: 4 -> 5, of which waited for: 0 -> 3; matrix products, arithmetic and copies ran while one was open for 0% -> 0% of each run, Pallas kernels for 7% -> 6%
where the time goes in v4:
time: 86.7 us; the launch traced here: 86.5 us
  waiting for transfers between devices  44.1 us (51%)
  Pallas kernels  24 us (28%)
  starting transfers between devices  16.4 us (19%)
  local copies, waits for them, and re-layouts  1.68 us (2%)
    all_to_all x1, waiting for transfers between devices, shards(): lax.all_to_all(sent, ('lat', 'lon'), split_axis=0, concat_axis=0, tiled=T...  41.1 us
    pallas_call x1, Pallas kernels, frame_call(): pl.pallas_call(frame_kernel, out_shape=(pltpu.VMEM((TH, NP, NQ, C), BF),...  12 us
    all_to_all x1, starting transfers between devices, shards(): lax.all_to_all(sent, ('lat', 'lon'), split_axis=0, concat_axis=0, tiled=T...  10.4 us
    pallas_call x1, Pallas kernels, ring_call(): pl.pallas_call(ring_kernel, out_shape=jax.ShapeDtypeStruct((TH, TW, C), B...  4.05 us
    ppermute x1, starting transfers between devices, shards(): rows_b = lax.ppermute(rows_b, 'lat', swaps('lat', 1, False))  3.29 us
    pallas_call x1, Pallas kernels, inner_one_call(): pl.pallas_call(inner_one_kernel, out_shape=(pltpu.VMEM((TH + 2, NP + 2, N...  2.83 us
    ppermute x1, waiting for transfers between devices, shards(): rows_b = lax.ppermute(rows_b, 'lat', swaps('lat', 1, False))  2.8 us
    pallas_call x1, Pallas kernels, inner_two_call(): pl.pallas_call(inner_two_kernel, out_shape=pltpu.VMEM((TH - 4, TW, C), BF...  2.53 us
  transfers between devices with their start and end apart: 5, of which 3 were waited for; matrix products, arithmetic and copies ran while one was open for 0% of the time, Pallas kernels for 6%

profile of v4, /device:TPU:8, one launch (start us, length us, event | category | flops | bytes accessed | tf_op | source)
XLA Modules:
  0.0 86.5 jit_solution(17714825660399169027)
XLA Ops:
  0.0 1.9 %send.1 = bf16[128,49,2,128]{3,2,1,0:T(2,128)(2,1)S(1)} custom-call(s32[1]{0:T(128)} %bitcast.3.shift_ref, bf16[128,48,2,128]{3,2,1,0:T(2,128)(2,1)} %bitcast.17, s32[96,128]{1,0:T(8,128)} %bitcast.18, s32[1,128]{1,0:T(1,128)} %bitcast.19), custom_call_target="tpu_custom_call" | custom-call | tf_op jit(solution)/shard_map/send/pallas_call | solution.py:501
  2.0 0.0 copy-start
  2.0 1.7 %copy-done = bf16[128,49,2,128]{3,2,1,0:T(2,128)(2,1)} copy-done((bf16[128,49,2,128]{3,2,1,0:T(2,128)(2,1)}, bf16[128,49,2,128]{3,2,1,0:T(2,128)(2,1)S(1)}, u32[]{:S(2)}) %copy-start) | copy-done | bytes 3211288
  3.6 10.4 %all-to-all-start = ((bf16[128,49,2,128]{3,2,1,0:T(2,128)(2,1)}), bf16[128,49,2,128]{3,2,1,0:T(2,128)(2,1)S(1)}, u32[]{:S(2)}, u32[]{:S(2)}) async-start(bf16[128,49,2,128]{3,2,1,0:T(2,128)(2,1)} %copy-done), calls=%async_computation | async-start | bytes 6422528 | tf_op jit(solution)/shard_map/all_to_all | solution.py:624
  14.1 0.1 pad_add_fusion.odd_ref
  14.2 41.1 %all-to-all-done.where_ref = bf16[128,49,2,128]{3,2,1,0:T(2,128)(2,1)S(1)} async-done(((bf16[128,49,2,128]{3,2,1,0:T(2,128)(2,1)}), bf16[128,49,2,128]{3,2,1,0:T(2,128)(2,1)S(1)}, u32[]{:S(2)}, u32[]{:S(2)}) %all-to-all-start) | async-done | bytes 3211296 | tf_op jit(solution)/shard_map/all_to_all | solution.py:624
  55.3 0.0 copy-done.3
  55.3 0.0 copy-done.4
  55.3 0.0 copy-done.5
  55.3 0.0 copy-start.1
  55.3 12.0 %frame.1 = (bf16[24,6,16,256]{3,2,1,0:T(8,128)(2,1)S(1)}, bf16[2,24,256]{2,1,0:T(8,128)(2,1)S(1)}, bf16[2,24,256]{2,1,0:T(8,128)(2,1)S(1)}, bf16[2,24,256]{2,1,0...) custom-call(s32[2]{0:T(128)S(1)} %pad_add_fusion.odd_ref, ...), custom_call_target="tpu_custom_call" | custom-call | tf_op jit(solution)/shard_map/frame/pallas_call | solution.py:525
  67.4 0.1 collective-permute-start
  67.5 1.7 %collective-permute-start.1 = (bf16[2,24,256]{2,1,0:T(8,128)(2,1)S(1)}, bf16[2,24,256]{2,1,0:T(8,128)(2,1)S(1)}, u32[]{:S(2)}, u32[]{:S(2)}) collective-permute-start(bf16[2,24,256]{2,1,0:T(8,128)(2,1)S(1)} %get-tuple-element.20), channel_id=1, source_target_pairs={{1,2},{3,4},{5,6},{7,0},{2,1},{4,3},{6,5},{0,7},{9,10},{11,12},{13... | collective-permute-start | bytes 73736 | tf_op jit(solution)/shard_map/ppermute | solution.py:629
  69.2 0.0 copy-done.1
  69.2 2.8 %inner_one.1 = (bf16[26,8,16,256]{3,2,1,0:T(8,128)(2,1)S(1)}, f32[4,40,256]{2,1,0:T(8,128)S(1)}) custom-call(bf16[24,6,16,256]{3,2,1,0:T(8,128)(2,1)S(1)} %get-tuple-element.16.grid_ref, bf16[9,256,256]{2,1,0:T(8,128)(2,1)S(1)} %bitcast.12), custom_call_target="tpu_custom_call" | custom-call | flops 2491416576 | tf_op jit(solution)/shard_map/inner_one/pallas_call | solution.py:566
  72.1 0.0 collective-permute-done.cols_a_ref
  72.1 0.1 collective-permute-done.1.cols_b_ref
  72.2 0.6 corner.1
  72.8 0.8 collective-permute-start.2
  73.6 3.3 %collective-permute-start.3 = (bf16[200,256]{1,0:T(8,128)(2,1)S(1)}, bf16[200,256]{1,0:T(8,128)(2,1)S(1)}, u32[]{:S(2)}, u32[]{:S(2)}) collective-permute-start(bf16[200,256]{1,0:T(8,128)(2,1)S(1)} %get-tuple-element.22), channel_id=1, source_target_pairs={{8,16},{24,32},{40,48},{56,64},{72,80},{88,96},{104,112},{16,8},{3... | collective-permute-start | bytes 307208 | tf_op jit(solution)/shard_map/ppermute | solution.py:633
  76.9 2.5 %inner_two.1.body_ref = bf16[20,96,256]{2,1,0:T(8,128)(2,1)S(1)} custom-call(bf16[26,8,16,256]{3,2,1,0:T(8,128)(2,1)S(1)} %get-tuple-element.25.hp_ref, bf16[24,6,16,256]{3,2,1,0:T(8,128)(2,1)S(1)} %get-tuple-element.16.grid_ref, bf16[9,256,256]{2,1,0:T(8,128)(2,1)S(1)} %bitcast.14), custom_call_target="tpu_custom_call" | custom-call | flops 2264924160 | tf_op jit(solution)/shard_map/inner_two/pallas_call | solution.py:579
  79.5 0.0 collective-permute-done.2.rows_a_ref
  79.5 2.8 %collective-permute-done.3.rows_b_ref = bf16[200,256]{1,0:T(8,128)(2,1)S(1)} collective-permute-done((bf16[200,256]{1,0:T(8,128)(2,1)S(1)}, bf16[200,256]{1,0:T(8,128)(2,1)S(1)}, u32[]{:S(2)}, u32[]{:S(2)}) %collective-permute-start.3) | collective-permute-done | bytes 102432 | tf_op jit(solution)/shard_map/ppermute | solution.py:633
  82.3 4.0 %ring.1 = bf16[24,96,256]{2,1,0:T(8,128)(2,1)} custom-call(s32[1]{0:T(128)} %bitcast.lat_ref, s32[2]{0:T(128)S(1)} %pad_add_fusion.odd_ref, bf16[24,6,16,256]{3,2,1,0:T(8,128)(2,1)S(1)} %get-tuple-element.16.grid_ref, bf16[200,256]{1,0:T(8,128)(2,1)S(1)} %collective-permute-done.2.rows_a_ref, bf16[200,256]{1,0:T(8,128)(2,1)S(1)} %collective-permute-done.3.rows_b_ref, ...), custom_call_target="tpu_custom_call" | custom-call | flops 905969664 | tf_op jit(solution)/shard_map/ring/pallas_call | solution.py:592
  (5 shorter events, 0.0 us)
Async XLA Ops:
  2.0 1.7 %copy-start = (bf16[128,49,2,128]{3,2,1,0:T(2,128)(2,1)}, bf16[128,49,2,128]{3,2,1,0:T(2,128)(2,1)S(1)}, u32[]{:S(2)}) copy-start(bf16[128,49,2,128]{3,2,1,0:T(2,128)(2,1)S(1)} %send.1) | copy-start | bytes 9633796
  3.6 51.7 %copy-start.3 = (bf16[128,256]{1,0:T(8,128)(2,1)S(1)}, bf16[128,256]{1,0:T(8,128)(2,1)}, u32[]{:S(2)}) copy-start(bf16[128,256]{1,0:T(8,128)(2,1)} %win_ref.1) | copy-start | bytes 196612
  3.6 51.7 %copy-start.4 = (f32[3,3]{1,0:T(4,128)S(1)}, f32[3,3]{1,0:T(4,128)}, u32[]{:S(2)}) copy-start(f32[3,3]{1,0:T(4,128)} %spread_ref.1) | copy-start | bytes 112
  3.6 51.7 %copy-start.5 = (f32[256]{0:T(256)S(1)}, f32[256]{0:T(256)}, u32[]{:S(2)}) copy-start(f32[256]{0:T(256)} %param.13) | copy-start | bytes 3076
  3.6 51.7 %all-to-all-start = ((bf16[128,49,2,128]{3,2,1,0:T(2,128)(2,1)}), bf16[128,49,2,128]{3,2,1,0:T(2,128)(2,1)S(1)}, u32[]{:S(2)}, u32[]{:S(2)}) async-start(bf16[128,49,2,128]{3,2,1,0:T(2,128)(2,1)} %copy-done), calls=%async_computation | async-start | bytes 6422528 | tf_op jit(solution)/shard_map/all_to_all | solution.py:624
  55.3 13.9 %copy-start.1 = (bf16[3,3,256,256]{3,2,1,0:T(8,128)(2,1)S(1)}, bf16[3,3,256,256]{3,2,1,0:T(8,128)(2,1)}, u32[]{:S(2)}) copy-start(bf16[3,3,256,256]{3,2,1,0:T(8,128)(2,1)} %param.14) | copy-start | bytes 3538948
  67.4 4.7 %collective-permute-start = (bf16[2,24,256]{2,1,0:T(8,128)(2,1)S(1)}, bf16[2,24,256]{2,1,0:T(8,128)(2,1)S(1)}, u32[]{:S(2)}, u32[]{:S(2)}) collective-permute-start(bf16[2,24,256]{2,1,0:T(8,128)(2,1)S(1)} %get-tuple-element.19), channel_id=1, source_target_pairs={{0,1},{2,3},{4,5},{6,7},{1,0},{3,2},{5,4},{7,6},{8,9},{10,11},{12,... | collective-permute-start | bytes 73736 | tf_op jit(solution)/shard_map/ppermute | solution.py:630
  67.5 4.7 %collective-permute-start.1 = (bf16[2,24,256]{2,1,0:T(8,128)(2,1)S(1)}, bf16[2,24,256]{2,1,0:T(8,128)(2,1)S(1)}, u32[]{:S(2)}, u32[]{:S(2)}) collective-permute-start(bf16[2,24,256]{2,1,0:T(8,128)(2,1)S(1)} %get-tuple-element.20), channel_id=1, source_target_pairs={{1,2},{3,4},{5,6},{7,0},{2,1},{4,3},{6,5},{0,7},{9,10},{11,12},{13... | collective-permute-start | bytes 73736 | tf_op jit(solution)/shard_map/ppermute | solution.py:629
  69.2 7.7 %copy-start.2 = (bf16[3,3,256,256]{3,2,1,0:T(8,128)(2,1)S(1)}, bf16[3,3,256,256]{3,2,1,0:T(8,128)(2,1)}, u32[]{:S(2)}) copy-start(bf16[3,3,256,256]{3,2,1,0:T(8,128)(2,1)} %param.15) | copy-start | bytes 3538948
  72.8 6.7 %collective-permute-start.2 = (bf16[200,256]{1,0:T(8,128)(2,1)S(1)}, bf16[200,256]{1,0:T(8,128)(2,1)S(1)}, u32[]{:S(2)}, u32[]{:S(2)}) collective-permute-start(bf16[200,256]{1,0:T(8,128)(2,1)S(1)} %get-tuple-element.21), channel_id=1, source_target_pairs={{0,8},{16,24},{32,40},{48,56},{64,72},{80,88},{96,104},{112,120},{... | collective-permute-start | bytes 307208 | tf_op jit(solution)/shard_map/ppermute | solution.py:634
  73.6 8.7 %collective-permute-start.3 = (bf16[200,256]{1,0:T(8,128)(2,1)S(1)}, bf16[200,256]{1,0:T(8,128)(2,1)S(1)}, u32[]{:S(2)}, u32[]{:S(2)}) collective-permute-start(bf16[200,256]{1,0:T(8,128)(2,1)S(1)} %get-tuple-element.22), channel_id=1, source_target_pairs={{8,16},{24,32},{40,48},{56,64},{72,80},{88,96},{104,112},{16,8},{3... | collective-permute-start | bytes 307208 | tf_op jit(solution)/shard_map/ppermute | solution.py:633

commit v5 on v4

--- a/solution.py
+++ b/solution.py
@@ -6,6 +6,7 @@
 from jax.experimental import pallas as pl
 from jax.experimental.pallas import tpu as pltpu
 from jax.sharding import PartitionSpec as P
+
 
 TH = 24
 TW = 96
@@ -37,12 +38,21 @@
     return lax.broadcasted_iota(jnp.int32, shape, dim)
 
 
+def places():
+    return lax.axis_index("lat").astype(jnp.int32), lax.axis_index("lon").astype(jnp.int32)
+
+
+def parities():
+    lat, lon = places()
+    return lax.rem(lat, 2), lax.rem(lon, 2)
+
+
 def with_row(tile, shift, row, at):
     rolled = pltpu.roll(tile, shift, 0)
     return jnp.where(iota(tile.shape, 0) == at, row, rolled)
 
 
-def send_kernel(shift_ref, features_ref, index_ref, used_ref, out_ref, cells, counts, flat, where, used, sems):
+def send_kernel(features_ref, index_ref, used_ref, out_ref, cells, counts, flat, where, used, sems):
     fetch = pltpu.make_async_copy(index_ref, cells, sems.at[5])
     fetch.start()
     fetch_used = pltpu.make_async_copy(used_ref, counts, sems.at[6])
@@ -63,6 +73,8 @@
     used[...] = jnp.transpose(count)
     fetch.wait()
     lines = [cells[pl.ds(v, 32, stride=3), :].astype(F32) for v in range(3)]
+    lat, lon = places()
+    shift = lax.rem((lat * 8 + lon) * ROWS, 128)
     lane = iota((32, 128), 1)
     blocks = [
         lines[0],
@@ -77,8 +89,8 @@
         pos = (s - 1.0 - q * NP) * NQ + q
         pos = jnp.where(s == 0.0, float(TW), jnp.where(s == PW - 1.0, TW + 1.0, pos))
         r = jnp.where(lane.astype(F32) < used[pl.ds(j, 32, stride=4), :], r, 63.0)
-        flat[pl.ds(2 * j, 32, stride=8), :] = pltpu.roll(r, shift_ref[0], 1)
-        flat[pl.ds(2 * j + 1, 32, stride=8), :] = pltpu.roll(pos, shift_ref[0], 1)
+        flat[pl.ds(2 * j, 32, stride=8), :] = pltpu.roll(r, shift, 1)
+        flat[pl.ds(2 * j + 1, 32, stride=8), :] = pltpu.roll(pos, shift, 1)
     for t in range(SOURCES):
         where[t, 0] = flat[2 * t : 2 * t + 2, :].astype(BF)
     last = pltpu.make_async_copy(where, out_ref.at[:, PAIRS - 1 : PAIRS], sems.at[4])
@@ -89,7 +101,6 @@
 
 
 def frame_kernel(
-    odd_ref,
     x_ref,
     where_ref,
     spread_ref,
@@ -160,7 +171,7 @@
             x = x_ref[128 * t : 128 * (t + 1), :]
             up = x * jnp.broadcast_to(upper[:, t : t + 1], (128, 128)).astype(BF)
             right.append(jnp.concatenate([x - up, up], axis=1))
-        part = dot(left, jnp.concatenate(right, axis=0))
+        right = jnp.concatenate(right, axis=0)
         some = lax.dot_general(
             jnp.concatenate([hot(r16, 0), hot(r16, 1)], axis=0),
             jnp.concatenate(place, axis=0),
@@ -168,22 +179,32 @@
             preferred_element_type=F32,
         )
         if g == 0:
-            acc[...] = part
+            acc[...] = dot(left, right)
             cnt[...] = some
+        elif g + 1 < GROUPS:
+            acc[...] += dot(left, right)
+            cnt[...] += some
         else:
-            acc[...] += part
             cnt[...] += some
+
+    def weight(a, b, shape):
+        return jnp.broadcast_to(spread_ref[a : a + 1, b : b + 1], shape)
 
     def tile(r, p):
         lanes_of = slice((r // HALF) * 128, (r // HALF) * 128 + 128)
         base = (r % HALF) * TW + NQ * (p - 1)
         return pads[r, p // NP] if p in (0, NP + 1) else acc[base : base + NQ, lanes_of]
 
-    for r in range(PH):
-        lanes_of = slice((r // HALF) * 128, (r // HALF) * 128 + 128)
-        at = MAIN + r % HALF
-        pads[r, 0] = with_row(tile(r, NP), 1, acc[at : at + 1, lanes_of], 0)
-        pads[r, 1] = with_row(tile(r, 1), NQ - 1, acc[at + HALF : at + HALF + 1, lanes_of], NQ - 1)
+    def complete(start, stop):
+        rows = slice(start * TW, stop * TW)
+        acc[rows, :] += dot(left[rows], right)
+        for r in (*range(start, stop), *range(HALF + start, HALF + stop)):
+            lanes_of = slice((r // HALF) * 128, (r // HALF) * 128 + 128)
+            at = MAIN + r % HALF
+            pads[r, 0] = with_row(tile(r, NP), 1, acc[at : at + 1, lanes_of], 0)
+            pads[r, 1] = with_row(tile(r, 1), NQ - 1, acc[at + HALF : at + HALF + 1, lanes_of], NQ - 1)
+
+    acc[MAIN:, :] += dot(left[MAIN:], right)
 
     number = jnp.transpose(jnp.concatenate([cnt[...], jnp.zeros((96, 128), F32)], axis=0))
     number = [
@@ -193,17 +214,16 @@
     ]
     density = None
     for a in range(3):
-        line = [sum(spread_ref[a, b] * number[p + b] for b in range(3)) for p in range(NP)]
+        line = [sum(weight(a, b, (NQ, 128)) * number[p + b] for b in range(3)) for p in range(NP)]
         line = jnp.concatenate(line, axis=0)[:, a : a + TH]
         density = line if density is None else density + line
     scale = 1.0 / (1.0 + density)
     log_density = jnp.log(1.0 + density)
 
-    step = 4
-    weights = [[spread_ref[a, b] for b in range(3)] for a in range(3)]
-
-    def average(block):
-        for i in range(block * step, (block + 1) * step):
+    weights = [[weight(a, b, (NQ, F)) for b in range(3)] for a in range(3)]
+
+    def average(rows):
+        for i in rows:
             wide = jnp.broadcast_to(scale[:, i : i + 1], (TW, F))
             for p in range(NP):
                 data = None
@@ -214,12 +234,11 @@
                 at = i * TW + p * NQ
                 mean[at : at + NQ, :] = (data * wide[p * NQ : (p + 1) * NQ]).astype(BF)
 
-    def project(block):
-        return dot(mean[block * step * TW : (block + 1) * step * TW, :], win_ref[...])
-
-    def finish(block, out):
-        for k in range(step):
-            i = block * step + k
+    def project(rows):
+        return dot(jnp.concatenate([mean[i * TW : (i + 1) * TW, :] for i in rows], axis=0), win_ref[...])
+
+    def finish(rows, out):
+        for k, i in enumerate(rows):
             extra = jnp.broadcast_to(log_density[:, i : i + 1], (TW, C)) * wdens_ref[...]
             cell = (out[k * TW : (k + 1) * TW] + extra).astype(BF)
             grid_ref[i] = cell.reshape(NP, NQ, C)
@@ -227,15 +246,25 @@
             for c, at in enumerate((0, NQ, 5 * NQ - 1, 6 * NQ - 1)):
                 cols[c, i : i + 1, :] = wide[at : at + 1]
 
-    blocks = TH // step
-    average(0)
-    for n in range(blocks):
-        out = project(n)
-        if n + 1 < blocks:
-            average(n + 1)
-        finish(n, out)
+    plan = (
+        (0, 5, ((0, 1, 2), (13, 14, 15))),
+        (5, 9, ((3, 4, 5, 6), (16, 17, 18, 19))),
+        (9, 13, ((7, 8, 9, 10), (20, 21, 22, 23), (11, 12))),
+    )
+    waiting = None
+    for start, stop, sets in plan:
+        complete(start, stop)
+        for rows in sets:
+            average(rows)
+            out = project(rows)
+            if waiting is not None:
+                finish(*waiting)
+            waiting = (rows, out)
+    finish(*waiting)
     west_ref[...] = cols[0:2].astype(BF)
     east_ref[...] = cols[2:4].astype(BF)
+
+    lat_odd, lon_odd = parities()
 
     def give(odd, a_ref, b_ref, after, before):
         @pl.when(odd == 0)
@@ -248,16 +277,16 @@
             a_ref[...] = before
             b_ref[...] = after
 
-    give(odd_ref[1], cols_a_ref, cols_b_ref, cols[2:4].astype(BF), cols[0:2].astype(BF))
+    give(lon_odd, cols_a_ref, cols_b_ref, cols[2:4].astype(BF), cols[0:2].astype(BF))
     rows = [grid_ref[at : at + 2].reshape(2 * TW, C) for at in (TH - 2, 0)]
-    give(odd_ref[0], rows_a_ref.at[: 2 * TW], rows_b_ref.at[: 2 * TW], *rows)
+    give(lat_odd, rows_a_ref.at[: 2 * TW], rows_b_ref.at[: 2 * TW], *rows)
 
 
 def silu(v):
     return v / (1.0 + jnp.exp(-v))
 
 
-def corner_kernel(odd_ref, a_in, b_in, cols_a_ref, cols_b_ref, a_ref, b_ref, part):
+def corner_kernel(a_in, b_in, cols_a_ref, cols_b_ref, a_ref, b_ref, part):
     def write(lon_odd, lat_odd):
         west, east = (cols_a_ref, cols_b_ref) if lon_odd else (cols_b_ref, cols_a_ref)
         for ref, at in ((a_ref, 0 if lat_odd else TH - 2), (b_ref, TH - 2 if lat_odd else 0)):
@@ -266,9 +295,10 @@
                 part[2 * c : 2 * c + 2, :] = column[at : at + 2]
             ref[2 * TW : EDGE, :] = part[...].astype(BF)
 
+    own = parities()
     for lat_odd in (0, 1):
         for lon_odd in (0, 1):
-            pl.when((odd_ref[0] == lat_odd) & (odd_ref[1] == lon_odd))(functools.partial(write, lon_odd, lat_odd))
+            pl.when((own[0] == lat_odd) & (own[1] == lon_odd))(functools.partial(write, lon_odd, lat_odd))
 
 
 def nine(weight, window):
@@ -327,8 +357,6 @@
 
 
 def ring_kernel(
-    lat_ref,
-    odd_ref,
     grid_ref,
     rows_a_ref,
     rows_b_ref,
@@ -360,7 +388,8 @@
         body_ref.at[:, 8 : TW - 8], out_ref.at[2 : TH - 2, 8 : TW - 8], sems.at[4]
     )
     inside.start()
-    lat = lat_ref[0]
+    lat, _ = places()
+    lat_odd, lon_odd = parities()
     keep_top = jnp.where(lat > 0, 1.0, 0.0)
     keep_bottom = jnp.where(lat < 15, 1.0, 0.0)
 
@@ -375,8 +404,8 @@
             after_ref[...] = b_ref[...]
             before_ref[...] = a_ref[...]
 
-    take(odd_ref[0], rows_a_ref, rows_b_ref, south_ref, north_ref)
-    take(odd_ref[1], cols_a_ref, cols_b_ref, east_ref, west_ref)
+    take(lat_odd, rows_a_ref, rows_b_ref, south_ref, north_ref)
+    take(lon_odd, cols_a_ref, cols_b_ref, east_ref, west_ref)
     cs[:, 24:, :] = jnp.zeros((8, 16, C), F32)
     for n, ref in enumerate((west_ref, own_west_ref, own_east_ref, east_ref)):
         for c in range(2):
@@ -480,10 +509,6 @@
     return [pl.BlockSpec(memory_space=pl.ANY)] * count
 
 
-def smem():
-    return pl.BlockSpec(memory_space=pltpu.SMEM)
-
-
 LIMIT = 40 * 1024 * 1024
 
 
@@ -496,12 +521,10 @@
 
 
 def send_call(features, cell_index, tile_rows):
-    here = lax.axis_index("lat") * lax.axis_size("lon") + lax.axis_index("lon")
-    shift = lax.rem(here * ROWS, 128).reshape(1).astype(jnp.int32)
     return pl.pallas_call(
         send_kernel,
         out_shape=pltpu.VMEM((SOURCES, PAIRS, 2, F), BF),
-        in_specs=[smem(), *far(3)],
+        in_specs=far(3),
         out_specs=vmem(1)[0],
         scratch_shapes=[
             pltpu.VMEM((96, 128), jnp.int32),
@@ -514,14 +537,13 @@
         compiler_params=pltpu.CompilerParams(vmem_limit_bytes=LIMIT),
         name="send",
     )(
-        shift,
         in_hbm(features.reshape(SOURCES, PAIRS - 1, 2, F)),
         in_hbm(cell_index.reshape(96, 128)),
         in_hbm(tile_rows.reshape(1, 128)),
     )
 
 
-def frame_call(odd, received, spread, w_in, w_dens):
+def frame_call(received, spread, w_in, w_dens):
     return pl.pallas_call(
         frame_kernel,
         out_shape=(
@@ -529,7 +551,7 @@
             *(pltpu.VMEM((2, TH, C), BF),) * 4,
             *(pltpu.VMEM((EDGE, C), BF),) * 2,
         ),
-        in_specs=[smem(), *vmem(2), smem(), *vmem(2)],
+        in_specs=vmem(5),
         out_specs=tuple(vmem(7)),
         scratch_shapes=[
             pltpu.VMEM((SOURCES * 2, 128), F32),
@@ -542,20 +564,20 @@
         ],
         compiler_params=pltpu.CompilerParams(vmem_limit_bytes=LIMIT),
         name="frame",
-    )(odd, near(received.reshape(SOURCES * ROWS, F)), near(received), spread, near(w_in), near(w_dens.reshape(1, C)))
-
-
-def corner_call(odd, rows_a, rows_b, cols_a, cols_b):
+    )(near(received.reshape(SOURCES * ROWS, F)), near(received), near(spread), near(w_in), near(w_dens.reshape(1, C)))
+
+
+def corner_call(rows_a, rows_b, cols_a, cols_b):
     return pl.pallas_call(
         corner_kernel,
         out_shape=(pltpu.VMEM((EDGE, C), BF),) * 2,
-        in_specs=[smem(), *vmem(4)],
+        in_specs=vmem(4),
         out_specs=tuple(vmem(2)),
         scratch_shapes=[pltpu.VMEM((8, C), F32)],
-        input_output_aliases={1: 0, 2: 1},
+        input_output_aliases={0: 0, 1: 1},
         compiler_params=pltpu.CompilerParams(vmem_limit_bytes=LIMIT),
         name="corner",
-    )(odd, near(rows_a), near(rows_b), near(cols_a), near(cols_b))
+    )(near(rows_a), near(rows_b), near(cols_a), near(cols_b))
 
 
 def work(rows):
@@ -588,11 +610,11 @@
     )(near(hp), near(grid), near(two))
 
 
-def ring_call(lat, odd, *inside):
+def ring_call(*inside):
     return pl.pallas_call(
         ring_kernel,
         out_shape=jax.ShapeDtypeStruct((TH, TW, C), BF),
-        in_specs=[smem(), smem(), *vmem(12)],
+        in_specs=vmem(12),
         out_specs=far(1)[0],
         scratch_shapes=[
             *(pltpu.VMEM((EDGE, C), BF),) * 2,
@@ -610,7 +632,7 @@
         compiler_params=pltpu.CompilerParams(vmem_limit_bytes=LIMIT),
         cost_estimate=work(8),
         name="ring",
-    )(lat, odd, *(near(value) for value in inside))
+    )(*(near(value) for value in inside))
 
 
 def swaps(axis, first, around):
@@ -622,20 +644,16 @@
 def shards(features, cell_index, tile_rows, spread, w_in, w_dens, w_one, w_two):
     sent = send_call(features, cell_index, tile_rows)
     received = lax.all_to_all(sent, ("lat", "lon"), split_axis=0, concat_axis=0, tiled=True)
-    lat = lax.axis_index("lat").astype(jnp.int32)
-    odd = jnp.stack([lat % 2, lax.axis_index("lon").astype(jnp.int32) % 2])
-    grid, own_west, own_east, cols_a, cols_b, rows_a, rows_b = frame_call(odd, received, spread, w_in, w_dens)
+    grid, own_west, own_east, cols_a, cols_b, rows_a, rows_b = frame_call(received, spread, w_in, w_dens)
     one, two = w_one.reshape(9, C, C), w_two.reshape(9, C, C)
     cols_b = lax.ppermute(cols_b, "lon", swaps("lon", 1, True))
     cols_a = lax.ppermute(cols_a, "lon", swaps("lon", 0, True))
     hp, hcols = inner_one_call(grid, one)
-    rows_a, rows_b = corner_call(odd, rows_a, rows_b, cols_a, cols_b)
+    rows_a, rows_b = corner_call(rows_a, rows_b, cols_a, cols_b)
     rows_b = lax.ppermute(rows_b, "lat", swaps("lat", 1, False))
     rows_a = lax.ppermute(rows_a, "lat", swaps("lat", 0, False))
     body = inner_two_call(hp, grid, two)
-    return ring_call(
-        lat.reshape(1), odd, grid, rows_a, rows_b, cols_a, cols_b, own_west, own_east, hp, hcols, body, one, two
-    )
+    return ring_call(grid, rows_a, rows_b, cols_a, cols_b, own_west, own_east, hp, hcols, body, one, two)
 
 
 def solution(mesh):

time: 86.7 us -> 84.6 us (0.976)
  blocking collectives: 0 us -> 51.5 us
  waiting for transfers between devices: 44.1 us -> 2.81 us
  starting transfers between devices: 16.4 us -> 5.98 us
  local copies, waits for them, and re-layouts: 1.68 us -> 0.03 us
    all_to_all x0 -> x1, blocking collectives: none -> 51.5 us  [shards(): lax.all_to_all(sent, ('lat', 'lon'), split_axis=0, concat_axis=0, tiled=T...]
    all_to_all x1 -> x0, waiting for transfers between devices: 41.1 us -> none  [shards(): lax.all_to_all(sent, ('lat', 'lon'), split_axis=0, concat_axis=0, tiled=T...]
    all_to_all x1 -> x0, starting transfers between devices: 10.4 us -> none  [shards(): lax.all_to_all(sent, ('lat', 'lon'), split_axis=0, concat_axis=0, tiled=T...]
    unnamed x12 -> x10, local copies, waits for them, and re-layouts: 1.68 us -> 0.03 us
    pallas_call x1, Pallas kernels: 12 us -> 13 us  [frame_call(): pl.pallas_call(frame_kernel, out_shape=(pltpu.VMEM((TH, NP, NQ, C), BF),...]
  transfers between devices with their start and end apart: 5 -> 4, of which waited for: 3 -> 2; matrix products, arithmetic and copies ran while one was open for 0% -> 0% of each run, Pallas kernels for 6% -> 6%
where the time goes in v5:
time: 84.6 us; the launch traced here: 84.5 us
  blocking collectives  51.5 us (61%)
  Pallas kernels  23.9 us (28%)
  starting transfers between devices  5.98 us (7%)
  waiting for transfers between devices  2.81 us (3%)
    all_to_all x1, blocking collectives, shards(): lax.all_to_all(sent, ('lat', 'lon'), split_axis=0, concat_axis=0, tiled=T...  51.5 us
    pallas_call x1, Pallas kernels, frame_call(): pl.pallas_call(frame_kernel, out_shape=(pltpu.VMEM((TH, NP, NQ, C), BF),...  13 us
    pallas_call x1, Pallas kernels, ring_call(): pl.pallas_call(ring_kernel, out_shape=jax.ShapeDtypeStruct((TH, TW, C), B...  3.52 us
    ppermute x1, starting transfers between devices, shards(): rows_b = lax.ppermute(rows_b, 'lat', swaps('lat', 1, False))  3.36 us
    pallas_call x1, Pallas kernels, inner_one_call(): pl.pallas_call(inner_one_kernel, out_shape=(pltpu.VMEM((TH + 2, NP + 2, N...  2.87 us
    ppermute x1, waiting for transfers between devices, shards(): rows_b = lax.ppermute(rows_b, 'lat', swaps('lat', 1, False))  2.7 us
    pallas_call x1, Pallas kernels, inner_two_call(): pl.pallas_call(inner_two_kernel, out_shape=pltpu.VMEM((TH - 4, TW, C), BF...  2.55 us
    pallas_call x1, Pallas kernels, send_call(): pl.pallas_call(send_kernel, out_shape=pltpu.VMEM((SOURCES, PAIRS, 2, F),...  1.95 us
  transfers between devices with their start and end apart: 4, of which 2 were waited for; matrix products, arithmetic and copies ran while one was open for 0% of the time, Pallas kernels for 6%

profile of v5, /device:TPU:8, one launch (start us, length us, event | category | flops | bytes accessed | tf_op | source)
XLA Modules:
  0.0 84.5 jit_solution(14068179995811973741)
XLA Ops:
  0.0 1.9 %send.1 = bf16[128,49,2,128]{3,2,1,0:T(2,128)(2,1)S(1)} custom-call(bf16[128,48,2,128]{3,2,1,0:T(2,128)(2,1)} %bitcast.13, s32[96,128]{1,0:T(8,128)} %bitcast.14, s32[1,128]{1,0:T(1,128)} %bitcast.15), custom_call_target="tpu_custom_call" | custom-call | tf_op jit(solution)/shard_map/send/pallas_call | solution.py:524
  2.0 0.0 copy-start.2
  2.0 0.0 copy-start.3
  2.0 0.0 copy-start.4
  2.0 51.5 %all_to_all.5.where_ref = bf16[128,49,2,128]{3,2,1,0:T(2,128)(2,1)S(1)} all-to-all(bf16[128,49,2,128]{3,2,1,0:T(2,128)(2,1)S(1)} %send.1), channel_id=1, replica_groups=mesh['lat'=16,'lon'=8] {'lat','lon'}, dimensions={0} | all-to-all | bytes 6422528 | tf_op jit(solution)/shard_map/all_to_all | solution.py:646
  53.5 0.0 copy-done.2
  53.5 0.0 copy-done.3
  53.5 0.0 copy-done.4
  53.5 0.0 copy-start
  53.5 13.0 %frame.1 = (bf16[24,6,16,256]{3,2,1,0:T(8,128)(2,1)S(1)}, bf16[2,24,256]{2,1,0:T(8,128)(2,1)S(1)}, bf16[2,24,256]{2,1,0:T(8,128)(2,1)S(1)}, bf16[2,24,256]{2,1,0...) custom-call(bf16[12544,128]{1,0:T(8,128)(2,1)S(1)} %bitcast.7, ...), custom_call_target="tpu_custom_call" | custom-call | tf_op jit(solution)/shard_map/frame/pallas_call | solution.py:547
  66.5 0.1 collective-permute-start
  66.6 1.7 %collective-permute-start.1 = (bf16[2,24,256]{2,1,0:T(8,128)(2,1)S(1)}, bf16[2,24,256]{2,1,0:T(8,128)(2,1)S(1)}, u32[]{:S(2)}, u32[]{:S(2)}) collective-permute-start(bf16[2,24,256]{2,1,0:T(8,128)(2,1)S(1)} %get-tuple-element.20), channel_id=1, source_target_pairs={{1,2},{3,4},{5,6},{7,0},{2,1},{4,3},{6,5},{0,7},{9,10},{11,12},{13... | collective-permute-start | bytes 73736 | tf_op jit(solution)/shard_map/ppermute | solution.py:649
  68.3 0.0 copy-done
  68.3 0.0 copy-start.1
  68.3 2.9 %inner_one.1 = (bf16[26,8,16,256]{3,2,1,0:T(8,128)(2,1)S(1)}, f32[4,40,256]{2,1,0:T(8,128)S(1)}) custom-call(bf16[24,6,16,256]{3,2,1,0:T(8,128)(2,1)S(1)} %get-tuple-element.16.grid_ref, bf16[9,256,256]{2,1,0:T(8,128)(2,1)S(1)} %bitcast.8), custom_call_target="tpu_custom_call" | custom-call | flops 2491416576 | tf_op jit(solution)/shard_map/inner_one/pallas_call | solution.py:588
  71.2 0.0 collective-permute-done.cols_a_ref
  71.2 0.1 collective-permute-done.1.cols_b_ref
  71.3 0.8 collective-permute-start.2
  72.1 3.4 %collective-permute-start.3 = (bf16[200,256]{1,0:T(8,128)(2,1)S(1)}, bf16[200,256]{1,0:T(8,128)(2,1)S(1)}, u32[]{:S(2)}, u32[]{:S(2)}) collective-permute-start(bf16[200,256]{1,0:T(8,128)(2,1)S(1)} %get-tuple-element.22), channel_id=1, source_target_pairs={{8,16},{24,32},{40,48},{56,64},{72,80},{88,96},{104,112},{16,8},{3... | collective-permute-start | bytes 307208 | tf_op jit(solution)/shard_map/ppermute | solution.py:653
  75.5 0.0 copy-done.1
  75.5 2.6 %inner_two.1.body_ref = bf16[20,96,256]{2,1,0:T(8,128)(2,1)S(1)} custom-call(bf16[26,8,16,256]{3,2,1,0:T(8,128)(2,1)S(1)} %get-tuple-element.25.hp_ref, bf16[24,6,16,256]{3,2,1,0:T(8,128)(2,1)S(1)} %get-tuple-element.16.grid_ref, bf16[9,256,256]{2,1,0:T(8,128)(2,1)S(1)} %bitcast.10), custom_call_target="tpu_custom_call" | custom-call | flops 2264924160 | tf_op jit(solution)/shard_map/inner_two/pallas_call | solution.py:601
  78.1 0.0 collective-permute-done.2.rows_a_ref
  78.1 2.7 %collective-permute-done.3.rows_b_ref = bf16[200,256]{1,0:T(8,128)(2,1)S(1)} collective-permute-done((bf16[200,256]{1,0:T(8,128)(2,1)S(1)}, bf16[200,256]{1,0:T(8,128)(2,1)S(1)}, u32[]{:S(2)}, u32[]{:S(2)}) %collective-permute-start.3) | collective-permute-done | bytes 102432 | tf_op jit(solution)/shard_map/ppermute | solution.py:653
  80.8 3.5 %ring.1 = bf16[24,96,256]{2,1,0:T(8,128)(2,1)} custom-call(bf16[24,6,16,256]{3,2,1,0:T(8,128)(2,1)S(1)} %get-tuple-element.16.grid_ref, bf16[200,256]{1,0:T(8,128)(2,1)S(1)} %collective-permute-done.2.rows_a_ref, bf16[200,256]{1,0:T(8,128)(2,1)S(1)} %collective-permute-done.3.rows_b_ref, bf16[2,24,256]{2,1,0:T(8,128)(2,1)S(1)} %collective-permute-done.cols_a_ref, ...), custom_call_target="tpu_custom_call" | custom-call | flops 905969664 | tf_op jit(solution)/shard_map/ring/pallas_call | solution.py:614
  (1 shorter events, 0.0 us)
Async XLA Ops:
  2.0 51.5 %copy-start.2 = (bf16[128,256]{1,0:T(8,128)(2,1)S(1)}, bf16[128,256]{1,0:T(8,128)(2,1)}, u32[]{:S(2)}) copy-start(bf16[128,256]{1,0:T(8,128)(2,1)} %win_ref.1) | copy-start | bytes 196612
  2.0 51.5 %copy-start.3 = (f32[3,3]{1,0:T(4,128)S(1)}, f32[3,3]{1,0:T(4,128)}, u32[]{:S(2)}) copy-start(f32[3,3]{1,0:T(4,128)} %spread_ref.1) | copy-start | bytes 112
  2.0 51.5 %copy-start.4 = (f32[256]{0:T(256)S(1)}, f32[256]{0:T(256)}, u32[]{:S(2)}) copy-start(f32[256]{0:T(256)} %param.13) | copy-start | bytes 3076
  53.5 14.8 %copy-start = (bf16[3,3,256,256]{3,2,1,0:T(8,128)(2,1)S(1)}, bf16[3,3,256,256]{3,2,1,0:T(8,128)(2,1)}, u32[]{:S(2)}) copy-start(bf16[3,3,256,256]{3,2,1,0:T(8,128)(2,1)} %param.14) | copy-start | bytes 3538948
  66.5 4.7 %collective-permute-start = (bf16[2,24,256]{2,1,0:T(8,128)(2,1)S(1)}, bf16[2,24,256]{2,1,0:T(8,128)(2,1)S(1)}, u32[]{:S(2)}, u32[]{:S(2)}) collective-permute-start(bf16[2,24,256]{2,1,0:T(8,128)(2,1)S(1)} %get-tuple-element.19), channel_id=1, source_target_pairs={{0,1},{2,3},{4,5},{6,7},{1,0},{3,2},{5,4},{7,6},{8,9},{10,11},{12,... | collective-permute-start | bytes 73736 | tf_op jit(solution)/shard_map/ppermute | solution.py:650
  66.6 4.7 %collective-permute-start.1 = (bf16[2,24,256]{2,1,0:T(8,128)(2,1)S(1)}, bf16[2,24,256]{2,1,0:T(8,128)(2,1)S(1)}, u32[]{:S(2)}, u32[]{:S(2)}) collective-permute-start(bf16[2,24,256]{2,1,0:T(8,128)(2,1)S(1)} %get-tuple-element.20), channel_id=1, source_target_pairs={{1,2},{3,4},{5,6},{7,0},{2,1},{4,3},{6,5},{0,7},{9,10},{11,12},{13... | collective-permute-start | bytes 73736 | tf_op jit(solution)/shard_map/ppermute | solution.py:649
  68.3 7.2 %copy-start.1 = (bf16[3,3,256,256]{3,2,1,0:T(8,128)(2,1)S(1)}, bf16[3,3,256,256]{3,2,1,0:T(8,128)(2,1)}, u32[]{:S(2)}) copy-start(bf16[3,3,256,256]{3,2,1,0:T(8,128)(2,1)} %param.15) | copy-start | bytes 3538948
  71.3 6.8 %collective-permute-start.2 = (bf16[200,256]{1,0:T(8,128)(2,1)S(1)}, bf16[200,256]{1,0:T(8,128)(2,1)S(1)}, u32[]{:S(2)}, u32[]{:S(2)}) collective-permute-start(bf16[200,256]{1,0:T(8,128)(2,1)S(1)} %get-tuple-element.21), channel_id=1, source_target_pairs={{0,8},{16,24},{32,40},{48,56},{64,72},{80,88},{96,104},{112,120},{... | collective-permute-start | bytes 307208 | tf_op jit(solution)/shard_map/ppermute | solution.py:654
  72.1 8.7 %collective-permute-start.3 = (bf16[200,256]{1,0:T(8,128)(2,1)S(1)}, bf16[200,256]{1,0:T(8,128)(2,1)S(1)}, u32[]{:S(2)}, u32[]{:S(2)}) collective-permute-start(bf16[200,256]{1,0:T(8,128)(2,1)S(1)} %get-tuple-element.22), channel_id=1, source_target_pairs={{8,16},{24,32},{40,48},{56,64},{72,80},{88,96},{104,112},{16,8},{3... | collective-permute-start | bytes 307208 | tf_op jit(solution)/shard_map/ppermute | solution.py:653

commit v6 on v5

--- a/solution.py
+++ b/solution.py
@@ -22,7 +22,6 @@
 ROWS = CAP + 2
 PAIRS = ROWS // 2
 MAIN = HALF * TW
-EDGE = 2 * TW + 8
 LHS = MAIN + 32
 GROUPS = 7
 PER = ROWS // GROUPS
@@ -109,8 +108,6 @@
     grid_ref,
     west_ref,
     east_ref,
-    cols_a_ref,
-    cols_b_ref,
     rows_a_ref,
     rows_b_ref,
     c32,
@@ -181,10 +178,8 @@
         if g == 0:
             acc[...] = dot(left, right)
             cnt[...] = some
-        elif g + 1 < GROUPS:
+        else:
             acc[...] += dot(left, right)
-            cnt[...] += some
-        else:
             cnt[...] += some
 
     def weight(a, b, shape):
@@ -195,16 +190,11 @@
         base = (r % HALF) * TW + NQ * (p - 1)
         return pads[r, p // NP] if p in (0, NP + 1) else acc[base : base + NQ, lanes_of]
 
-    def complete(start, stop):
-        rows = slice(start * TW, stop * TW)
-        acc[rows, :] += dot(left[rows], right)
-        for r in (*range(start, stop), *range(HALF + start, HALF + stop)):
-            lanes_of = slice((r // HALF) * 128, (r // HALF) * 128 + 128)
-            at = MAIN + r % HALF
-            pads[r, 0] = with_row(tile(r, NP), 1, acc[at : at + 1, lanes_of], 0)
-            pads[r, 1] = with_row(tile(r, 1), NQ - 1, acc[at + HALF : at + HALF + 1, lanes_of], NQ - 1)
-
-    acc[MAIN:, :] += dot(left[MAIN:], right)
+    for r in range(PH):
+        lanes_of = slice((r // HALF) * 128, (r // HALF) * 128 + 128)
+        at = MAIN + r % HALF
+        pads[r, 0] = with_row(tile(r, NP), 1, acc[at : at + 1, lanes_of], 0)
+        pads[r, 1] = with_row(tile(r, 1), NQ - 1, acc[at + HALF : at + HALF + 1, lanes_of], NQ - 1)
 
     number = jnp.transpose(jnp.concatenate([cnt[...], jnp.zeros((96, 128), F32)], axis=0))
     number = [
@@ -246,59 +236,53 @@
             for c, at in enumerate((0, NQ, 5 * NQ - 1, 6 * NQ - 1)):
                 cols[c, i : i + 1, :] = wide[at : at + 1]
 
-    plan = (
-        (0, 5, ((0, 1, 2), (13, 14, 15))),
-        (5, 9, ((3, 4, 5, 6), (16, 17, 18, 19))),
-        (9, 13, ((7, 8, 9, 10), (20, 21, 22, 23), (11, 12))),
-    )
-    waiting = None
-    for start, stop, sets in plan:
-        complete(start, stop)
-        for rows in sets:
-            average(rows)
-            out = project(rows)
-            if waiting is not None:
-                finish(*waiting)
-            waiting = (rows, out)
-    finish(*waiting)
+    sets = [range(i, i + 4) for i in range(0, TH, 4)]
+    average(sets[0])
+    for n, rows in enumerate(sets):
+        out = project(rows)
+        if n + 1 < len(sets):
+            average(sets[n + 1])
+        finish(rows, out)
     west_ref[...] = cols[0:2].astype(BF)
     east_ref[...] = cols[2:4].astype(BF)
 
-    lat_odd, lon_odd = parities()
-
-    def give(odd, a_ref, b_ref, after, before):
-        @pl.when(odd == 0)
-        def _():
-            a_ref[...] = after
-            b_ref[...] = before
-
-        @pl.when(odd != 0)
-        def _():
-            a_ref[...] = before
-            b_ref[...] = after
-
-    give(lon_odd, cols_a_ref, cols_b_ref, cols[2:4].astype(BF), cols[0:2].astype(BF))
+    lat_odd, _ = parities()
     rows = [grid_ref[at : at + 2].reshape(2 * TW, C) for at in (TH - 2, 0)]
-    give(lat_odd, rows_a_ref.at[: 2 * TW], rows_b_ref.at[: 2 * TW], *rows)
+    give(lat_odd, rows_a_ref, rows_b_ref, *rows)
+
+
+def give(odd, a_ref, b_ref, after, before):
+    @pl.when(odd == 0)
+    def _():
+        a_ref[...] = after
+        b_ref[...] = before
+
+    @pl.when(odd != 0)
+    def _():
+        a_ref[...] = before
+        b_ref[...] = after
 
 
 def silu(v):
     return v / (1.0 + jnp.exp(-v))
 
 
-def corner_kernel(a_in, b_in, cols_a_ref, cols_b_ref, a_ref, b_ref, part):
-    def write(lon_odd, lat_odd):
-        west, east = (cols_a_ref, cols_b_ref) if lon_odd else (cols_b_ref, cols_a_ref)
-        for ref, at in ((a_ref, 0 if lat_odd else TH - 2), (b_ref, TH - 2 if lat_odd else 0)):
-            for c in range(4):
-                column = (west if c < 2 else east)[c % 2].astype(F32)
-                part[2 * c : 2 * c + 2, :] = column[at : at + 2]
-            ref[2 * TW : EDGE, :] = part[...].astype(BF)
-
-    own = parities()
-    for lat_odd in (0, 1):
-        for lon_odd in (0, 1):
-            pl.when((own[0] == lat_odd) & (own[1] == lon_odd))(functools.partial(write, lon_odd, lat_odd))
+def column_kernel(rows_a_ref, rows_b_ref, west_ref, east_ref, a_ref, b_ref, tall):
+    lat_odd, lon_odd = parities()
+    tall[:, 24:, :] = jnp.zeros((4, 8, C), F32)
+    for c in range(4):
+        tall[c, 2 : 2 + TH, :] = (west_ref if c < 2 else east_ref)[c % 2].astype(F32)
+
+    def halo(north, south):
+        for ref, at in ((north, 0), (south, 2 + TH)):
+            for k in range(2):
+                for c, p in enumerate((0, 1, 4, 5)):
+                    tile = ref[k * TW + p * NQ : k * TW + (p + 1) * NQ, :].astype(F32)
+                    tall[c, at + k : at + k + 1, :] = tile[:1] if c < 2 else tile[NQ - 1 :]
+
+    pl.when(lat_odd == 0)(lambda: halo(rows_b_ref, rows_a_ref))
+    pl.when(lat_odd != 0)(lambda: halo(rows_a_ref, rows_b_ref))
+    give(lon_odd, a_ref, b_ref, tall[2:4].astype(BF), tall[0:2].astype(BF))
 
 
 def nine(weight, window):
@@ -356,148 +340,128 @@
             body_ref[at : at + step, :, 128 * h : 128 * (h + 1)] = block
 
 
-def ring_kernel(
-    grid_ref,
-    rows_a_ref,
-    rows_b_ref,
-    cols_a_ref,
-    cols_b_ref,
-    own_west_ref,
-    own_east_ref,
-    hp_ref,
+def keeps():
+    lat, _ = places()
+    return jnp.where(lat > 0, 1.0, 0.0), jnp.where(lat < 15, 1.0, 0.0)
+
+
+def edge_kernel(
+    grid_ref, rows_a_ref, rows_b_ref, hp_ref, one_ref, two_ref, out_ref, ecols_ref, north_ref, south_ref, gp, hr, flat
+):
+    keep_top, keep_bottom = keeps()
+    lat_odd, _ = parities()
+
+    @pl.when(lat_odd == 0)
+    def _():
+        south_ref[...] = rows_a_ref[...]
+        north_ref[...] = rows_b_ref[...]
+
+    @pl.when(lat_odd != 0)
+    def _():
+        south_ref[...] = rows_b_ref[...]
+        north_ref[...] = rows_a_ref[...]
+
+    tiles = [north_ref[k * TW : (k + 1) * TW, :].reshape(NP, NQ, C) for k in range(2)]
+    tiles += [grid_ref[g] for g in (0, 1, TH - 2, TH - 1)]
+    tiles += [south_ref[k * TW : (k + 1) * TW, :].reshape(NP, NQ, C) for k in range(2)]
+    for slot, tile in enumerate(tiles):
+        first, last = tile[0].astype(F32), tile[NP - 1].astype(F32)
+        padded(gp, slot, tile, first, last, first[:1], last[NQ - 1 :])
+
+    def window(src, a, b):
+        return jnp.concatenate(
+            [src[at + a : at + a + 2, b : b + NP].reshape(2 * TW, C) for at in (0, 4)], axis=0
+        )
+
+    value = silu(nine(one_ref, functools.partial(window, gp)))
+    for n, slot in enumerate((0, 1, 6, 7)):
+        row = value[n * TW : (n + 1) * TW]
+        if n == 0:
+            row = row * keep_top
+        if n == 3:
+            row = row * keep_bottom
+        row = row.reshape(NP, NQ, C)
+        for c, (p, q) in enumerate(((1, 0), (2, 0), (3, NQ - 1), (4, NQ - 1))):
+            ecols_ref[c, n : n + 1, :] = row[p, q : q + 1]
+        padded(hr, slot, row.astype(BF), row[0], row[NP - 1], row[0, :1], row[NP - 1, NQ - 1 :])
+    for slot, g in ((2, 2), (3, 3), (4, TH - 2), (5, TH - 1)):
+        hr[slot] = hp_ref[g]
+    value = nine(two_ref, functools.partial(window, hr))
+    for n, i in enumerate((0, 1, TH - 2, TH - 1)):
+        spread_out(flat, n, value[n * TW : (n + 1) * TW].reshape(NP, NQ, C) + grid_ref[i].astype(F32))
+    for h in range(2):
+        out_ref[:, :, 128 * h : 128 * (h + 1)] = flat[h].astype(BF).reshape(4, TW, 128)
+
+
+def last_kernel(
+    sent_a_ref,
+    sent_b_ref,
+    got_a_ref,
+    got_b_ref,
     hcols_ref,
+    ecols_ref,
     body_ref,
+    edge_ref,
     one_ref,
     two_ref,
     out_ref,
-    north_ref,
-    south_ref,
-    west_ref,
-    east_ref,
     cs,
-    gp,
     hc,
-    hr,
-    flat,
     oc,
-    lines,
     strips,
     sems,
 ):
-    inside = pltpu.make_async_copy(
-        body_ref.at[:, 8 : TW - 8], out_ref.at[2 : TH - 2, 8 : TW - 8], sems.at[4]
-    )
-    inside.start()
-    lat, _ = places()
-    lat_odd, lon_odd = parities()
-    keep_top = jnp.where(lat > 0, 1.0, 0.0)
-    keep_bottom = jnp.where(lat < 15, 1.0, 0.0)
-
-    def take(odd, a_ref, b_ref, after_ref, before_ref):
-        @pl.when(odd == 0)
-        def _():
-            after_ref[...] = a_ref[...]
-            before_ref[...] = b_ref[...]
-
-        @pl.when(odd != 0)
-        def _():
-            after_ref[...] = b_ref[...]
-            before_ref[...] = a_ref[...]
-
-    take(lat_odd, rows_a_ref, rows_b_ref, south_ref, north_ref)
-    take(lon_odd, cols_a_ref, cols_b_ref, east_ref, west_ref)
-    cs[:, 24:, :] = jnp.zeros((8, 16, C), F32)
-    for n, ref in enumerate((west_ref, own_west_ref, own_east_ref, east_ref)):
-        for c in range(2):
-            cs[2 * n + c, 2 : 2 + TH, :] = ref[c].astype(F32)
-    for ref, at in ((north_ref, 0), (south_ref, 2 + TH)):
-        corner = ref[2 * TW : EDGE, :].astype(F32)
-        for n, c in enumerate((0, 1, 6, 7)):
-            cs[c, at : at + 2, :] = corner[2 * n : 2 * n + 2]
-        for k in range(2):
-            line = ref[k * TW : (k + 1) * TW, :].astype(F32)
-            for c, place in ((2, 0), (3, NQ), (4, 5 * NQ - 1), (5, 6 * NQ - 1)):
-                cs[c, at + k : at + k + 1, :] = line[place : place + 1]
-            tile = ref[k * TW : (k + 1) * TW, :].reshape(NP, NQ, C)
-            row = at + k
-            slot = row if at == 0 else row - 20
-            padded(gp, slot, tile, line[:NQ], line[TW - NQ :], cs[1, row : row + 1, :], cs[6, row : row + 1, :])
-    for g, slot in ((0, 2), (1, 3), (TH - 2, 4), (TH - 1, 5)):
-        tile = grid_ref[g]
-        row = g + 2
-        padded(
-            gp,
-            slot,
-            tile,
-            tile[0].astype(F32),
-            tile[NP - 1].astype(F32),
-            cs[1, row : row + 1, :],
-            cs[6, row : row + 1, :],
-        )
-
-    def ring(rows, columns, a, b):
-        parts = [rows[at + a : at + a + 2, b : b + NP].reshape(2 * TW, C) for at in (0, 4)]
-        parts += [columns[c + b, a : a + 32, :].astype(BF) for c in (0, 1, 4, 5)]
-        return jnp.concatenate(parts, axis=0)
-
-    value = silu(nine(one_ref, functools.partial(ring, gp, cs)))
+    middle = slice(8, TW - 8)
+    copies = [
+        pltpu.make_async_copy(body_ref.at[:, middle], out_ref.at[2 : TH - 2, middle], sems.at[0]),
+        pltpu.make_async_copy(edge_ref.at[:2, middle], out_ref.at[:2, middle], sems.at[1]),
+        pltpu.make_async_copy(edge_ref.at[2:, middle], out_ref.at[TH - 2 :, middle], sems.at[2]),
+    ]
+    for copy in copies:
+        copy.start()
+    keep_top, keep_bottom = keeps()
+    _, lon_odd = parities()
+    cs[:, 32:, :] = jnp.zeros((8, 8, C), F32)
+    hc[:, 32:, :] = jnp.zeros((8, 8, C), F32)
+
+    def fill(got_before, sent_before, sent_after, got_after):
+        for n, ref in enumerate((got_before, sent_before, sent_after, got_after)):
+            cs[2 * n : 2 * n + 2, 0:32, :] = ref[...].astype(F32)
+
+    pl.when(lon_odd == 0)(lambda: fill(got_b_ref, sent_b_ref, sent_a_ref, got_a_ref))
+    pl.when(lon_odd != 0)(lambda: fill(got_a_ref, sent_a_ref, sent_b_ref, got_b_ref))
+
+    def window(src, a, b):
+        return jnp.concatenate([src[c + b, a : a + 32, :].astype(BF) for c in (0, 1, 4, 5)], axis=0)
+
+    value = silu(nine(one_ref, functools.partial(window, cs)))
     line = iota((32, C), 0)
     for n, c in enumerate((0, 1, 6, 7)):
-        column = value[4 * TW + 32 * n : 4 * TW + 32 * (n + 1)]
+        column = value[32 * n : 32 * (n + 1)]
         column = jnp.where(line == 0, column * keep_top, column)
         hc[c, 0:32, :] = jnp.where(line == TH + 1, column * keep_bottom, column)
     for c in range(4):
         hc[2 + c, 0:32, :] = hcols_ref[c, 0:32, :]
-    for c in range(8):
-        hc[c, 32:40, :] = jnp.zeros((8, C), F32)
-    for n, g in enumerate((0, 1, TH, TH + 1)):
-        row = value[n * TW : (n + 1) * TW]
-        if g == 0:
-            row = row * keep_top
-        if g == TH + 1:
-            row = row * keep_bottom
-        row = row.reshape(NP, NQ, C)
-        for c, (p, q) in enumerate(((1, 0), (2, 0), (3, NQ - 1), (4, NQ - 1))):
-            hc[2 + c, g : g + 1, :] = row[p, q : q + 1]
-        slot = g if g < 4 else g - 18
-        padded(
-            hr, slot, row.astype(BF), row[0], row[NP - 1], hc[0, g : g + 1, :], hc[7, g : g + 1, :]
-        )
-    place = iota((NQ, C), 0)
-    for g, slot in ((2, 2), (3, 3), (TH - 2, 4), (TH - 1, 5)):
-        tile = hp_ref[g, 1 : NP + 1]
-        first = jnp.where(place == 0, hc[1, g : g + 1, :], tile[0].astype(F32))
-        last = jnp.where(place == NQ - 1, hc[6, g : g + 1, :], tile[NP - 1].astype(F32))
-        padded(hr, slot, tile, first, last, hc[0, g : g + 1, :], hc[7, g : g + 1, :])
-        hr[slot, 1] = first.astype(BF)
-        hr[slot, NP] = last.astype(BF)
-
-    value = nine(two_ref, functools.partial(ring, hr, hc))
-    for n, i in enumerate((0, 1, TH - 2, TH - 1)):
-        row = value[n * TW : (n + 1) * TW].reshape(NP, NQ, C) + grid_ref[i].astype(F32)
-        spread_out(flat, n, row)
-    copies = []
-    for h in range(2):
-        lines[:, :, 128 * h : 128 * (h + 1)] = flat[h].astype(BF).reshape(4, TW, 128)
-    for n, i in enumerate((0, TH - 2)):
-        copies.append(pltpu.make_async_copy(lines.at[2 * n : 2 * n + 2], out_ref.at[i : i + 2], sems.at[n]))
-        copies[-1].start()
+        hc[2 + c, 0:2, :] = ecols_ref[c, 0:2, :]
+        hc[2 + c, TH : TH + 2, :] = ecols_ref[c, 2:4, :]
+    value = nine(two_ref, functools.partial(window, hc))
     for c in range(4):
-        column = value[4 * TW + 32 * c : 4 * TW + 32 * c + TH]
-        oc[c] = column + cs[2 + c, 2 : 2 + TH, :]
+        oc[c] = value[32 * c : 32 * c + TH] + cs[2 + c, 2 : 2 + TH, :]
     place = iota((8, C), 0)
-    for i in range(2, TH - 2):
-        left, right = body_ref[i - 2, :8].astype(F32), body_ref[i - 2, TW - 8 :].astype(F32)
+    for i in range(TH):
+        if 2 <= i < TH - 2:
+            rows, at = body_ref, i - 2
+        else:
+            rows, at = edge_ref, i if i < 2 else i - TH + 4
+        left, right = rows[at, :8].astype(F32), rows[at, TW - 8 :].astype(F32)
         left = jnp.where(place == 0, oc[0, i : i + 1, :], jnp.where(place == 1, oc[1, i : i + 1, :], left))
         right = jnp.where(place == 6, oc[2, i : i + 1, :], jnp.where(place == 7, oc[3, i : i + 1, :], right))
-        strips[0, i - 2] = left.astype(BF)
-        strips[1, i - 2] = right.astype(BF)
+        strips[0, i] = left.astype(BF)
+        strips[1, i] = right.astype(BF)
     for n, at in enumerate((0, TW - 8)):
-        copies.append(
-            pltpu.make_async_copy(strips.at[n], out_ref.at[2 : TH - 2, at : at + 8], sems.at[2 + n])
-        )
+        copies.append(pltpu.make_async_copy(strips.at[n], out_ref.at[:, at : at + 8], sems.at[3 + n]))
         copies[-1].start()
-    for copy in [*copies, inside]:
+    for copy in copies:
         copy.wait()
 
 
@@ -548,11 +512,11 @@
         frame_kernel,
         out_shape=(
             pltpu.VMEM((TH, NP, NQ, C), BF),
-            *(pltpu.VMEM((2, TH, C), BF),) * 4,
-            *(pltpu.VMEM((EDGE, C), BF),) * 2,
+            *(pltpu.VMEM((2, TH, C), BF),) * 2,
+            *(pltpu.VMEM((2 * TW, C), BF),) * 2,
         ),
         in_specs=vmem(5),
-        out_specs=tuple(vmem(7)),
+        out_specs=tuple(vmem(5)),
         scratch_shapes=[
             pltpu.VMEM((SOURCES * 2, 128), F32),
             pltpu.VMEM((4, 104, 128), F32),
@@ -567,17 +531,16 @@
     )(near(received.reshape(SOURCES * ROWS, F)), near(received), near(spread), near(w_in), near(w_dens.reshape(1, C)))
 
 
-def corner_call(rows_a, rows_b, cols_a, cols_b):
+def column_call(rows_a, rows_b, west, east):
     return pl.pallas_call(
-        corner_kernel,
-        out_shape=(pltpu.VMEM((EDGE, C), BF),) * 2,
+        column_kernel,
+        out_shape=(pltpu.VMEM((2, 32, C), BF),) * 2,
         in_specs=vmem(4),
         out_specs=tuple(vmem(2)),
-        scratch_shapes=[pltpu.VMEM((8, C), F32)],
-        input_output_aliases={0: 0, 1: 1},
+        scratch_shapes=[pltpu.VMEM((4, 32, C), F32)],
         compiler_params=pltpu.CompilerParams(vmem_limit_bytes=LIMIT),
-        name="corner",
-    )(near(rows_a), near(rows_b), near(cols_a), near(cols_b))
+        name="column",
+    )(*(near(value) for value in (rows_a, rows_b, west, east)))
 
 
 def work(rows):
@@ -610,28 +573,38 @@
     )(near(hp), near(grid), near(two))
 
 
-def ring_call(*inside):
+def edge_call(*inside):
     return pl.pallas_call(
-        ring_kernel,
+        edge_kernel,
+        out_shape=(pltpu.VMEM((4, TW, C), BF), pltpu.VMEM((4, 8, C), F32)),
+        in_specs=vmem(6),
+        out_specs=tuple(vmem(2)),
+        scratch_shapes=[
+            *(pltpu.VMEM((2 * TW, C), BF),) * 2,
+            *(pltpu.VMEM((8, NP + 2, NQ, C), BF),) * 2,
+            pltpu.VMEM((2, 4 * TW, 128), F32),
+        ],
+        compiler_params=pltpu.CompilerParams(vmem_limit_bytes=LIMIT),
+        cost_estimate=work(8),
+        name="edge",
+    )(*(near(value) for value in inside))
+
+
+def last_call(*inside):
+    return pl.pallas_call(
+        last_kernel,
         out_shape=jax.ShapeDtypeStruct((TH, TW, C), BF),
-        in_specs=vmem(12),
+        in_specs=vmem(10),
         out_specs=far(1)[0],
         scratch_shapes=[
-            *(pltpu.VMEM((EDGE, C), BF),) * 2,
-            *(pltpu.VMEM((2, TH, C), BF),) * 2,
-            pltpu.VMEM((8, 40, C), F32),
-            pltpu.VMEM((8, NP + 2, NQ, C), BF),
-            pltpu.VMEM((8, 40, C), F32),
-            pltpu.VMEM((8, NP + 2, NQ, C), BF),
-            pltpu.VMEM((2, 4 * TW, 128), F32),
+            *(pltpu.VMEM((8, 40, C), F32),) * 2,
             pltpu.VMEM((4, TH, C), F32),
-            pltpu.VMEM((4, TW, C), BF),
-            pltpu.VMEM((2, TH - 4, 8, C), BF),
+            pltpu.VMEM((2, TH, 8, C), BF),
             pltpu.SemaphoreType.DMA((5,)),
         ],
         compiler_params=pltpu.CompilerParams(vmem_limit_bytes=LIMIT),
-        cost_estimate=work(8),
-        name="ring",
+        cost_estimate=work(3),
+        name="last",
     )(*(near(value) for value in inside))
 
 
@@ -644,16 +617,17 @@
 def shards(features, cell_index, tile_rows, spread, w_in, w_dens, w_one, w_two):
     sent = send_call(features, cell_index, tile_rows)
     received = lax.all_to_all(sent, ("lat", "lon"), split_axis=0, concat_axis=0, tiled=True)
-    grid, own_west, own_east, cols_a, cols_b, rows_a, rows_b = frame_call(received, spread, w_in, w_dens)
+    grid, west, east, rows_a, rows_b = frame_call(received, spread, w_in, w_dens)
     one, two = w_one.reshape(9, C, C), w_two.reshape(9, C, C)
-    cols_b = lax.ppermute(cols_b, "lon", swaps("lon", 1, True))
-    cols_a = lax.ppermute(cols_a, "lon", swaps("lon", 0, True))
-    hp, hcols = inner_one_call(grid, one)
-    rows_a, rows_b = corner_call(rows_a, rows_b, cols_a, cols_b)
     rows_b = lax.ppermute(rows_b, "lat", swaps("lat", 1, False))
     rows_a = lax.ppermute(rows_a, "lat", swaps("lat", 0, False))
+    hp, hcols = inner_one_call(grid, one)
     body = inner_two_call(hp, grid, two)
-    return ring_call(grid, rows_a, rows_b, cols_a, cols_b, own_west, own_east, hp, hcols, body, one, two)
+    sent_a, sent_b = column_call(rows_a, rows_b, west, east)
+    got_b = lax.ppermute(sent_b, "lon", swaps("lon", 1, True))
+    got_a = lax.ppermute(sent_a, "lon", swaps("lon", 0, True))
+    edge, ecols = edge_call(grid, rows_a, rows_b, hp, one, two)
+    return last_call(sent_a, sent_b, got_a, got_b, hcols, ecols, body, edge, one, two)
 
 
 def solution(mesh):

time: 84.6 us -> 81.2 us (0.960)
  waiting for transfers between devices: 2.81 us -> 1.4 us
  Pallas kernels: 23.9 us -> 22.5 us
    ppermute x1, waiting for transfers between devices: 2.7 us -> 0.21 us  [shards(): rows_b = lax.ppermute(rows_b, 'lat', swaps('lat', 1, False))]
    pallas_call x1, Pallas kernels: 13 us -> 11.4 us  [frame_call(): pl.pallas_call(frame_kernel, out_shape=(pltpu.VMEM((TH, NP, NQ, C), BF),...]
    ppermute x2, waiting for transfers between devices: 0.1 us -> 1.19 us  [the longest x1 1.18 us: shards(): got_b = lax.ppermute(sent_b, 'lon', swaps('lon', 1, True))]
    pallas_call x2 -> x3, Pallas kernels: 3.54 us -> 3.75 us  [the longest x1 2.03 us: edge_call(): pl.pallas_call(edge_kernel, out_shape=(pltpu.VMEM((4, TW, C), BF), pltpu....]
  transfers between devices with their start and end apart: 4 -> 4, of which waited for: 2 -> 2; matrix products, arithmetic and copies ran while one was open for 0% -> 0% of each run, Pallas kernels for 6% -> 9%
where the time goes in v6:
time: 81.2 us; the launch traced here: 81 us
  blocking collectives  51.5 us (63%)
  Pallas kernels  22.5 us (28%)
  starting transfers between devices  5.3 us (7%)
  waiting for transfers between devices  1.4 us (2%)
    all_to_all x1, blocking collectives, shards(): lax.all_to_all(sent, ('lat', 'lon'), split_axis=0, concat_axis=0, tiled=T...  51.5 us
    pallas_call x1, Pallas kernels, frame_call(): pl.pallas_call(frame_kernel, out_shape=(pltpu.VMEM((TH, NP, NQ, C), BF),...  11.4 us
    ppermute x1, starting transfers between devices, shards(): rows_b = lax.ppermute(rows_b, 'lat', swaps('lat', 1, False))  2.98 us
    pallas_call x1, Pallas kernels, inner_one_call(): pl.pallas_call(inner_one_kernel, out_shape=(pltpu.VMEM((TH + 2, NP + 2, N...  2.83 us
    pallas_call x1, Pallas kernels, inner_two_call(): pl.pallas_call(inner_two_kernel, out_shape=pltpu.VMEM((TH - 4, TW, C), BF...  2.52 us
    pallas_call x1, Pallas kernels, edge_call(): pl.pallas_call(edge_kernel, out_shape=(pltpu.VMEM((4, TW, C), BF), pltpu....  2.03 us
    pallas_call x1, Pallas kernels, send_call(): pl.pallas_call(send_kernel, out_shape=pltpu.VMEM((SOURCES, PAIRS, 2, F),...  1.95 us
    pallas_call x1, Pallas kernels, last_call(): pl.pallas_call(last_kernel, out_shape=jax.ShapeDtypeStruct((TH, TW, C), B...  1.67 us
  transfers between devices with their start and end apart: 4, of which 2 were waited for; matrix products, arithmetic and copies ran while one was open for 0% of the time, Pallas kernels for 9%

profile of v6, /device:TPU:8, one launch (start us, length us, event | category | flops | bytes accessed | tf_op | source)
XLA Modules:
  0.0 81.0 jit_solution(7669319045400476539)
XLA Ops:
  0.0 1.9 %send.1 = bf16[128,49,2,128]{3,2,1,0:T(2,128)(2,1)S(1)} custom-call(bf16[128,48,2,128]{3,2,1,0:T(2,128)(2,1)} %bitcast.15, s32[96,128]{1,0:T(8,128)} %bitcast.16, s32[1,128]{1,0:T(1,128)} %bitcast.17), custom_call_target="tpu_custom_call" | custom-call | tf_op jit(solution)/shard_map/send/pallas_call | solution.py:488
  2.0 0.0 copy-start.2
  2.0 0.0 copy-start.3
  2.0 0.0 copy-start.4
  2.0 51.5 %all_to_all.5.where_ref = bf16[128,49,2,128]{3,2,1,0:T(2,128)(2,1)S(1)} all-to-all(bf16[128,49,2,128]{3,2,1,0:T(2,128)(2,1)S(1)} %send.1), channel_id=1, replica_groups=mesh['lat'=16,'lon'=8] {'lat','lon'}, dimensions={0} | all-to-all | bytes 6422528 | tf_op jit(solution)/shard_map/all_to_all | solution.py:619
  53.5 0.0 copy-done.2
  53.5 0.0 copy-done.3
  53.5 0.0 copy-done.4
  53.5 0.0 copy-start
  53.5 11.4 %frame.1 = (bf16[24,6,16,256]{3,2,1,0:T(8,128)(2,1)S(1)}, bf16[2,24,256]{2,1,0:T(8,128)(2,1)S(1)}, bf16[2,24,256]{2,1,0:T(8,128)(2,1)S(1)}, bf16[192,256]{1,0:T(8,128)(2,1)S(1)}, bf16[192,256]{1,0:T(8,128)(2,1)S(1)}) custom-call(bf16[12544,128]{1,0:T(8,128)(2,1)S(1)} %bitcast.7, bf16[128,49,2,128]{3,2,1,0:T(2,128)(2,1)S(1)} %all_to_all.5.where_ref, ...), custom_call_target="tpu_custom_call" | custom-call | tf_op jit(solution)/shard_map/frame/pallas_call | solution.py:511
  64.9 0.8 %collective-permute-start = (bf16[192,256]{1,0:T(8,128)(2,1)S(1)}, bf16[192,256]{1,0:T(8,128)(2,1)S(1)}, u32[]{:S(2)}, u32[]{:S(2)}) collective-permute-start(bf16[192,256]{1,0:T(8,128)(2,1)S(1)} %get-tuple-element.16), channel_id=1, source_target_pairs={{0,8},{16,24},{32,40},{48,56},{64,72},{80,88},{96,104},{112,120},{... | collective-permute-start | bytes 294920 | tf_op jit(solution)/shard_map/ppermute | solution.py:623
  65.8 3.0 %collective-permute-start.1 = (bf16[192,256]{1,0:T(8,128)(2,1)S(1)}, bf16[192,256]{1,0:T(8,128)(2,1)S(1)}, u32[]{:S(2)}, u32[]{:S(2)}) collective-permute-start(bf16[192,256]{1,0:T(8,128)(2,1)S(1)} %get-tuple-element.17), channel_id=1, source_target_pairs={{8,16},{24,32},{40,48},{56,64},{72,80},{88,96},{104,112},{16,8},{3... | collective-permute-start | bytes 294920 | tf_op jit(solution)/shard_map/ppermute | solution.py:622
  68.8 0.0 copy-done
  68.8 0.0 copy-start.1
  68.8 2.8 %inner_one.1 = (bf16[26,8,16,256]{3,2,1,0:T(8,128)(2,1)S(1)}, f32[4,40,256]{2,1,0:T(8,128)S(1)}) custom-call(bf16[24,6,16,256]{3,2,1,0:T(8,128)(2,1)S(1)} %get-tuple-element.22.grid_ref, bf16[9,256,256]{2,1,0:T(8,128)(2,1)S(1)} %bitcast.8), custom_call_target="tpu_custom_call" | custom-call | flops 2491416576 | tf_op jit(solution)/shard_map/inner_one/pallas_call | solution.py:551
  71.6 2.5 %inner_two.1.body_ref = bf16[20,96,256]{2,1,0:T(8,128)(2,1)S(1)} custom-call(bf16[26,8,16,256]{3,2,1,0:T(8,128)(2,1)S(1)} %get-tuple-element.24.hp_ref, bf16[24,6,16,256]{3,2,1,0:T(8,128)(2,1)S(1)} %get-tuple-element.22.grid_ref, bf16[9,256,256]{2,1,0:T(8,128)(2,1)S(1)} %bitcast.11), custom_call_target="tpu_custom_call" | custom-call | flops 2264924160 | tf_op jit(solution)/shard_map/inner_two/pallas_call | solution.py:564
  74.2 0.0 collective-permute-done.rows_a_ref
  74.2 0.2 collective-permute-done.1.rows_b_ref
  74.4 0.1 collective-permute-start.2
  74.5 1.4 %collective-permute-start.3 = (bf16[2,32,256]{2,1,0:T(8,128)(2,1)S(1)}, bf16[2,32,256]{2,1,0:T(8,128)(2,1)S(1)}, u32[]{:S(2)}, u32[]{:S(2)}) collective-permute-start(bf16[2,32,256]{2,1,0:T(8,128)(2,1)S(1)} %get-tuple-element.21.sent_b_ref), channel_id=1, source_target_pairs={{1,2},{3,4},{5,6},{7,0},{2,1},{4,3},{6,5},{0,7},{9,10},{11,12},{13... | collective-permute-start | bytes 98312 | tf_op jit(solution)/shard_map/ppermute | solution.py:627
  75.9 2.0 %edge.1 = (bf16[4,96,256]{2,1,0:T(8,128)(2,1)S(1)}, f32[4,8,256]{2,1,0:T(8,128)S(1)}) custom-call(bf16[24,6,16,256]{3,2,1,0:T(8,128)(2,1)S(1)} %get-tuple-element.22.grid_ref, bf16[192,256]{1,0:T(8,128)(2,1)S(1)} %collective-permute-done.rows_a_ref, bf16[192,256]{1,0:T(8,128)(2,1)S(1)} %collective-permute-done.1.rows_b_ref, ...), custom_call_target="tpu_custom_call" | custom-call | flops 905969664 | tf_op jit(solution)/shard_map/edge/pallas_call | solution.py:577
  78.0 0.0 collective-permute-done.2.got_a_ref
  78.0 1.2 %collective-permute-done.3.got_b_ref = bf16[2,32,256]{2,1,0:T(8,128)(2,1)S(1)} collective-permute-done((bf16[2,32,256]{2,1,0:T(8,128)(2,1)S(1)}, bf16[2,32,256]{2,1,0:T(8,128)(2,1)S(1)}, u32[]{:S(2)}, u32[]{:S(2)}) %collective-permute-start.3) | collective-permute-done | bytes 32800 | tf_op jit(solution)/shard_map/ppermute | solution.py:627
  79.2 1.7 %last.1 = bf16[24,96,256]{2,1,0:T(8,128)(2,1)} custom-call(bf16[2,32,256]{2,1,0:T(8,128)(2,1)S(1)} %get-tuple-element.20.sent_a_ref, bf16[2,32,256]{2,1,0:T(8,128)(2,1)S(1)} %get-tuple-element.21.sent_b_ref, bf16[2,32,256]{2,1,0:T(8,128)(2,1)S(1)} %collective-permute-done.2.got_a_ref, bf16[2,32,256]{2,1,0:T(8,128)(2,1)S(1)} %collective-permute-done.3.got_b_ref, ...), custom_call_target="tpu_custom_call" | custom-call | flops 339738624 | tf_op jit(solution)/shard_map/last/pallas_call | solution.py:594
  (2 shorter events, 0.0 us)
Async XLA Ops:
  2.0 51.5 %copy-start.2 = (bf16[128,256]{1,0:T(8,128)(2,1)S(1)}, bf16[128,256]{1,0:T(8,128)(2,1)}, u32[]{:S(2)}) copy-start(bf16[128,256]{1,0:T(8,128)(2,1)} %win_ref.1) | copy-start | bytes 196612
  2.0 51.5 %copy-start.3 = (f32[3,3]{1,0:T(4,128)S(1)}, f32[3,3]{1,0:T(4,128)}, u32[]{:S(2)}) copy-start(f32[3,3]{1,0:T(4,128)} %spread_ref.1) | copy-start | bytes 112
  2.0 51.5 %copy-start.4 = (f32[256]{0:T(256)S(1)}, f32[256]{0:T(256)}, u32[]{:S(2)}) copy-start(f32[256]{0:T(256)} %param.13) | copy-start | bytes 3076
  53.5 15.3 %copy-start = (bf16[3,3,256,256]{3,2,1,0:T(8,128)(2,1)S(1)}, bf16[3,3,256,256]{3,2,1,0:T(8,128)(2,1)}, u32[]{:S(2)}) copy-start(bf16[3,3,256,256]{3,2,1,0:T(8,128)(2,1)} %param.14) | copy-start | bytes 3538948
  64.9 9.2 %collective-permute-start = (bf16[192,256]{1,0:T(8,128)(2,1)S(1)}, bf16[192,256]{1,0:T(8,128)(2,1)S(1)}, u32[]{:S(2)}, u32[]{:S(2)}) collective-permute-start(bf16[192,256]{1,0:T(8,128)(2,1)S(1)} %get-tuple-element.16), channel_id=1, source_target_pairs={{0,8},{16,24},{32,40},{48,56},{64,72},{80,88},{96,104},{112,120},{... | collective-permute-start | bytes 294920 | tf_op jit(solution)/shard_map/ppermute | solution.py:623
  65.8 8.6 %collective-permute-start.1 = (bf16[192,256]{1,0:T(8,128)(2,1)S(1)}, bf16[192,256]{1,0:T(8,128)(2,1)S(1)}, u32[]{:S(2)}, u32[]{:S(2)}) collective-permute-start(bf16[192,256]{1,0:T(8,128)(2,1)S(1)} %get-tuple-element.17), channel_id=1, source_target_pairs={{8,16},{24,32},{40,48},{56,64},{72,80},{88,96},{104,112},{16,8},{3... | collective-permute-start | bytes 294920 | tf_op jit(solution)/shard_map/ppermute | solution.py:622
  68.8 2.9 %copy-start.1 = (bf16[3,3,256,256]{3,2,1,0:T(8,128)(2,1)S(1)}, bf16[3,3,256,256]{3,2,1,0:T(8,128)(2,1)}, u32[]{:S(2)}) copy-start(bf16[3,3,256,256]{3,2,1,0:T(8,128)(2,1)} %param.15) | copy-start | bytes 3538948
  74.4 3.5 %collective-permute-start.2 = (bf16[2,32,256]{2,1,0:T(8,128)(2,1)S(1)}, bf16[2,32,256]{2,1,0:T(8,128)(2,1)S(1)}, u32[]{:S(2)}, u32[]{:S(2)}) collective-permute-start(bf16[2,32,256]{2,1,0:T(8,128)(2,1)S(1)} %get-tuple-element.20.sent_a_ref), channel_id=1, source_target_pairs={{0,1},{2,3},{4,5},{6,7},{1,0},{3,2},{5,4},{7,6},{8,9},{10,11},{12,... | collective-permute-start | bytes 98312 | tf_op jit(solution)/shard_map/ppermute | solution.py:628
  74.5 4.6 %collective-permute-start.3 = (bf16[2,32,256]{2,1,0:T(8,128)(2,1)S(1)}, bf16[2,32,256]{2,1,0:T(8,128)(2,1)S(1)}, u32[]{:S(2)}, u32[]{:S(2)}) collective-permute-start(bf16[2,32,256]{2,1,0:T(8,128)(2,1)S(1)} %get-tuple-element.21.sent_b_ref), channel_id=1, source_target_pairs={{1,2},{3,4},{5,6},{7,0},{2,1},{4,3},{6,5},{0,7},{9,10},{11,12},{13... | collective-permute-start | bytes 98312 | tf_op jit(solution)/shard_map/ppermute | solution.py:627

commit v7 on v6

--- a/solution.py
+++ b/solution.py
@@ -24,6 +24,7 @@
 MAIN = HALF * TW
 LHS = MAIN + 32
 GROUPS = 7
+CUT = 10
 PER = ROWS // GROUPS
 BF = jnp.bfloat16
 F32 = jnp.float32
@@ -248,19 +249,11 @@
 
     lat_odd, _ = parities()
     rows = [grid_ref[at : at + 2].reshape(2 * TW, C) for at in (TH - 2, 0)]
-    give(lat_odd, rows_a_ref, rows_b_ref, *rows)
-
-
-def give(odd, a_ref, b_ref, after, before):
-    @pl.when(odd == 0)
-    def _():
-        a_ref[...] = after
-        b_ref[...] = before
-
-    @pl.when(odd != 0)
-    def _():
-        a_ref[...] = before
-        b_ref[...] = after
+    rows_a_ref[...], rows_b_ref[...] = chosen(lat_odd, *rows)
+
+
+def chosen(odd, a, b):
+    return jnp.where(odd == 0, a, b), jnp.where(odd == 0, b, a)
 
 
 def silu(v):
@@ -282,7 +275,9 @@
 
     pl.when(lat_odd == 0)(lambda: halo(rows_b_ref, rows_a_ref))
     pl.when(lat_odd != 0)(lambda: halo(rows_a_ref, rows_b_ref))
-    give(lon_odd, a_ref, b_ref, tall[2:4].astype(BF), tall[0:2].astype(BF))
+    after, before = chosen(lon_odd, tall[2:4], tall[0:2])
+    a_ref[...] = after.astype(BF)
+    b_ref[...] = before.astype(BF)
 
 
 def nine(weight, window):
@@ -327,12 +322,12 @@
         start += count
 
 
-def inner_two_kernel(hp_ref, grid_ref, two_ref, body_ref, flat):
+def inner_two_kernel(begin, end, hp_ref, grid_ref, two_ref, body_ref, flat):
     step = 4
-    for i in range(2, TH - 2, step):
+    for i in range(begin, end, step):
         value = rows_of(hp_ref, two_ref, i, step).reshape(step, NP, NQ, C)
         value = value + grid_ref[i : i + step].astype(F32)
-        at = i - 2
+        at = i - begin
         for k in range(step):
             spread_out(flat, at + k, value[k])
         for h in range(2):
@@ -346,24 +341,35 @@
 
 
 def edge_kernel(
-    grid_ref, rows_a_ref, rows_b_ref, hp_ref, one_ref, two_ref, out_ref, ecols_ref, north_ref, south_ref, gp, hr, flat
+    grid_ref,
+    rows_a_ref,
+    rows_b_ref,
+    hp_ref,
+    body_ref,
+    rest_ref,
+    one_ref,
+    two_ref,
+    out_ref,
+    ecols_ref,
+    partial_ref,
+    gp,
+    hr,
+    flat,
+    sems,
 ):
+    copies = [
+        pltpu.make_async_copy(body_ref, partial_ref.at[2:CUT], sems.at[0]),
+        pltpu.make_async_copy(rest_ref, partial_ref.at[CUT : TH - 2], sems.at[1]),
+    ]
+    for copy in copies:
+        copy.start()
     keep_top, keep_bottom = keeps()
     lat_odd, _ = parities()
 
-    @pl.when(lat_odd == 0)
-    def _():
-        south_ref[...] = rows_a_ref[...]
-        north_ref[...] = rows_b_ref[...]
-
-    @pl.when(lat_odd != 0)
-    def _():
-        south_ref[...] = rows_b_ref[...]
-        north_ref[...] = rows_a_ref[...]
-
-    tiles = [north_ref[k * TW : (k + 1) * TW, :].reshape(NP, NQ, C) for k in range(2)]
+    south, north = chosen(lat_odd, rows_a_ref[...], rows_b_ref[...])
+    tiles = [north[k * TW : (k + 1) * TW, :].reshape(NP, NQ, C) for k in range(2)]
     tiles += [grid_ref[g] for g in (0, 1, TH - 2, TH - 1)]
-    tiles += [south_ref[k * TW : (k + 1) * TW, :].reshape(NP, NQ, C) for k in range(2)]
+    tiles += [south[k * TW : (k + 1) * TW, :].reshape(NP, NQ, C) for k in range(2)]
     for slot, tile in enumerate(tiles):
         first, last = tile[0].astype(F32), tile[NP - 1].astype(F32)
         padded(gp, slot, tile, first, last, first[:1], last[NQ - 1 :])
@@ -391,6 +397,8 @@
         spread_out(flat, n, value[n * TW : (n + 1) * TW].reshape(NP, NQ, C) + grid_ref[i].astype(F32))
     for h in range(2):
         out_ref[:, :, 128 * h : 128 * (h + 1)] = flat[h].astype(BF).reshape(4, TW, 128)
+    for copy in copies:
+        copy.wait()
 
 
 def last_kernel(
@@ -401,9 +409,11 @@
     hcols_ref,
     ecols_ref,
     body_ref,
+    rest_ref,
     edge_ref,
     one_ref,
     two_ref,
+    partial_ref,
     out_ref,
     cs,
     hc,
@@ -413,7 +423,6 @@
 ):
     middle = slice(8, TW - 8)
     copies = [
-        pltpu.make_async_copy(body_ref.at[:, middle], out_ref.at[2 : TH - 2, middle], sems.at[0]),
         pltpu.make_async_copy(edge_ref.at[:2, middle], out_ref.at[:2, middle], sems.at[1]),
         pltpu.make_async_copy(edge_ref.at[2:, middle], out_ref.at[TH - 2 :, middle], sems.at[2]),
     ]
@@ -424,12 +433,10 @@
     cs[:, 32:, :] = jnp.zeros((8, 8, C), F32)
     hc[:, 32:, :] = jnp.zeros((8, 8, C), F32)
 
-    def fill(got_before, sent_before, sent_after, got_after):
-        for n, ref in enumerate((got_before, sent_before, sent_after, got_after)):
-            cs[2 * n : 2 * n + 2, 0:32, :] = ref[...].astype(F32)
-
-    pl.when(lon_odd == 0)(lambda: fill(got_b_ref, sent_b_ref, sent_a_ref, got_a_ref))
-    pl.when(lon_odd != 0)(lambda: fill(got_a_ref, sent_a_ref, sent_b_ref, got_b_ref))
+    got_after, got_before = chosen(lon_odd, got_a_ref[...].astype(F32), got_b_ref[...].astype(F32))
+    sent_after, sent_before = chosen(lon_odd, sent_a_ref[...].astype(F32), sent_b_ref[...].astype(F32))
+    for n, value in enumerate((got_before, sent_before, sent_after, got_after)):
+        cs[2 * n : 2 * n + 2, 0:32, :] = value
 
     def window(src, a, b):
         return jnp.concatenate([src[c + b, a : a + 32, :].astype(BF) for c in (0, 1, 4, 5)], axis=0)
@@ -449,8 +456,10 @@
         oc[c] = value[32 * c : 32 * c + TH] + cs[2 + c, 2 : 2 + TH, :]
     place = iota((8, C), 0)
     for i in range(TH):
-        if 2 <= i < TH - 2:
+        if 2 <= i < CUT:
             rows, at = body_ref, i - 2
+        elif CUT <= i < TH - 2:
+            rows, at = rest_ref, i - CUT
         else:
             rows, at = edge_ref, i if i < 2 else i - TH + 4
         left, right = rows[at, :8].astype(F32), rows[at, TW - 8 :].astype(F32)
@@ -560,29 +569,28 @@
     )(near(grid), near(one))
 
 
-def inner_two_call(hp, grid, two):
+def inner_two_call(begin, end, hp, grid, two):
     return pl.pallas_call(
-        inner_two_kernel,
-        out_shape=pltpu.VMEM((TH - 4, TW, C), BF),
+        functools.partial(inner_two_kernel, begin, end),
+        out_shape=pltpu.VMEM((end - begin, TW, C), BF),
         in_specs=vmem(3),
         out_specs=vmem(1)[0],
-        scratch_shapes=[pltpu.VMEM((2, (TH - 4) * TW, 128), F32)],
+        scratch_shapes=[pltpu.VMEM((2, (end - begin) * TW, 128), F32)],
         compiler_params=pltpu.CompilerParams(vmem_limit_bytes=LIMIT),
-        cost_estimate=work(TH - 4),
-        name="inner_two",
+        cost_estimate=work(end - begin),
     )(near(hp), near(grid), near(two))
 
 
 def edge_call(*inside):
     return pl.pallas_call(
         edge_kernel,
-        out_shape=(pltpu.VMEM((4, TW, C), BF), pltpu.VMEM((4, 8, C), F32)),
-        in_specs=vmem(6),
-        out_specs=tuple(vmem(2)),
+        out_shape=(pltpu.VMEM((4, TW, C), BF), pltpu.VMEM((4, 8, C), F32), pltpu.HBM((TH, TW, C), BF)),
+        in_specs=vmem(8),
+        out_specs=(*vmem(2), *far(1)),
         scratch_shapes=[
-            *(pltpu.VMEM((2 * TW, C), BF),) * 2,
             *(pltpu.VMEM((8, NP + 2, NQ, C), BF),) * 2,
             pltpu.VMEM((2, 4 * TW, 128), F32),
+            pltpu.SemaphoreType.DMA((2,)),
         ],
         compiler_params=pltpu.CompilerParams(vmem_limit_bytes=LIMIT),
         cost_estimate=work(8),
@@ -590,22 +598,23 @@
     )(*(near(value) for value in inside))
 
 
-def last_call(*inside):
+def last_call(partial, *inside):
     return pl.pallas_call(
         last_kernel,
         out_shape=jax.ShapeDtypeStruct((TH, TW, C), BF),
-        in_specs=vmem(10),
+        in_specs=[*vmem(11), *far(1)],
         out_specs=far(1)[0],
         scratch_shapes=[
             *(pltpu.VMEM((8, 40, C), F32),) * 2,
             pltpu.VMEM((4, TH, C), F32),
             pltpu.VMEM((2, TH, 8, C), BF),
-            pltpu.SemaphoreType.DMA((5,)),
+            pltpu.SemaphoreType.DMA((6,)),
         ],
+        input_output_aliases={11: 0},
         compiler_params=pltpu.CompilerParams(vmem_limit_bytes=LIMIT),
         cost_estimate=work(3),
         name="last",
-    )(*(near(value) for value in inside))
+    )(*(near(value) for value in inside), partial)
 
 
 def swaps(axis, first, around):
@@ -622,12 +631,13 @@
     rows_b = lax.ppermute(rows_b, "lat", swaps("lat", 1, False))
     rows_a = lax.ppermute(rows_a, "lat", swaps("lat", 0, False))
     hp, hcols = inner_one_call(grid, one)
-    body = inner_two_call(hp, grid, two)
+    body = inner_two_call(2, CUT, hp, grid, two)
     sent_a, sent_b = column_call(rows_a, rows_b, west, east)
     got_b = lax.ppermute(sent_b, "lon", swaps("lon", 1, True))
     got_a = lax.ppermute(sent_a, "lon", swaps("lon", 0, True))
-    edge, ecols = edge_call(grid, rows_a, rows_b, hp, one, two)
-    return last_call(sent_a, sent_b, got_a, got_b, hcols, ecols, body, edge, one, two)
+    rest = inner_two_call(CUT, TH - 2, hp, grid, two)
+    edge, ecols, partial = edge_call(grid, rows_a, rows_b, hp, body, rest, one, two)
+    return last_call(partial, sent_a, sent_b, got_a, got_b, hcols, ecols, body, rest, edge, one, two)
 
 
 def solution(mesh):

time: 81.2 us -> 81.3 us (level)
    pallas_call x1 -> x2, Pallas kernels: 2.52 us -> 2.68 us  [inner_two_call(): pl.pallas_call(functools.partial(inner_two_kernel, begin, end), out_shape...]
  transfers between devices with their start and end apart: 4 -> 4, of which waited for: 2 -> 1; matrix products, arithmetic and copies ran while one was open for 0% -> 0% of each run, Pallas kernels for 9% -> 9%
where the time goes in v7:
time: 81.3 us; the launch traced here: 80.9 us
  blocking collectives  51.5 us (63%)
  Pallas kernels  22.6 us (28%)
  starting transfers between devices  5.46 us (7%)
  waiting for transfers between devices  1.05 us (1%)
    all_to_all x1, blocking collectives, shards(): lax.all_to_all(sent, ('lat', 'lon'), split_axis=0, concat_axis=0, tiled=T...  51.5 us
    pallas_call x1, Pallas kernels, frame_call(): pl.pallas_call(frame_kernel, out_shape=(pltpu.VMEM((TH, NP, NQ, C), BF),...  11.4 us
    ppermute x1, starting transfers between devices, shards(): rows_b = lax.ppermute(rows_b, 'lat', swaps('lat', 1, False))  2.98 us
    pallas_call x1, Pallas kernels, inner_one_call(): pl.pallas_call(inner_one_kernel, out_shape=(pltpu.VMEM((TH + 2, NP + 2, N...  2.83 us
    pallas_call x2, Pallas kernels, inner_two_call(): pl.pallas_call(functools.partial(inner_two_kernel, begin, end), out_shape...  2.68 us
    pallas_call x1, Pallas kernels, edge_call(): pl.pallas_call(edge_kernel, out_shape=(pltpu.VMEM((4, TW, C), BF), pltpu....  2.05 us
    pallas_call x1, Pallas kernels, send_call(): pl.pallas_call(send_kernel, out_shape=pltpu.VMEM((SOURCES, PAIRS, 2, F),...  1.95 us
    pallas_call x1, Pallas kernels, last_call(): pl.pallas_call(last_kernel, out_shape=jax.ShapeDtypeStruct((TH, TW, C), B...  1.64 us
  transfers between devices with their start and end apart: 4, of which 1 were waited for; matrix products, arithmetic and copies ran while one was open for 0% of the time, Pallas kernels for 9%

profile of v7, /device:TPU:8, one launch (start us, length us, event | category | flops | bytes accessed | tf_op | source)
XLA Modules:
  0.0 80.9 jit_solution(15486156378548797012)
XLA Ops:
  0.0 1.9 %send.1 = bf16[128,49,2,128]{3,2,1,0:T(2,128)(2,1)S(1)} custom-call(bf16[128,48,2,128]{3,2,1,0:T(2,128)(2,1)} %bitcast.16, s32[96,128]{1,0:T(8,128)} %bitcast.17, s32[1,128]{1,0:T(1,128)} %bitcast.18), custom_call_target="tpu_custom_call" | custom-call | tf_op jit(solution)/shard_map/send/pallas_call | solution.py:497
  2.0 0.0 copy-start.2
  2.0 0.0 copy-start.3
  2.0 0.0 copy-start.4
  2.0 51.5 %all_to_all.5.where_ref = bf16[128,49,2,128]{3,2,1,0:T(2,128)(2,1)S(1)} all-to-all(bf16[128,49,2,128]{3,2,1,0:T(2,128)(2,1)S(1)} %send.1), channel_id=1, replica_groups=mesh['lat'=16,'lon'=8] {'lat','lon'}, dimensions={0} | all-to-all | bytes 6422528 | tf_op jit(solution)/shard_map/all_to_all | solution.py:628
  53.5 0.0 copy-done.2
  53.5 0.0 copy-done.3
  53.5 0.0 copy-done.4
  53.5 0.0 copy-start.1
  53.5 11.4 %frame.1 = (bf16[24,6,16,256]{3,2,1,0:T(8,128)(2,1)S(1)}, bf16[2,24,256]{2,1,0:T(8,128)(2,1)S(1)}, bf16[2,24,256]{2,1,0:T(8,128)(2,1)S(1)}, bf16[192,256]{1,0:T(8,128)(2,1)S(1)}, bf16[192,256]{1,0:T(8,128)(2,1)S(1)}) custom-call(bf16[12544,128]{1,0:T(8,128)(2,1)S(1)} %bitcast.7, bf16[128,49,2,128]{3,2,1,0:T(2,128)(2,1)S(1)} %all_to_all.5.where_ref, ...), custom_call_target="tpu_custom_call" | custom-call | tf_op jit(solution)/shard_map/frame/pallas_call | solution.py:520
  64.9 0.8 %collective-permute-start = (bf16[192,256]{1,0:T(8,128)(2,1)S(1)}, bf16[192,256]{1,0:T(8,128)(2,1)S(1)}, u32[]{:S(2)}, u32[]{:S(2)}) collective-permute-start(bf16[192,256]{1,0:T(8,128)(2,1)S(1)} %get-tuple-element.17), channel_id=1, source_target_pairs={{0,8},{16,24},{32,40},{48,56},{64,72},{80,88},{96,104},{112,120},{... | collective-permute-start | bytes 294920 | tf_op jit(solution)/shard_map/ppermute | solution.py:632
  65.7 3.0 %collective-permute-start.1 = (bf16[192,256]{1,0:T(8,128)(2,1)S(1)}, bf16[192,256]{1,0:T(8,128)(2,1)S(1)}, u32[]{:S(2)}, u32[]{:S(2)}) collective-permute-start(bf16[192,256]{1,0:T(8,128)(2,1)S(1)} %get-tuple-element.18), channel_id=1, source_target_pairs={{8,16},{24,32},{40,48},{56,64},{72,80},{88,96},{104,112},{16,8},{3... | collective-permute-start | bytes 294920 | tf_op jit(solution)/shard_map/ppermute | solution.py:631
  68.7 0.0 copy-start
  68.8 2.8 %inner_one.1 = (bf16[26,8,16,256]{3,2,1,0:T(8,128)(2,1)S(1)}, f32[4,40,256]{2,1,0:T(8,128)S(1)}) custom-call(bf16[24,6,16,256]{3,2,1,0:T(8,128)(2,1)S(1)} %get-tuple-element.23.grid_ref, bf16[9,256,256]{2,1,0:T(8,128)(2,1)S(1)} %bitcast.12), custom_call_target="tpu_custom_call" | custom-call | flops 2491416576 | tf_op jit(solution)/shard_map/inner_one/pallas_call | solution.py:560
  71.6 1.6 %shard_map.83.rest_ref = bf16[12,96,256]{2,1,0:T(8,128)(2,1)S(1)} custom-call(bf16[26,8,16,256]{3,2,1,0:T(8,128)(2,1)S(1)} %get-tuple-element.25.hp_ref, bf16[24,6,16,256]{3,2,1,0:T(8,128)(2,1)S(1)} %get-tuple-element.23.grid_ref, bf16[9,256,256]{2,1,0:T(8,128)(2,1)S(1)} %bitcast.8), custom_call_target="tpu_custom_call" | custom-call | flops 1358954496 | tf_op jit(solution)/shard_map/pallas_call | solution.py:573
  73.2 1.1 %shard_map.82.body_ref = bf16[8,96,256]{2,1,0:T(8,128)(2,1)S(1)} custom-call(bf16[26,8,16,256]{3,2,1,0:T(8,128)(2,1)S(1)} %get-tuple-element.25.hp_ref, bf16[24,6,16,256]{3,2,1,0:T(8,128)(2,1)S(1)} %get-tuple-element.23.grid_ref, bf16[9,256,256]{2,1,0:T(8,128)(2,1)S(1)} %bitcast.9), custom_call_target="tpu_custom_call" | custom-call | flops 905969664 | tf_op jit(solution)/shard_map/pallas_call | solution.py:573
  74.3 0.0 collective-permute-done.rows_a_ref
  74.3 0.0 collective-permute-done.1.rows_b_ref
  74.4 0.1 collective-permute-start.2
  74.5 1.6 %collective-permute-start.3 = (bf16[2,32,256]{2,1,0:T(8,128)(2,1)S(1)}, bf16[2,32,256]{2,1,0:T(8,128)(2,1)S(1)}, u32[]{:S(2)}, u32[]{:S(2)}) collective-permute-start(bf16[2,32,256]{2,1,0:T(8,128)(2,1)S(1)} %get-tuple-element.22.sent_b_ref), channel_id=1, source_target_pairs={{1,2},{3,4},{5,6},{7,0},{2,1},{4,3},{6,5},{0,7},{9,10},{11,12},{13... | collective-permute-start | bytes 98312 | tf_op jit(solution)/shard_map/ppermute | solution.py:636
  76.1 2.0 %edge.1 = (bf16[4,96,256]{2,1,0:T(8,128)(2,1)S(1)}, f32[4,8,256]{2,1,0:T(8,128)S(1)}, bf16[24,96,256]{2,1,0:T(8,128)(2,1)}) custom-call(bf16[24,6,16,256]{3,2,1,0:T(8,128)(2,1)S(1)} %get-tuple-element.23.grid_ref, bf16[192,256]{1,0:T(8,128)(2,1)S(1)} %collective-permute-done.rows_a_ref, bf16[192,256]{1,0:T(8,128)(2,1)S(1)} %collective-permute-done.1.rows_b_ref, ...), custom_call_target="tpu_custom_call" | custom-call | flops 905969664 | tf_op jit(solution)/shard_map/edge/pallas_call | solution.py:585
  78.1 0.0 collective-permute-done.2.got_a_ref
  78.1 1.0 %collective-permute-done.3.got_b_ref = bf16[2,32,256]{2,1,0:T(8,128)(2,1)S(1)} collective-permute-done((bf16[2,32,256]{2,1,0:T(8,128)(2,1)S(1)}, bf16[2,32,256]{2,1,0:T(8,128)(2,1)S(1)}, u32[]{:S(2)}, u32[]{:S(2)}) %collective-permute-start.3) | collective-permute-done | bytes 32800 | tf_op jit(solution)/shard_map/ppermute | solution.py:636
  79.1 1.6 %last.1 = bf16[24,96,256]{2,1,0:T(8,128)(2,1)} custom-call(bf16[2,32,256]{2,1,0:T(8,128)(2,1)S(1)} %get-tuple-element.21.sent_a_ref, bf16[2,32,256]{2,1,0:T(8,128)(2,1)S(1)} %get-tuple-element.22.sent_b_ref, bf16[2,32,256]{2,1,0:T(8,128)(2,1)S(1)} %collective-permute-done.2.got_a_ref, ...), custom_call_target="tpu_custom_call", output_to_operand_aliasing={{}: (11, {})} | custom-call | flops 339738624 | tf_op jit(solution)/shard_map/last/pallas_call | solution.py:602
  (3 shorter events, 0.0 us)
Async XLA Ops:
  2.0 51.5 %copy-start.2 = (bf16[128,256]{1,0:T(8,128)(2,1)S(1)}, bf16[128,256]{1,0:T(8,128)(2,1)}, u32[]{:S(2)}) copy-start(bf16[128,256]{1,0:T(8,128)(2,1)} %win_ref.1) | copy-start | bytes 196612
  2.0 51.5 %copy-start.3 = (f32[3,3]{1,0:T(4,128)S(1)}, f32[3,3]{1,0:T(4,128)}, u32[]{:S(2)}) copy-start(f32[3,3]{1,0:T(4,128)} %spread_ref.1) | copy-start | bytes 112
  2.0 51.5 %copy-start.4 = (f32[256]{0:T(256)S(1)}, f32[256]{0:T(256)}, u32[]{:S(2)}) copy-start(f32[256]{0:T(256)} %param.13) | copy-start | bytes 3076
  53.5 15.2 %copy-start.1 = (bf16[3,3,256,256]{3,2,1,0:T(8,128)(2,1)S(1)}, bf16[3,3,256,256]{3,2,1,0:T(8,128)(2,1)}, u32[]{:S(2)}) copy-start(bf16[3,3,256,256]{3,2,1,0:T(8,128)(2,1)} %param.14) | copy-start | bytes 3538948
  64.9 9.4 %collective-permute-start = (bf16[192,256]{1,0:T(8,128)(2,1)S(1)}, bf16[192,256]{1,0:T(8,128)(2,1)S(1)}, u32[]{:S(2)}, u32[]{:S(2)}) collective-permute-start(bf16[192,256]{1,0:T(8,128)(2,1)S(1)} %get-tuple-element.17), channel_id=1, source_target_pairs={{0,8},{16,24},{32,40},{48,56},{64,72},{80,88},{96,104},{112,120},{... | collective-permute-start | bytes 294920 | tf_op jit(solution)/shard_map/ppermute | solution.py:632
  65.7 8.6 %collective-permute-start.1 = (bf16[192,256]{1,0:T(8,128)(2,1)S(1)}, bf16[192,256]{1,0:T(8,128)(2,1)S(1)}, u32[]{:S(2)}, u32[]{:S(2)}) collective-permute-start(bf16[192,256]{1,0:T(8,128)(2,1)S(1)} %get-tuple-element.18), channel_id=1, source_target_pairs={{8,16},{24,32},{40,48},{56,64},{72,80},{88,96},{104,112},{16,8},{3... | collective-permute-start | bytes 294920 | tf_op jit(solution)/shard_map/ppermute | solution.py:631
  68.7 2.9 %copy-start = (bf16[3,3,256,256]{3,2,1,0:T(8,128)(2,1)S(1)}, bf16[3,3,256,256]{3,2,1,0:T(8,128)(2,1)}, u32[]{:S(2)}) copy-start(bf16[3,3,256,256]{3,2,1,0:T(8,128)(2,1)} %param.15) | copy-start | bytes 3538948
  74.4 3.7 %collective-permute-start.2 = (bf16[2,32,256]{2,1,0:T(8,128)(2,1)S(1)}, bf16[2,32,256]{2,1,0:T(8,128)(2,1)S(1)}, u32[]{:S(2)}, u32[]{:S(2)}) collective-permute-start(bf16[2,32,256]{2,1,0:T(8,128)(2,1)S(1)} %get-tuple-element.21.sent_a_ref), channel_id=1, source_target_pairs={{0,1},{2,3},{4,5},{6,7},{1,0},{3,2},{5,4},{7,6},{8,9},{10,11},{12,... | collective-permute-start | bytes 98312 | tf_op jit(solution)/shard_map/ppermute | solution.py:637
  74.5 4.6 %collective-permute-start.3 = (bf16[2,32,256]{2,1,0:T(8,128)(2,1)S(1)}, bf16[2,32,256]{2,1,0:T(8,128)(2,1)S(1)}, u32[]{:S(2)}, u32[]{:S(2)}) collective-permute-start(bf16[2,32,256]{2,1,0:T(8,128)(2,1)S(1)} %get-tuple-element.22.sent_b_ref), channel_id=1, source_target_pairs={{1,2},{3,4},{5,6},{7,0},{2,1},{4,3},{6,5},{0,7},{9,10},{11,12},{13... | collective-permute-start | bytes 98312 | tf_op jit(solution)/shard_map/ppermute | solution.py:636

commit v8 on v7

--- a/solution.py
+++ b/solution.py
@@ -455,19 +455,18 @@
     for c in range(4):
         oc[c] = value[32 * c : 32 * c + TH] + cs[2 + c, 2 : 2 + TH, :]
     place = iota((8, C), 0)
-    for i in range(TH):
-        if 2 <= i < CUT:
-            rows, at = body_ref, i - 2
-        elif CUT <= i < TH - 2:
-            rows, at = rest_ref, i - CUT
-        else:
-            rows, at = edge_ref, i if i < 2 else i - TH + 4
-        left, right = rows[at, :8].astype(F32), rows[at, TW - 8 :].astype(F32)
-        left = jnp.where(place == 0, oc[0, i : i + 1, :], jnp.where(place == 1, oc[1, i : i + 1, :], left))
-        right = jnp.where(place == 6, oc[2, i : i + 1, :], jnp.where(place == 7, oc[3, i : i + 1, :], right))
-        strips[0, i] = left.astype(BF)
-        strips[1, i] = right.astype(BF)
-    for n, at in enumerate((0, TW - 8)):
+    for n, (at, first) in enumerate(((0, 0), (TW - 8, 6))):
+        for i in range(TH):
+            if 2 <= i < CUT:
+                rows, line = body_ref, i - 2
+            elif CUT <= i < TH - 2:
+                rows, line = rest_ref, i - CUT
+            else:
+                rows, line = edge_ref, i if i < 2 else i - TH + 4
+            strip = rows[line, at : at + 8].astype(F32)
+            for k in range(2):
+                strip = jnp.where(place == first + k, oc[2 * n + k, i : i + 1, :], strip)
+            strips[n, i] = strip.astype(BF)
         copies.append(pltpu.make_async_copy(strips.at[n], out_ref.at[:, at : at + 8], sems.at[3 + n]))
         copies[-1].start()
     for copy in copies:

time: 81.3 us -> 81.3 us (level)
  no operation moved by 1% of the time
where the time goes in v8:
time: 81.3 us; the launch traced here: 80.9 us
  blocking collectives  51.5 us (63%)
  Pallas kernels  22.6 us (28%)
  starting transfers between devices  5.46 us (7%)
  waiting for transfers between devices  1.05 us (1%)
    all_to_all x1, blocking collectives, shards(): lax.all_to_all(sent, ('lat', 'lon'), split_axis=0, concat_axis=0, tiled=T...  51.5 us
    pallas_call x1, Pallas kernels, frame_call(): pl.pallas_call(frame_kernel, out_shape=(pltpu.VMEM((TH, NP, NQ, C), BF),...  11.4 us
    ppermute x1, starting transfers between devices, shards(): rows_b = lax.ppermute(rows_b, 'lat', swaps('lat', 1, False))  2.98 us
    pallas_call x1, Pallas kernels, inner_one_call(): pl.pallas_call(inner_one_kernel, out_shape=(pltpu.VMEM((TH + 2, NP + 2, N...  2.83 us
    pallas_call x2, Pallas kernels, inner_two_call(): pl.pallas_call(functools.partial(inner_two_kernel, begin, end), out_shape...  2.68 us
    pallas_call x1, Pallas kernels, edge_call(): pl.pallas_call(edge_kernel, out_shape=(pltpu.VMEM((4, TW, C), BF), pltpu....  2.05 us
    pallas_call x1, Pallas kernels, send_call(): pl.pallas_call(send_kernel, out_shape=pltpu.VMEM((SOURCES, PAIRS, 2, F),...  1.95 us
    pallas_call x1, Pallas kernels, last_call(): pl.pallas_call(last_kernel, out_shape=jax.ShapeDtypeStruct((TH, TW, C), B...  1.63 us
  transfers between devices with their start and end apart: 4, of which 1 were waited for; matrix products, arithmetic and copies ran while one was open for 0% of the time, Pallas kernels for 9%

profile of v8, /device:TPU:8, one launch (start us, length us, event | category | flops | bytes accessed | tf_op | source)
XLA Modules:
  0.0 80.9 jit_solution(14428317966376408807)
XLA Ops:
  0.0 1.9 %send.1 = bf16[128,49,2,128]{3,2,1,0:T(2,128)(2,1)S(1)} custom-call(bf16[128,48,2,128]{3,2,1,0:T(2,128)(2,1)} %bitcast.16, s32[96,128]{1,0:T(8,128)} %bitcast.17, s32[1,128]{1,0:T(1,128)} %bitcast.18), custom_call_target="tpu_custom_call" | custom-call | tf_op jit(solution)/shard_map/send/pallas_call | solution.py:496
  2.0 0.0 copy-start.2
  2.0 0.0 copy-start.3
  2.0 0.0 copy-start.4
  2.0 51.5 %all_to_all.5.where_ref = bf16[128,49,2,128]{3,2,1,0:T(2,128)(2,1)S(1)} all-to-all(bf16[128,49,2,128]{3,2,1,0:T(2,128)(2,1)S(1)} %send.1), channel_id=1, replica_groups=mesh['lat'=16,'lon'=8] {'lat','lon'}, dimensions={0} | all-to-all | bytes 6422528 | tf_op jit(solution)/shard_map/all_to_all | solution.py:627
  53.5 0.0 copy-done.2
  53.5 0.0 copy-done.3
  53.5 0.0 copy-done.4
  53.5 0.0 copy-start.1
  53.5 11.4 %frame.1 = (bf16[24,6,16,256]{3,2,1,0:T(8,128)(2,1)S(1)}, bf16[2,24,256]{2,1,0:T(8,128)(2,1)S(1)}, bf16[2,24,256]{2,1,0:T(8,128)(2,1)S(1)}, bf16[192,256]{1,0:T(8,128)(2,1)S(1)}, bf16[192,256]{1,0:T(8,128)(2,1)S(1)}) custom-call(bf16[12544,128]{1,0:T(8,128)(2,1)S(1)} %bitcast.7, bf16[128,49,2,128]{3,2,1,0:T(2,128)(2,1)S(1)} %all_to_all.5.where_ref, ...), custom_call_target="tpu_custom_call" | custom-call | tf_op jit(solution)/shard_map/frame/pallas_call | solution.py:519
  64.9 0.8 %collective-permute-start = (bf16[192,256]{1,0:T(8,128)(2,1)S(1)}, bf16[192,256]{1,0:T(8,128)(2,1)S(1)}, u32[]{:S(2)}, u32[]{:S(2)}) collective-permute-start(bf16[192,256]{1,0:T(8,128)(2,1)S(1)} %get-tuple-element.17), channel_id=1, source_target_pairs={{0,8},{16,24},{32,40},{48,56},{64,72},{80,88},{96,104},{112,120},{... | collective-permute-start | bytes 294920 | tf_op jit(solution)/shard_map/ppermute | solution.py:631
  65.7 3.0 %collective-permute-start.1 = (bf16[192,256]{1,0:T(8,128)(2,1)S(1)}, bf16[192,256]{1,0:T(8,128)(2,1)S(1)}, u32[]{:S(2)}, u32[]{:S(2)}) collective-permute-start(bf16[192,256]{1,0:T(8,128)(2,1)S(1)} %get-tuple-element.18), channel_id=1, source_target_pairs={{8,16},{24,32},{40,48},{56,64},{72,80},{88,96},{104,112},{16,8},{3... | collective-permute-start | bytes 294920 | tf_op jit(solution)/shard_map/ppermute | solution.py:630
  68.7 0.0 copy-start
  68.8 2.8 %inner_one.1 = (bf16[26,8,16,256]{3,2,1,0:T(8,128)(2,1)S(1)}, f32[4,40,256]{2,1,0:T(8,128)S(1)}) custom-call(bf16[24,6,16,256]{3,2,1,0:T(8,128)(2,1)S(1)} %get-tuple-element.23.grid_ref, bf16[9,256,256]{2,1,0:T(8,128)(2,1)S(1)} %bitcast.12), custom_call_target="tpu_custom_call" | custom-call | flops 2491416576 | tf_op jit(solution)/shard_map/inner_one/pallas_call | solution.py:559
  71.6 1.6 %shard_map.83.rest_ref = bf16[12,96,256]{2,1,0:T(8,128)(2,1)S(1)} custom-call(bf16[26,8,16,256]{3,2,1,0:T(8,128)(2,1)S(1)} %get-tuple-element.25.hp_ref, bf16[24,6,16,256]{3,2,1,0:T(8,128)(2,1)S(1)} %get-tuple-element.23.grid_ref, bf16[9,256,256]{2,1,0:T(8,128)(2,1)S(1)} %bitcast.8), custom_call_target="tpu_custom_call" | custom-call | flops 1358954496 | tf_op jit(solution)/shard_map/pallas_call | solution.py:572
  73.2 1.1 %shard_map.82.body_ref = bf16[8,96,256]{2,1,0:T(8,128)(2,1)S(1)} custom-call(bf16[26,8,16,256]{3,2,1,0:T(8,128)(2,1)S(1)} %get-tuple-element.25.hp_ref, bf16[24,6,16,256]{3,2,1,0:T(8,128)(2,1)S(1)} %get-tuple-element.23.grid_ref, bf16[9,256,256]{2,1,0:T(8,128)(2,1)S(1)} %bitcast.9), custom_call_target="tpu_custom_call" | custom-call | flops 905969664 | tf_op jit(solution)/shard_map/pallas_call | solution.py:572
  74.3 0.0 collective-permute-done.rows_a_ref
  74.3 0.0 collective-permute-done.1.rows_b_ref
  74.4 0.1 collective-permute-start.2
  74.5 1.6 %collective-permute-start.3 = (bf16[2,32,256]{2,1,0:T(8,128)(2,1)S(1)}, bf16[2,32,256]{2,1,0:T(8,128)(2,1)S(1)}, u32[]{:S(2)}, u32[]{:S(2)}) collective-permute-start(bf16[2,32,256]{2,1,0:T(8,128)(2,1)S(1)} %get-tuple-element.22.sent_b_ref), channel_id=1, source_target_pairs={{1,2},{3,4},{5,6},{7,0},{2,1},{4,3},{6,5},{0,7},{9,10},{11,12},{13... | collective-permute-start | bytes 98312 | tf_op jit(solution)/shard_map/ppermute | solution.py:635
  76.1 2.0 %edge.1 = (bf16[4,96,256]{2,1,0:T(8,128)(2,1)S(1)}, f32[4,8,256]{2,1,0:T(8,128)S(1)}, bf16[24,96,256]{2,1,0:T(8,128)(2,1)}) custom-call(bf16[24,6,16,256]{3,2,1,0:T(8,128)(2,1)S(1)} %get-tuple-element.23.grid_ref, bf16[192,256]{1,0:T(8,128)(2,1)S(1)} %collective-permute-done.rows_a_ref, bf16[192,256]{1,0:T(8,128)(2,1)S(1)} %collective-permute-done.1.rows_b_ref, ...), custom_call_target="tpu_custom_call" | custom-call | flops 905969664 | tf_op jit(solution)/shard_map/edge/pallas_call | solution.py:584
  78.1 0.0 collective-permute-done.2.got_a_ref
  78.1 1.0 %collective-permute-done.3.got_b_ref = bf16[2,32,256]{2,1,0:T(8,128)(2,1)S(1)} collective-permute-done((bf16[2,32,256]{2,1,0:T(8,128)(2,1)S(1)}, bf16[2,32,256]{2,1,0:T(8,128)(2,1)S(1)}, u32[]{:S(2)}, u32[]{:S(2)}) %collective-permute-start.3) | collective-permute-done | bytes 32800 | tf_op jit(solution)/shard_map/ppermute | solution.py:635
  79.1 1.6 %last.1 = bf16[24,96,256]{2,1,0:T(8,128)(2,1)} custom-call(bf16[2,32,256]{2,1,0:T(8,128)(2,1)S(1)} %get-tuple-element.21.sent_a_ref, bf16[2,32,256]{2,1,0:T(8,128)(2,1)S(1)} %get-tuple-element.22.sent_b_ref, bf16[2,32,256]{2,1,0:T(8,128)(2,1)S(1)} %collective-permute-done.2.got_a_ref, ...), custom_call_target="tpu_custom_call", output_to_operand_aliasing={{}: (11, {})} | custom-call | flops 339738624 | tf_op jit(solution)/shard_map/last/pallas_call | solution.py:601
  (3 shorter events, 0.0 us)
Async XLA Ops:
  2.0 51.5 %copy-start.2 = (bf16[128,256]{1,0:T(8,128)(2,1)S(1)}, bf16[128,256]{1,0:T(8,128)(2,1)}, u32[]{:S(2)}) copy-start(bf16[128,256]{1,0:T(8,128)(2,1)} %win_ref.1) | copy-start | bytes 196612
  2.0 51.5 %copy-start.3 = (f32[3,3]{1,0:T(4,128)S(1)}, f32[3,3]{1,0:T(4,128)}, u32[]{:S(2)}) copy-start(f32[3,3]{1,0:T(4,128)} %spread_ref.1) | copy-start | bytes 112
  2.0 51.5 %copy-start.4 = (f32[256]{0:T(256)S(1)}, f32[256]{0:T(256)}, u32[]{:S(2)}) copy-start(f32[256]{0:T(256)} %param.13) | copy-start | bytes 3076
  53.5 15.2 %copy-start.1 = (bf16[3,3,256,256]{3,2,1,0:T(8,128)(2,1)S(1)}, bf16[3,3,256,256]{3,2,1,0:T(8,128)(2,1)}, u32[]{:S(2)}) copy-start(bf16[3,3,256,256]{3,2,1,0:T(8,128)(2,1)} %param.14) | copy-start | bytes 3538948
  64.9 9.4 %collective-permute-start = (bf16[192,256]{1,0:T(8,128)(2,1)S(1)}, bf16[192,256]{1,0:T(8,128)(2,1)S(1)}, u32[]{:S(2)}, u32[]{:S(2)}) collective-permute-start(bf16[192,256]{1,0:T(8,128)(2,1)S(1)} %get-tuple-element.17), channel_id=1, source_target_pairs={{0,8},{16,24},{32,40},{48,56},{64,72},{80,88},{96,104},{112,120},{... | collective-permute-start | bytes 294920 | tf_op jit(solution)/shard_map/ppermute | solution.py:631
  65.7 8.6 %collective-permute-start.1 = (bf16[192,256]{1,0:T(8,128)(2,1)S(1)}, bf16[192,256]{1,0:T(8,128)(2,1)S(1)}, u32[]{:S(2)}, u32[]{:S(2)}) collective-permute-start(bf16[192,256]{1,0:T(8,128)(2,1)S(1)} %get-tuple-element.18), channel_id=1, source_target_pairs={{8,16},{24,32},{40,48},{56,64},{72,80},{88,96},{104,112},{16,8},{3... | collective-permute-start | bytes 294920 | tf_op jit(solution)/shard_map/ppermute | solution.py:630
  68.7 2.9 %copy-start = (bf16[3,3,256,256]{3,2,1,0:T(8,128)(2,1)S(1)}, bf16[3,3,256,256]{3,2,1,0:T(8,128)(2,1)}, u32[]{:S(2)}) copy-start(bf16[3,3,256,256]{3,2,1,0:T(8,128)(2,1)} %param.15) | copy-start | bytes 3538948
  74.4 3.7 %collective-permute-start.2 = (bf16[2,32,256]{2,1,0:T(8,128)(2,1)S(1)}, bf16[2,32,256]{2,1,0:T(8,128)(2,1)S(1)}, u32[]{:S(2)}, u32[]{:S(2)}) collective-permute-start(bf16[2,32,256]{2,1,0:T(8,128)(2,1)S(1)} %get-tuple-element.21.sent_a_ref), channel_id=1, source_target_pairs={{0,1},{2,3},{4,5},{6,7},{1,0},{3,2},{5,4},{7,6},{8,9},{10,11},{12,... | collective-permute-start | bytes 98312 | tf_op jit(solution)/shard_map/ppermute | solution.py:636
  74.5 4.6 %collective-permute-start.3 = (bf16[2,32,256]{2,1,0:T(8,128)(2,1)S(1)}, bf16[2,32,256]{2,1,0:T(8,128)(2,1)S(1)}, u32[]{:S(2)}, u32[]{:S(2)}) collective-permute-start(bf16[2,32,256]{2,1,0:T(8,128)(2,1)S(1)} %get-tuple-element.22.sent_b_ref), channel_id=1, source_target_pairs={{1,2},{3,4},{5,6},{7,0},{2,1},{4,3},{6,5},{0,7},{9,10},{11,12},{13... | collective-permute-start | bytes 98312 | tf_op jit(solution)/shard_map/ppermute | solution.py:635
